TPU v7x, 32 devices: a whole 2x2x4 slice. The times are simulated.
32 devices in a mesh: row: 8 (over y, x, core), col: 4 (over z).
Axes of the slice: x: 2, y: 2, z: 4, core: 2. Of those that a mesh axis runs over, the one named last changes fastest.
Arguments:
- source_points: float32 [3, 32768], P(None, 'col'), may hold values from 0 to 1
- source_areas: float32 [32768], P('col'), may hold values from 0.02 to 0.2
- source_fill: int32 [128], P('col'), may hold values from 128 to 256
- target_points: float32 [3, 32768], P(None, 'row'), may hold values from 0 to 1
- target_fill: int32 [128], P('row'), may hold values from 128 to 256
- charges: bfloat16 [64, 32768], P('row', 'col'), may hold values from -6 to 6
- near_fill: int32 [8, 4], P('row', 'col'), may hold values from 32 to 256, as said below
- near_source: int32 [8, 1024], P('row', 'col'), may hold values from 0 to 31
- near_target: int32 [8, 1024], P('row', 'col'), may hold values from 0 to 15
- far_source: int32 [8, 384], P('row', 'col'), may hold values from 0 to 31
- far_target: int32 [8, 384], P('row', 'col'), may hold values from 0 to 15
- far_rank: int32 [8, 384], P('row', 'col'), may hold values from 8 to 32
- left_basis: bfloat16 [8, 384, 32, 256], P('row', 'col'), may hold values from -0.25 to 0.25
- right_basis: bfloat16 [8, 384, 32, 256], P('row', 'col'), may hold values from -0.375 to 0.375
Outputs:
- potential: float32 [64, 32768], P('col', 'row')
Inputs may be any that keep to these rules, and one draw needn't show every extreme that they name: `near_fill`: used slots are the first ones of a device; in every row some device uses all 256. `near_source`: index among the 32 source leaves of the device's column group. `near_target`: index among the 16 target leaves of the device's row group. `far_source`: index among the 32 source leaves of the device's column group. `far_target`: index among the 16 target leaves of the device's row group. `far_rank`: factor rows from the rank on are padding.
All inputs are finite; a program needn't handle non-finite values.
Results may differ from a plain program's by a relative error of at most 0.0029.
Values may be sent and summed in bfloat16 or wider, within the bound.
No kernel may reach another device: no remote copies, remote signals or barrier semaphores. Data moves between devices by JAX's collectives and lax.ppermute only.
A program may use at most 64 MiB of HBM per device.

v0:
```python
import functools

import jax
import jax.numpy as jnp
from jax import lax
from jax.experimental import pallas as pl
from jax.experimental.pallas import tpu as pltpu
from jax.sharding import PartitionSpec as P


INV_FOUR_PI = 0.07957747154594767
SOFTENING_SQ = 0.0025
F32 = jnp.float32
BF16 = jnp.bfloat16


def split3(value):
    first = value.astype(BF16).astype(F32)
    rest = value - first
    second = rest.astype(BF16).astype(F32)
    return first, second, rest - second


def feature_rows(rows):
    count = rows[0].shape[1]
    index = lax.broadcasted_iota(jnp.int32, (8, count), 0)
    out = jnp.zeros((8, count), F32)
    for position, row in enumerate(rows):
        out = jnp.where(index == position, jnp.broadcast_to(row, (8, count)), out)
    return out


def build_list(ids_ref, list_ref, half_id):
    slots = ids_ref.shape[1]
    square = (slots, slots)

    def across(row):
        return jnp.broadcast_to(row, square).T

    id_row = ids_ref[...].astype(F32)
    id_r = jnp.broadcast_to(id_row, square)
    lane = lax.broadcasted_iota(jnp.int32, square, 1)
    sub = lax.broadcasted_iota(jnp.int32, square, 0)
    same = jnp.where(id_r == across(id_row), 1.0, 0.0)
    count_r = jnp.sum(same, axis=0, keepdims=True)
    earlier_r = jnp.sum(jnp.where(sub < lane, same, 0.0), axis=0, keepdims=True)
    first_r = (earlier_r == 0.0) & (id_row >= 0.0)
    key_c = across(jnp.where(first_r, id_row, 1e9))
    rank_r = jnp.sum(jnp.where(key_c < id_r, 1.0, 0.0), axis=0, keepdims=True)
    rank_c = across(jnp.where(first_r, rank_r, -1.0))
    count_c = across(count_r)
    hit = rank_c == lane.astype(F32)
    list_r = jnp.sum(jnp.where(hit, key_c, 0.0), axis=0, keepdims=True)
    copies_r = jnp.sum(jnp.where(hit, count_c, 0.0), axis=0, keepdims=True)
    total = jnp.sum(jnp.where(first_r, 1.0, 0.0))
    half = jnp.sum(jnp.where(first_r & (id_row < float(half_id)), 1.0, 0.0))
    index = lax.broadcasted_iota(jnp.int32, (8, slots), 0)
    table = jnp.where(index == 0, jnp.broadcast_to(list_r, (8, slots)), 0.0)
    table = jnp.where(index == 1, jnp.broadcast_to(copies_r, (8, slots)), table)
    table = jnp.where(index == 2, total, table)
    table = jnp.where(index == 3, half, table)
    list_ref[...] = table.astype(jnp.int32)


def entry_loop(table_ref, s_ref, t_ref, entries_refs, first, last):
    parts = len(entries_refs)
    column_leaves, leaf, width = s_ref.shape
    depth = t_ref.shape[1]
    rows = 8 // parts
    trips = (last - first + 7) // 8

    def work(*accs):
        for acc in accs:
            pltpu.matmul_pop(acc)

        def drain(u, turn):
            row = jnp.maximum(turn * rows + u // parts, 0)
            entries_refs[u % parts][row] = lax.rsqrt(pltpu.matmul_pop(accs[u])).astype(BF16)

        @pl.loop(0, trips)
        def _(turn):
            for u in range(8):
                pair = table_ref[0, first + turn * 8 + u]
                rhs = jnp.concatenate([t_ref[pair // column_leaves], jnp.zeros((leaf - depth, leaf), BF16)], axis=0)
                lhs = jnp.concatenate([s_ref[pair % column_leaves], jnp.zeros((leaf, leaf - width), BF16)], axis=1)
                stage = (u // 2) % 2
                pltpu.matmul_push_rhs(rhs, staging_register=stage, mxu_index=u % 2)
                pltpu.matmul_acc_lhs(accs[u], lhs, load_staged_rhs=stage)
                if u < 4:
                    drain(u + 4, turn - 1)
                else:
                    drain(u - 4, turn)

        for u in range(4, 8):
            drain(u, trips - 1)

    pl.run_scoped(work, *[pltpu.ACC(u % 2)((leaf, leaf), F32) for u in range(8)])


def first_entries_kernel(*refs, column_leaves, row_leaves, leaf, parts):
    ids_ref, inputs, outputs, scratch = refs[0], refs[1:4], refs[4 : 7 + parts], refs[7 + parts :]
    entries_refs, (table_ref, s_ref, t_ref) = outputs[:parts], outputs[parts:]
    copies, (list_ref, sem, in_sem) = scratch[:3], scratch[3:]
    loads = [pltpu.make_async_copy(src, dst, in_sem.at[i]) for i, (src, dst) in enumerate(zip(inputs, copies))]
    for load in loads:
        load.start()
    spts_ref, area_ref, tpts_ref = copies
    build_list(ids_ref, list_ref, (row_leaves // 2) * column_leaves)
    copy = pltpu.make_async_copy(list_ref, table_ref, sem)
    copy.start()
    for load in loads:
        load.wait()

    tx, ty, tz = (tpts_ref[i : i + 1, :] - 0.5 for i in range(3))
    norm = tx * tx + ty * ty + tz * tz
    h1, h2, h3 = split3(feature_rows([tx, ty, tz, jnp.ones_like(tx), norm]))
    features = jnp.concatenate([h1, h2, h1, h2, h3, h1, jnp.zeros((16,) + h1.shape[1:], F32)], axis=0).astype(BF16)
    for t in range(row_leaves):
        t_ref[t] = features[:, t * leaf : (t + 1) * leaf]

    sx, sy, sz = (spts_ref[i : i + 1, :] - 0.5 for i in range(3))
    scale = area_ref[...] * INV_FOUR_PI
    weight = 1.0 / (scale * scale)
    norm = sx * sx + sy * sy + sz * sz + SOFTENING_SQ
    g1, g2, g3 = split3(
        feature_rows([-2.0 * weight * sx, -2.0 * weight * sy, -2.0 * weight * sz, weight * norm, weight])
    )
    features = jnp.concatenate([g1, g1, g2, g2, g1, g3, jnp.zeros((16,) + g1.shape[1:], F32)], axis=0).astype(BF16)
    for s in range(column_leaves):
        column = features[:, s * leaf : (s + 1) * leaf].T
        s_ref[s] = jnp.concatenate([column, jnp.zeros((leaf, 128 - column.shape[1]), BF16)], axis=1)

    copy.wait()
    group = parts * entries_refs[0].shape[0]
    entry_loop(table_ref, s_ref, t_ref, entries_refs, 0, jnp.minimum(table_ref[2, 0], group))


def second_entries_kernel(table_ref, s_ref, t_ref, *entries_refs):
    first = table_ref.shape[1] - len(entries_refs) * entries_refs[0].shape[0]
    entry_loop(table_ref, s_ref, t_ref, entries_refs, first, jnp.maximum(table_ref[2, 0], first))


VMEM = pl.BlockSpec(memory_space=pltpu.VMEM)
SMEM = pl.BlockSpec(memory_space=pltpu.SMEM)
HBM = pl.BlockSpec(memory_space=pltpu.HBM)


def first_entries(ids, source_points, source_areas, target_points, column_leaves, row_leaves):
    slots = ids.shape[1]
    leaf = source_points.shape[1] // column_leaves
    depth = 64
    inputs = tuple(
        pltpu.with_memory_space_constraint(value, pltpu.HBM)
        for value in (source_points, source_areas[None, :], target_points)
    )
    return pl.pallas_call(
        functools.partial(
            first_entries_kernel, column_leaves=column_leaves, row_leaves=row_leaves, leaf=leaf, parts=2
        ),
        out_shape=(pltpu.VMEM((slots // 4, leaf, leaf), BF16),) * 2
        + (
            pltpu.SMEM((8, slots), jnp.int32),
            pltpu.VMEM((column_leaves, leaf, 128), BF16),
            pltpu.VMEM((row_leaves, depth, leaf), BF16),
        ),
        in_specs=[VMEM] + [HBM] * len(inputs),
        out_specs=(VMEM, VMEM, SMEM, VMEM, VMEM),
        scratch_shapes=[pltpu.VMEM(value.shape, value.dtype) for value in inputs]
        + [pltpu.VMEM((8, slots), jnp.int32), pltpu.SemaphoreType.DMA, pltpu.SemaphoreType.DMA((len(inputs),))],
        compiler_params=pltpu.CompilerParams(vmem_limit_bytes=10 << 20),
        cost_estimate=pl.CostEstimate(flops=8_000_000_000, bytes_accessed=1 << 20, transcendentals=0),
        name="entries",
    )(ids, *inputs)


def second_entries(table, s_features, t_features):
    slots = table.shape[1]
    leaf = s_features.shape[1]
    return pl.pallas_call(
        second_entries_kernel,
        out_shape=(pltpu.VMEM((slots // 4, leaf, leaf), BF16),) * 2,
        in_specs=[SMEM, VMEM, VMEM],
        out_specs=(VMEM, VMEM),
        compiler_params=pltpu.CompilerParams(vmem_limit_bytes=4 << 20),
        cost_estimate=pl.CostEstimate(flops=8_000_000_000, bytes_accessed=1 << 20, transcendentals=0),
        name="entries_rest",
    )(table, s_features, t_features)


def far_kernel(*refs, pieces, plain, leaf, unroll):
    (sfill_ref, fsrc_ref, ftgt_ref, frank_ref, left_ref, right_ref) = refs[:6]
    piece_refs = refs[6 : 6 + pieces]
    x_ref, acc_ref, coef_ref = refs[6 + pieces :]
    column_leaves, rhs, _ = x_ref.shape
    far_slots, rank, _ = left_ref.shape

    lane = lax.broadcasted_iota(jnp.int32, (rhs, leaf), 1)
    if not plain:
        parity = lax.rem(lax.axis_index("row"), 2)
    for s in range(column_leaves):
        window = slice(s * leaf, (s + 1) * leaf)
        if plain:
            block = piece_refs[0][:, window].astype(F32)
        else:
            rows = []
            for j in range(pieces // 2):
                mine = piece_refs[j][:, window].astype(F32)
                other = piece_refs[pieces // 2 + j][:, window].astype(F32)
                rows.append(jnp.where(parity == 0, mine, other))
                rows.append(jnp.where(parity == 0, other, mine))
            block = jnp.concatenate(rows, axis=0)
        x_ref[s] = jnp.where(lane < sfill_ref[s], block, 0.0).astype(BF16)

    acc_ref[...] = jnp.zeros_like(acc_ref)

    rank_lane = lax.broadcasted_iota(jnp.int32, (rhs, rank), 1)

    @pl.loop(0, far_slots // unroll)
    def _(turn):
        for u in range(unroll):
            k = turn * unroll + u
            coef = lax.dot_general(
                x_ref[fsrc_ref[0, k]], right_ref[k], (((1,), (1,)), ((), ())), preferred_element_type=F32
            )
            coef_ref[k] = jnp.where(rank_lane < frank_ref[0, k], coef, 0.0).astype(BF16)

    @pl.loop(0, far_slots // unroll)
    def _(turn):
        blocks = []
        for u in range(unroll):
            k = turn * unroll + u
            blocks.append(jnp.dot(coef_ref[k], left_ref[k], preferred_element_type=F32))
        for u in range(unroll):
            t = ftgt_ref[0, turn * unroll + u]
            acc_ref[t] = acc_ref[t] + blocks[u]


def near_kernel(*refs, groups, chunk, chunks, plain):
    (table_ref, tfill_ref, far_ref, x_ref) = refs[:4]
    entries_refs = refs[4 : 4 + 2 * groups]
    carried = 1 if chunk > 0 and not plain else 0
    carried_refs = refs[4 + 2 * groups : 4 + 2 * groups + carried]
    out_refs, acc_ref = refs[4 + 2 * groups + carried : -1], refs[-1]
    chunk_leaves, rhs, leaf = acc_ref.shape
    column_leaves = x_ref.shape[0]
    base_leaf = chunk * chunk_leaves
    group = table_ref.shape[1] // groups
    total, half = table_ref[2, 0], table_ref[3, 0]
    low = half if chunk > 0 else 0
    high = total if chunk == chunks - 1 else half
    acc_ref[...] = jnp.zeros_like(acc_ref)

    def work(*accs):
        for acc in accs:
            pltpu.matmul_pop(acc)

        def drain(u, k):
            inside = (k >= low) & (k < high)
            slot = jnp.maximum(k, 0)
            t = jnp.clip(table_ref[0, slot] // column_leaves - base_leaf, 0, chunk_leaves - 1)
            copies = jnp.where(inside, table_ref[1, slot], 0).astype(F32)
            block = pltpu.matmul_pop(accs[u])
            acc_ref[t] = acc_ref[t] + jnp.where(inside, block * copies, 0.0)

        for g in range(groups):
            pair_refs = entries_refs[2 * g : 2 * g + 2]
            start = jnp.clip(low, g * group, (g + 1) * group) // 16
            stop = (jnp.clip(high, g * group, (g + 1) * group) + 15) // 16

            @pl.loop(start, stop)
            def _(turn):
                for u in range(16):
                    k = turn * 16 + u
                    source = table_ref[0, k] % column_leaves
                    stage = (u // 2) % 2
                    entries = pair_refs[u % 2][turn * 8 - g * (group // 2) + u // 2]
                    pltpu.matmul_push_rhs(entries, staging_register=stage, mxu_index=u % 2)
                    pltpu.matmul_acc_lhs(accs[u], x_ref[source], load_staged_rhs=stage)
                    if u >= 8:
                        drain(u - 8, k - 8)
                    else:
                        drain(u + 8, k - 8)

        end = (high + 15) // 16 * 16
        for u in range(8, 16):
            drain(u, end - 16 + u)

    pl.run_scoped(work, *[pltpu.ACC(u % 2)((rhs, leaf), F32) for u in range(16)])

    if plain:
        lane_t = lax.broadcasted_iota(jnp.int32, (rhs, leaf), 1)
        for t in range(chunk_leaves):
            value = acc_ref[t] + far_ref[base_leaf + t]
            out_refs[0][:, t * leaf : (t + 1) * leaf] = jnp.where(lane_t < tfill_ref[base_leaf + t], value, 0.0)
    else:
        owners = len(out_refs)
        height = rhs // owners
        lane_t = lax.broadcasted_iota(jnp.int32, (height, leaf), 1)
        base = lax.axis_index("col") ^ (lax.axis_index("row") // 2)
        for m in range(owners):
            start = pl.multiple_of((base ^ m) * height, height)
            shift = out_refs[m].shape[1] - chunk_leaves * leaf
            if shift:
                out_refs[m][:, :shift] = carried_refs[0][...]
            for t in range(chunk_leaves):
                value = acc_ref[t, pl.ds(start, height), :] + far_ref[base_leaf + t, pl.ds(start, height), :]
                value = jnp.where(lane_t < tfill_ref[base_leaf + t], value, 0.0)
                window = slice(shift + t * leaf, shift + (t + 1) * leaf)
                out_refs[m][:, window] = value.astype(out_refs[m].dtype)


def far_field(source_fill, row_leaves, far_source, far_target, far_rank, left, right, pieces, plain):
    column_leaves = source_fill.shape[0]
    far_slots, rank, leaf = left.shape
    rhs = sum(p.shape[0] for p in pieces)
    vmem = pl.BlockSpec(memory_space=pltpu.VMEM)
    smem = pl.BlockSpec(memory_space=pltpu.SMEM)
    unroll = next(u for u in (32, 16, 8, 4, 2, 1) if far_slots % u == 0)
    return pl.pallas_call(
        functools.partial(far_kernel, pieces=len(pieces), plain=plain, leaf=leaf, unroll=unroll),
        out_shape=(pltpu.VMEM((column_leaves, rhs, leaf), BF16), pltpu.VMEM((row_leaves, rhs, leaf), F32)),
        in_specs=[smem] * 4 + [vmem] * (2 + len(pieces)),
        out_specs=(vmem, vmem),
        scratch_shapes=[pltpu.VMEM((far_slots, rhs, rank), BF16)],
        compiler_params=pltpu.CompilerParams(vmem_limit_bytes=12 << 20),
        cost_estimate=pl.CostEstimate(flops=2_000_000_000, bytes_accessed=8 << 20, transcendentals=0),
        name="far",
    )(source_fill, far_source, far_target, far_rank, left, right, *pieces)


def near_field(table, target_fill, far, x, entries, owners, plain, chunk, chunks, carried=()):
    row_leaves, rhs, leaf = far.shape
    width = row_leaves // chunks * leaf
    if plain:
        out_shape = (jax.ShapeDtypeStruct((rhs, width), F32),)
    else:
        out_shape = tuple(
            jax.ShapeDtypeStruct(
                (rhs // owners, width + (carried[0].shape[1] if m == 1 and carried else 0)), F32 if m == 0 else BF16
            )
            for m in range(owners)
        )
    return pl.pallas_call(
        functools.partial(near_kernel, groups=len(entries) // 2, chunk=chunk, chunks=chunks, plain=plain),
        out_shape=out_shape,
        in_specs=[SMEM] * 2 + [VMEM] * (2 + len(entries) + len(carried)),
        out_specs=(VMEM,) * len(out_shape),
        scratch_shapes=[pltpu.VMEM((row_leaves // chunks, rhs, leaf), F32)],
        compiler_params=pltpu.CompilerParams(vmem_limit_bytes=4 << 20),
        cost_estimate=pl.CostEstimate(flops=4_000_000_000, bytes_accessed=8 << 20, transcendentals=0),
        name="near",
    )(table, target_fill, far, x, *entries, *carried)


def shards(
    source_points, source_areas, source_fill, target_points, target_fill, charges, near_fill, near_source,
    near_target, far_source, far_target, far_rank, left_basis, right_basis, *, rows, columns,
):
    plain = charges.shape[0] % 8 != 0 or rows != 2 * columns
    if plain:
        pieces = [lax.all_gather(charges, "row", axis=0, tiled=True)]
    else:

        def swap(value, axis, size, mask):
            return lax.ppermute(value, axis, [(i, i ^ mask) for i in range(size)])

        pieces = [charges] + [swap(charges, "row", rows, mask) for mask in range(2, rows, 2)]
    used = jnp.arange(near_source.shape[1])[None, :] < near_fill
    ids = jnp.where(used, near_target * source_fill.shape[0] + near_source, -1)
    row_leaves = target_fill.shape[0]
    *entries, table, s_features, t_features = first_entries(
        ids, source_points, source_areas, target_points, source_fill.shape[0], row_leaves
    )
    if not plain:
        pieces, table = lax.optimization_barrier((pieces, table))
        pieces = pieces + [swap(piece, "row", rows, 1) for piece in pieces]
    entries = entries + list(second_entries(table, s_features, t_features))
    if not plain:
        pieces, entries[-1] = lax.optimization_barrier((pieces, entries[-1]))
    x, far = far_field(
        source_fill, row_leaves, far_source, far_target, far_rank, left_basis[0], right_basis[0], pieces, plain
    )
    if plain or row_leaves % 2 or columns < 3:
        outs = near_field(table, target_fill, far, x, entries, columns, plain, 0, 1)
        if plain:
            return lax.psum_scatter(outs[0], "col", scatter_dimension=0, tiled=True)
        result = outs[0]
        for mask in reversed(range(1, columns)):
            result = result + swap(outs[mask], "col", columns, mask).astype(F32)
        return result

    def exchange(value, mask):
        return swap(value, "col", columns, mask)

    first = near_field(table, target_fill, far, x, entries, columns, plain, 0, 2)
    early = [exchange(first[mask], mask) for mask in reversed(range(2, columns))]
    second = near_field(table, target_fill, far, x, entries, columns, plain, 1, 2, (first[1],))
    neighbour = exchange(second[1], 1)
    late = [exchange(second[mask], mask) for mask in reversed(range(2, columns))]
    result = jnp.concatenate([first[0], second[0]], axis=1) + neighbour.astype(F32)
    for a, b in zip(early, late):
        result = result + jnp.concatenate([a, b], axis=1).astype(F32)
    return result


def solution(mesh):
    placed = (
        P(None, "col"), P("col"), P("col"), P(None, "row"), P("row"), P("row", "col"), P("row", "col"),
        P("row", "col"), P("row", "col"), P("row", "col"), P("row", "col"), P("row", "col"),
        P("row", "col", None, None), P("row", "col", None, None),
    )
    return jax.shard_map(
        functools.partial(shards, rows=mesh.shape["row"], columns=mesh.shape["col"]),
        mesh=mesh, in_specs=placed, out_specs=P("col", "row"), check_vma=False,
    )
```

profile of v0, /device:TPU:0, one launch (start us, length us, event | category | flops | bytes accessed | tf_op | source)
XLA Modules:
  0.0 44.6 jit_solution(2988164965675359421)
XLA Ops:
  0.0 3.0 %collective-permute-start = (bf16[8,8192]{1,0:T(8,128)(2,1)}, bf16[8,8192]{1,0:T(8,128)(2,1)S(1)}, u32[]{:S(2)}, u32[]{:S(2)}) collective-permute-start(bf16[8,8192]{1,0:T(8,128)(2,1)} %refs_6_), channel_id=1, source_target_pairs={{0,8},{4,12},{8,0},{12,4},{16,24},{20,28},{24,16},{28,20},{1,9},{5... | collective-permute-start | bytes 393224 | tf_op jit(solution)/shard_map/ppermute | solution.py:365
  3.0 1.5 %collective-permute-start.1 = (bf16[8,8192]{1,0:T(8,128)(2,1)}, bf16[8,8192]{1,0:T(8,128)(2,1)S(1)}, u32[]{:S(2)}, u32[]{:S(2)}) collective-permute-start(bf16[8,8192]{1,0:T(8,128)(2,1)} %refs_6_), channel_id=1, source_target_pairs={{0,16},{4,20},{8,24},{12,28},{16,0},{20,4},{24,8},{28,12},{1,17},{... | collective-permute-start | bytes 393224 | tf_op jit(solution)/shard_map/ppermute | solution.py:365
  4.5 0.0 collective-permute-start.2
  5.1 0.7 %compare_select_fusion.refs_0_ = s32[1,256]{1,0:T(1,128)S(1)} fusion(s32[1,256]{1,0:T(1,128)} %param.21, s32[1,256]{1,0:T(1,128)} %param.22, s32[]{:T(128)} %bitcast.4), kind=kLoop, calls=%fused_computation.3 | loop fusion | flops 1024 | bytes 3076 | tf_op jit(solution)/shard_map/jit(_where)/select_n | solution.py:369
  5.8 0.0 copy-start.3
  5.8 7.8 %entries.1 = (bf16[64,256,256]{2,1,0:T(8,128)(2,1)S(1)}, bf16[64,256,256]{2,1,0:T(8,128)(2,1)S(1)}, s32[8,256]{1,0:T(8,128)S(4)}, bf16[32,256,128]{2,1,0:T(8,128)(2,1)S(1)}, bf16[16,64,256]{2,1,0:T(8,128)(2,1)S(1)}) custom-call(s32[1,256]{1,0:T(1,128)S(1)} %compare_select_fusion.refs_0_, f32[3,8192]{1,0:T(4,128)} %refs_1_.4, f32[1,8192]{1,0:T(1,128)} %bitcast.7, ...), custom_call_target="tpu_custom_call" | custom-call | flops 8000000000 | bytes 1048576 | tf_op jit(solution)/shard_map/entries/pallas_call | solution.py:156
  13.6 0.0 collective-permute-done.refs_7_
  13.7 0.0 collective-permute-done.1.refs_8_
  13.7 0.0 collective-permute-done.2.refs_9_
  13.7 0.0 copy-done.3
  13.7 0.1 collective-permute-start.3
  13.8 0.5 %collective-permute-start.4 = (bf16[8,8192]{1,0:T(8,128)(2,1)S(1)}, bf16[8,8192]{1,0:T(8,128)(2,1)S(1)}, u32[]{:S(2)}, u32[]{:S(2)}) collective-permute-start(bf16[8,8192]{1,0:T(8,128)(2,1)S(1)} %collective-permute-done.refs_7_), channel_id=1, source_target_pairs={{0,4},{4,0},{8,12},{12,8},{16,20},{20,16},{24,28},{28,24},{1,5},{5... | collective-permute-start | bytes 393224 | tf_op jit(solution)/shard_map/ppermute | solution.py:365
  14.3 0.1 collective-permute-start.5
  14.3 0.4 collective-permute-start.6
  14.8 0.0 copy-start.1
  14.8 0.0 copy-start.2
  14.8 0.0 copy-start.4
  14.8 0.0 copy-start.5
  14.8 0.0 copy-start.6
  14.8 0.0 copy-start.7
  14.8 0.0 copy-start
  14.8 3.5 %entries_rest.1 = (bf16[64,256,256]{2,1,0:T(8,128)(2,1)S(1)}, bf16[64,256,256]{2,1,0:T(8,128)(2,1)S(1)}) custom-call(s32[8,256]{1,0:T(8,128)S(4)} %get-tuple-element.37.table_ref.refs_0_, bf16[32,256,128]{2,1,0:T(8,128)(2,1)S(1)} %get-tuple-element.42.s_ref, bf16[16,64,256]{2,1,0:T(8,128)(2,1)S(1)} %get-tuple-element.43.t_ref), custom_call_target="tpu_custom_call" | custom-call | flops 8000000000 | bytes 1048576 | tf_op jit(solution)/shard_map/entries_rest/pallas_call | solution.py:179
  18.4 0.0 collective-permute-done.3.refs_10_
  18.4 0.0 collective-permute-done.4.refs_11_
  18.4 0.0 collective-permute-done.5.refs_12_
  18.4 0.0 collective-permute-done.6.refs_13_
  18.4 0.0 copy-done.1
  18.4 0.0 copy-done.2
  18.4 0.0 copy-done.4
  18.4 0.0 copy-done.5
  18.5 0.0 copy-done.6
  18.5 0.0 copy-done.7
  18.5 3.4 %far.1 = (bf16[32,64,256]{2,1,0:T(8,128)(2,1)S(1)}, f32[16,64,256]{2,1,0:T(8,128)S(1)}) custom-call(s32[32]{0:T(128)S(1)} %copy-done.4, s32[1,96]{1,0:T(1,128)S(1)} %copy-done.5, s32[1,96]{1,0:T(1,128)S(1)} %copy-done.6, s32[1,96]{1,0:T(1,128)S(1)} %copy-done.7, bf16[96,32,256]{2,1,0:T(8,128)(2,1)S(1)} %bitcast.5, bf16[96,32,256]{2,1,0:T(8,128)(2,1)S(1)} %bitcast.6, ...), custom_call_target="tpu_custom_call" | custom-call | flops 2000000000 | bytes 8388608 | tf_op jit(solution)/shard_map/far/pallas_call | solution.py:319
  21.9 0.0 copy-done
  21.9 3.3 %near.2 = (f32[16,2048]{1,0:T(8,128)S(1)}, bf16[16,2048]{1,0:T(8,128)(2,1)S(1)}, bf16[16,2048]{1,0:T(8,128)(2,1)S(1)}, bf16[16,2048]{1,0:T(8,128)(2,1)S(1)}) custom-call(s32[8,256]{1,0:T(8,128)S(4)} %get-tuple-element.37.table_ref.refs_0_, s32[16]{0:T(128)S(1)} %copy-done, f32[16,64,256]{2,1,0:T(8,128)S(1)} %get-tuple-element.53.refs_2_, ...), custom_call_target="tpu_custom_call" | custom-call | flops 4000000000 | bytes 8388608 | tf_op jit(solution)/shard_map/near/pallas_call | solution.py:343
  25.2 4.2 %near.3 = (f32[16,2048]{1,0:T(8,128)S(1)}, bf16[16,4096]{1,0:T(8,128)(2,1)S(1)}, bf16[16,2048]{1,0:T(8,128)(2,1)S(1)}, bf16[16,2048]{1,0:T(8,128)(2,1)S(1)}) custom-call(s32[8,256]{1,0:T(8,128)S(4)} %get-tuple-element.37.table_ref.refs_0_, s32[16]{0:T(128)S(1)} %copy-done, f32[16,64,256]{2,1,0:T(8,128)S(1)} %get-tuple-element.53.refs_2_, ...), custom_call_target="tpu_custom_call" | custom-call | flops 4000000000 | bytes 8388608 | tf_op jit(solution)/shard_map/near/pallas_call | solution.py:343
  29.4 0.1 collective-permute-start.7
  29.5 0.1 collective-permute-start.11
  29.6 4.3 %collective-permute-start.9 = (bf16[16,2048]{1,0:T(8,128)(2,1)S(1)}, bf16[16,2048]{1,0:T(8,128)(2,1)S(1)}, u32[]{:S(2)}, u32[]{:S(2)}) collective-permute-start(bf16[16,2048]{1,0:T(8,128)(2,1)S(1)} %get-tuple-element.64), channel_id=1, source_target_pairs={{0,3},{1,2},{2,1},{3,0},{4,7},{5,6},{6,5},{7,4},{8,11},{9,10},{10,... | collective-permute-start | bytes 196616 | tf_op jit(solution)/shard_map/ppermute | solution.py:365
  33.9 0.0 collective-permute-start.10
  33.9 1.5 %collective-permute-start.8 = (bf16[16,2048]{1,0:T(8,128)(2,1)S(1)}, bf16[16,2048]{1,0:T(8,128)(2,1)S(1)}, u32[]{:S(2)}, u32[]{:S(2)}) collective-permute-start(bf16[16,2048]{1,0:T(8,128)(2,1)S(1)} %get-tuple-element.63), channel_id=1, source_target_pairs={{0,3},{1,2},{2,1},{3,0},{4,7},{5,6},{6,5},{7,4},{8,11},{9,10},{10,... | collective-permute-start | bytes 196616 | tf_op jit(solution)/shard_map/ppermute | solution.py:365
  35.4 5.6 %collective-permute-done.11 = bf16[16,2048]{1,0:T(8,128)(2,1)S(1)} collective-permute-done((bf16[16,2048]{1,0:T(8,128)(2,1)S(1)}, bf16[16,2048]{1,0:T(8,128)(2,1)S(1)}, u32[]{:S(2)}, u32[]{:S(2)}) %collective-permute-start.11) | collective-permute-done | bytes 65568 | tf_op jit(solution)/shard_map/ppermute | solution.py:365
  41.1 0.0 collective-permute-done.9
  41.1 2.8 %collective-permute-done.10 = bf16[16,2048]{1,0:T(8,128)(2,1)S(1)} collective-permute-done((bf16[16,2048]{1,0:T(8,128)(2,1)S(1)}, bf16[16,2048]{1,0:T(8,128)(2,1)S(1)}, u32[]{:S(2)}, u32[]{:S(2)}) %collective-permute-start.10) | collective-permute-done | bytes 65568 | tf_op jit(solution)/shard_map/ppermute | solution.py:365
  43.9 0.0 collective-permute-done.8
  43.9 0.0 collective-permute-done.7
  43.9 0.8 %fusion.1 = f32[16,4096]{1,0:T(8,128)} fusion(f32[16,2048]{1,0:T(8,128)S(1)} %get-tuple-element.61, f32[16,2048]{1,0:T(8,128)S(1)} %get-tuple-element.59, bf16[16,4096]{1,0:T(8,128)(2,1)S(1)} %collective-permute-done.7, bf16[16,2048]{1,0:T(8,128)(2,1)S(1)} %collective-permute-done.9, bf16[16,2048]{1,0:T(8,128)(2,1)S(1)} %collective-permute-done.8, ...), kind=kLoop, calls=%fused_computation.2 | loop fusion | flops 851968 | bytes 917504 | tf_op jit(solution)/shard_map/add | solution.py:402
Async XLA Ops:
  0.0 13.6 %collective-permute-start = (bf16[8,8192]{1,0:T(8,128)(2,1)}, bf16[8,8192]{1,0:T(8,128)(2,1)S(1)}, u32[]{:S(2)}, u32[]{:S(2)}) collective-permute-start(bf16[8,8192]{1,0:T(8,128)(2,1)} %refs_6_), channel_id=1, source_target_pairs={{0,8},{4,12},{8,0},{12,4},{16,24},{20,28},{24,16},{28,20},{1,9},{5... | collective-permute-start | bytes 393224 | tf_op jit(solution)/shard_map/ppermute | solution.py:365
  3.0 10.7 %collective-permute-start.1 = (bf16[8,8192]{1,0:T(8,128)(2,1)}, bf16[8,8192]{1,0:T(8,128)(2,1)S(1)}, u32[]{:S(2)}, u32[]{:S(2)}) collective-permute-start(bf16[8,8192]{1,0:T(8,128)(2,1)} %refs_6_), channel_id=1, source_target_pairs={{0,16},{4,20},{8,24},{12,28},{16,0},{20,4},{24,8},{28,12},{1,17},{... | collective-permute-start | bytes 393224 | tf_op jit(solution)/shard_map/ppermute | solution.py:365
  4.5 9.2 %collective-permute-start.2 = (bf16[8,8192]{1,0:T(8,128)(2,1)}, bf16[8,8192]{1,0:T(8,128)(2,1)S(1)}, u32[]{:S(2)}, u32[]{:S(2)}) collective-permute-start(bf16[8,8192]{1,0:T(8,128)(2,1)} %refs_6_), channel_id=1, source_target_pairs={{0,24},{4,28},{8,16},{12,20},{16,8},{20,12},{24,0},{28,4},{1,25},{... | collective-permute-start | bytes 393224 | tf_op jit(solution)/shard_map/ppermute | solution.py:365
  5.8 7.8 %copy-start.3 = (bf16[8,8192]{1,0:T(8,128)(2,1)S(1)}, bf16[8,8192]{1,0:T(8,128)(2,1)}, u32[]{:S(2)}) copy-start(bf16[8,8192]{1,0:T(8,128)(2,1)} %refs_6_) | copy-start | bytes 393220
  13.7 4.7 %collective-permute-start.3 = (bf16[8,8192]{1,0:T(8,128)(2,1)S(1)}, bf16[8,8192]{1,0:T(8,128)(2,1)S(1)}, u32[]{:S(2)}, u32[]{:S(2)}) collective-permute-start(bf16[8,8192]{1,0:T(8,128)(2,1)S(1)} %copy-done.3), channel_id=1, source_target_pairs={{0,4},{4,0},{8,12},{12,8},{16,20},{20,16},{24,28},{28,24},{1,5},{5... | collective-permute-start | bytes 393224 | tf_op jit(solution)/shard_map/ppermute | solution.py:365
  13.8 4.6 %collective-permute-start.4 = (bf16[8,8192]{1,0:T(8,128)(2,1)S(1)}, bf16[8,8192]{1,0:T(8,128)(2,1)S(1)}, u32[]{:S(2)}, u32[]{:S(2)}) collective-permute-start(bf16[8,8192]{1,0:T(8,128)(2,1)S(1)} %collective-permute-done.refs_7_), channel_id=1, source_target_pairs={{0,4},{4,0},{8,12},{12,8},{16,20},{20,16},{24,28},{28,24},{1,5},{5... | collective-permute-start | bytes 393224 | tf_op jit(solution)/shard_map/ppermute | solution.py:365
  14.3 4.1 %collective-permute-start.5 = (bf16[8,8192]{1,0:T(8,128)(2,1)S(1)}, bf16[8,8192]{1,0:T(8,128)(2,1)S(1)}, u32[]{:S(2)}, u32[]{:S(2)}) collective-permute-start(bf16[8,8192]{1,0:T(8,128)(2,1)S(1)} %collective-permute-done.1.refs_8_), channel_id=1, source_target_pairs={{0,4},{4,0},{8,12},{12,8},{16,20},{20,16},{24,28},{28,24},{1,5},{5... | collective-permute-start | bytes 393224 | tf_op jit(solution)/shard_map/ppermute | solution.py:365
  14.3 4.1 %collective-permute-start.6 = (bf16[8,8192]{1,0:T(8,128)(2,1)S(1)}, bf16[8,8192]{1,0:T(8,128)(2,1)S(1)}, u32[]{:S(2)}, u32[]{:S(2)}) collective-permute-start(bf16[8,8192]{1,0:T(8,128)(2,1)S(1)} %collective-permute-done.2.refs_9_), channel_id=1, source_target_pairs={{0,4},{4,0},{8,12},{12,8},{16,20},{20,16},{24,28},{28,24},{1,5},{5... | collective-permute-start | bytes 393224 | tf_op jit(solution)/shard_map/ppermute | solution.py:365
  14.8 3.6 %copy-start.1 = (bf16[1,96,32,256]{3,2,1,0:T(8,128)(2,1)S(1)}, bf16[1,96,32,256]{3,2,1,0:T(8,128)(2,1)}, u32[]{:S(2)}) copy-start(bf16[1,96,32,256]{3,2,1,0:T(8,128)(2,1)} %param.26) | copy-start | bytes 4718596
  14.8 3.6 %copy-start.2 = (bf16[1,96,32,256]{3,2,1,0:T(8,128)(2,1)S(1)}, bf16[1,96,32,256]{3,2,1,0:T(8,128)(2,1)}, u32[]{:S(2)}) copy-start(bf16[1,96,32,256]{3,2,1,0:T(8,128)(2,1)} %param.27) | copy-start | bytes 4718596
  14.8 3.7 %copy-start.4 = (s32[32]{0:T(128)S(1)}, s32[32]{0:T(128)}, u32[]{:S(2)}) copy-start(s32[32]{0:T(128)} %refs_0_.1) | copy-start | bytes 388
  14.8 3.7 %copy-start.5 = (s32[1,96]{1,0:T(1,128)S(1)}, s32[1,96]{1,0:T(1,128)}, u32[]{:S(2)}) copy-start(s32[1,96]{1,0:T(1,128)} %refs_1_.5) | copy-start | bytes 1156
  14.8 3.7 %copy-start.6 = (s32[1,96]{1,0:T(1,128)S(1)}, s32[1,96]{1,0:T(1,128)}, u32[]{:S(2)}) copy-start(s32[1,96]{1,0:T(1,128)} %refs_2_.1) | copy-start | bytes 1156
  14.8 3.7 %copy-start.7 = (s32[1,96]{1,0:T(1,128)S(1)}, s32[1,96]{1,0:T(1,128)}, u32[]{:S(2)}) copy-start(s32[1,96]{1,0:T(1,128)} %refs_3_.3) | copy-start | bytes 1156
  14.8 7.1 %copy-start = (s32[16]{0:T(128)S(1)}, s32[16]{0:T(128)}, u32[]{:S(2)}) copy-start(s32[16]{0:T(128)} %refs_1_.7) | copy-start | bytes 196
  29.4 14.4 %collective-permute-start.7 = (bf16[16,4096]{1,0:T(8,128)(2,1)S(1)}, bf16[16,4096]{1,0:T(8,128)(2,1)S(1)}, u32[]{:S(2)}, u32[]{:S(2)}) collective-permute-start(bf16[16,4096]{1,0:T(8,128)(2,1)S(1)} %get-tuple-element.62), channel_id=1, source_target_pairs={{0,1},{1,0},{2,3},{3,2},{4,5},{5,4},{6,7},{7,6},{8,9},{9,8},{10,11... | collective-permute-start | bytes 393224 | tf_op jit(solution)/shard_map/ppermute | solution.py:365
  29.5 11.5 %collective-permute-start.11 = (bf16[16,2048]{1,0:T(8,128)(2,1)S(1)}, bf16[16,2048]{1,0:T(8,128)(2,1)S(1)}, u32[]{:S(2)}, u32[]{:S(2)}) collective-permute-start(bf16[16,2048]{1,0:T(8,128)(2,1)S(1)} %get-tuple-element.66), channel_id=1, source_target_pairs={{0,2},{1,3},{2,0},{3,1},{4,6},{5,7},{6,4},{7,5},{8,10},{9,11},{10,... | collective-permute-start | bytes 196616 | tf_op jit(solution)/shard_map/ppermute | solution.py:365
  29.6 11.5 %collective-permute-start.9 = (bf16[16,2048]{1,0:T(8,128)(2,1)S(1)}, bf16[16,2048]{1,0:T(8,128)(2,1)S(1)}, u32[]{:S(2)}, u32[]{:S(2)}) collective-permute-start(bf16[16,2048]{1,0:T(8,128)(2,1)S(1)} %get-tuple-element.64), channel_id=1, source_target_pairs={{0,3},{1,2},{2,1},{3,0},{4,7},{5,6},{6,5},{7,4},{8,11},{9,10},{10,... | collective-permute-start | bytes 196616 | tf_op jit(solution)/shard_map/ppermute | solution.py:365
  33.9 10.0 %collective-permute-start.10 = (bf16[16,2048]{1,0:T(8,128)(2,1)S(1)}, bf16[16,2048]{1,0:T(8,128)(2,1)S(1)}, u32[]{:S(2)}, u32[]{:S(2)}) collective-permute-start(bf16[16,2048]{1,0:T(8,128)(2,1)S(1)} %get-tuple-element.65), channel_id=1, source_target_pairs={{0,2},{1,3},{2,0},{3,1},{4,6},{5,7},{6,4},{7,5},{8,10},{9,11},{10,... | collective-permute-start | bytes 196616 | tf_op jit(solution)/shard_map/ppermute | solution.py:365
  33.9 10.0 %collective-permute-start.8 = (bf16[16,2048]{1,0:T(8,128)(2,1)S(1)}, bf16[16,2048]{1,0:T(8,128)(2,1)S(1)}, u32[]{:S(2)}, u32[]{:S(2)}) collective-permute-start(bf16[16,2048]{1,0:T(8,128)(2,1)S(1)} %get-tuple-element.63), channel_id=1, source_target_pairs={{0,3},{1,2},{2,1},{3,0},{4,7},{5,6},{6,5},{7,4},{8,11},{9,10},{10,... | collective-permute-start | bytes 196616 | tf_op jit(solution)/shard_map/ppermute | solution.py:365
where the time goes:
time: 44.9 us; the launch traced here: 44.6 us
  Pallas kernels  22.3 us (50%)
  starting transfers between devices  11.5 us (26%)
  waiting for transfers between devices  8.46 us (19%)
  other arithmetic  1.46 us (3%)
  between operations  0.87 us (2%)
    ppermute x12, starting transfers between devices, swap(): return lax.ppermute(value, axis, [(i, i ^ mask) for i in range(size)])  11.5 us
    ppermute x12, waiting for transfers between devices, swap(): return lax.ppermute(value, axis, [(i, i ^ mask) for i in range(size)])  8.46 us
    pallas_call x1, Pallas kernels, first_entries(): pl.pallas_call(functools.partial(first_entries_kernel, column_leaves=colu...  7.79 us
    pallas_call x2, Pallas kernels, near_field(): pl.pallas_call(functools.partial(near_kernel, groups=len(entries) // 2, c...  7.5 us
    pallas_call x1, Pallas kernels, second_entries(): pl.pallas_call(second_entries_kernel, out_shape=(pltpu.VMEM((slots // 4,...  3.54 us
    pallas_call x1, Pallas kernels, far_field(): pl.pallas_call(functools.partial(far_kernel, pieces=len(pieces), plain=pl...  3.43 us
  transfers between devices with their start and end apart: 12, of which 2 were waited for; matrix products, arithmetic and copies ran while one was open for 2% of the time, Pallas kernels for 25%

commit v1 on v0

--- a/solution.py
+++ b/solution.py
@@ -30,14 +30,14 @@
     return out
 
 
-def build_list(ids_ref, list_ref, half_id):
-    slots = ids_ref.shape[1]
+def build_list(id_row, list_ref, half_id):
+    slots = id_row.shape[1]
     square = (slots, slots)
 
     def across(row):
         return jnp.broadcast_to(row, square).T
 
-    id_row = ids_ref[...].astype(F32)
+    id_row = id_row.astype(F32)
     id_r = jnp.broadcast_to(id_row, square)
     lane = lax.broadcasted_iota(jnp.int32, square, 1)
     sub = lax.broadcasted_iota(jnp.int32, square, 0)
@@ -97,18 +97,24 @@
     pl.run_scoped(work, *[pltpu.ACC(u % 2)((leaf, leaf), F32) for u in range(8)])
 
 
-def first_entries_kernel(*refs, column_leaves, row_leaves, leaf, parts):
-    ids_ref, inputs, outputs, scratch = refs[0], refs[1:4], refs[4 : 7 + parts], refs[7 + parts :]
-    entries_refs, (table_ref, s_ref, t_ref) = outputs[:parts], outputs[parts:]
-    copies, (list_ref, sem, in_sem) = scratch[:3], scratch[3:]
-    loads = [pltpu.make_async_copy(src, dst, in_sem.at[i]) for i, (src, dst) in enumerate(zip(inputs, copies))]
+def first_entries_kernel(*refs, column_leaves, row_leaves, leaf, parts, indices):
+    fill_ref, inputs, index_inputs = refs[0], refs[1:6], refs[6 : 6 + indices]
+    outputs, scratch = refs[6 + indices : 9 + parts + 2 * indices], refs[9 + parts + 2 * indices :]
+    entries_refs, (table_ref, s_ref, t_ref), index_outputs = outputs[:parts], outputs[parts : parts + 3], outputs[parts + 3 :]
+    copies, (list_ref, sem, in_sem) = scratch[:5], scratch[5:]
+    moves = list(zip(inputs, copies)) + list(zip(index_inputs, index_outputs))
+    loads = [pltpu.make_async_copy(src, dst, in_sem.at[i]) for i, (src, dst) in enumerate(moves)]
     for load in loads:
         load.start()
-    spts_ref, area_ref, tpts_ref = copies
-    build_list(ids_ref, list_ref, (row_leaves // 2) * column_leaves)
+    nsrc_ref, ntgt_ref, spts_ref, area_ref, tpts_ref = copies
+    for load in loads[:2]:
+        load.wait()
+    used = lax.broadcasted_iota(jnp.int32, nsrc_ref.shape, 1) < fill_ref[0, 0]
+    ids = jnp.where(used, ntgt_ref[...] * column_leaves + nsrc_ref[...], -1)
+    build_list(ids, list_ref, (row_leaves // 2) * column_leaves)
     copy = pltpu.make_async_copy(list_ref, table_ref, sem)
     copy.start()
-    for load in loads:
+    for load in loads[2:]:
         load.wait()
 
     tx, ty, tz = (tpts_ref[i : i + 1, :] - 0.5 for i in range(3))
@@ -145,32 +151,33 @@
 HBM = pl.BlockSpec(memory_space=pltpu.HBM)
 
 
-def first_entries(ids, source_points, source_areas, target_points, column_leaves, row_leaves):
-    slots = ids.shape[1]
+def first_entries(near_fill, near_source, near_target, source_points, source_areas, target_points, indices, leaves):
+    column_leaves, row_leaves = leaves
+    slots = near_source.shape[1]
     leaf = source_points.shape[1] // column_leaves
     depth = 64
-    inputs = tuple(
-        pltpu.with_memory_space_constraint(value, pltpu.HBM)
-        for value in (source_points, source_areas[None, :], target_points)
-    )
+    inputs = (near_source, near_target, source_points, source_areas[None, :], target_points)
+    hbm_inputs = tuple(pltpu.with_memory_space_constraint(value, pltpu.HBM) for value in inputs + tuple(indices))
     return pl.pallas_call(
         functools.partial(
-            first_entries_kernel, column_leaves=column_leaves, row_leaves=row_leaves, leaf=leaf, parts=2
+            first_entries_kernel, column_leaves=column_leaves, row_leaves=row_leaves, leaf=leaf, parts=2,
+            indices=len(indices),
         ),
         out_shape=(pltpu.VMEM((slots // 4, leaf, leaf), BF16),) * 2
         + (
             pltpu.SMEM((8, slots), jnp.int32),
             pltpu.VMEM((column_leaves, leaf, 128), BF16),
             pltpu.VMEM((row_leaves, depth, leaf), BF16),
-        ),
-        in_specs=[VMEM] + [HBM] * len(inputs),
-        out_specs=(VMEM, VMEM, SMEM, VMEM, VMEM),
+        )
+        + tuple(pltpu.SMEM(value.shape, jnp.int32) for value in indices),
+        in_specs=[SMEM] + [HBM] * len(hbm_inputs),
+        out_specs=(VMEM, VMEM, SMEM, VMEM, VMEM) + (SMEM,) * len(indices),
         scratch_shapes=[pltpu.VMEM(value.shape, value.dtype) for value in inputs]
-        + [pltpu.VMEM((8, slots), jnp.int32), pltpu.SemaphoreType.DMA, pltpu.SemaphoreType.DMA((len(inputs),))],
+        + [pltpu.VMEM((8, slots), jnp.int32), pltpu.SemaphoreType.DMA, pltpu.SemaphoreType.DMA((len(hbm_inputs),))],
         compiler_params=pltpu.CompilerParams(vmem_limit_bytes=10 << 20),
         cost_estimate=pl.CostEstimate(flops=8_000_000_000, bytes_accessed=1 << 20, transcendentals=0),
         name="entries",
-    )(ids, *inputs)
+    )(near_fill, *hbm_inputs)
 
 
 def second_entries(table, s_features, t_features):
@@ -235,10 +242,10 @@
             acc_ref[t] = acc_ref[t] + blocks[u]
 
 
-def near_kernel(*refs, groups, chunk, chunks, plain):
+def near_kernel(*refs, groups, chunk, chunks, plain, out_carried):
     (table_ref, tfill_ref, far_ref, x_ref) = refs[:4]
     entries_refs = refs[4 : 4 + 2 * groups]
-    carried = 1 if chunk > 0 and not plain else 0
+    carried = len(out_carried)
     carried_refs = refs[4 + 2 * groups : 4 + 2 * groups + carried]
     out_refs, acc_ref = refs[4 + 2 * groups + carried : -1], refs[-1]
     chunk_leaves, rhs, leaf = acc_ref.shape
@@ -301,7 +308,7 @@
             start = pl.multiple_of((base ^ m) * height, height)
             shift = out_refs[m].shape[1] - chunk_leaves * leaf
             if shift:
-                out_refs[m][:, :shift] = carried_refs[0][...]
+                out_refs[m][:, :shift] = carried_refs[out_carried.index(m)][...]
             for t in range(chunk_leaves):
                 value = acc_ref[t, pl.ds(start, height), :] + far_ref[base_leaf + t, pl.ds(start, height), :]
                 value = jnp.where(lane_t < tfill_ref[base_leaf + t], value, 0.0)
@@ -328,7 +335,7 @@
     )(source_fill, far_source, far_target, far_rank, left, right, *pieces)
 
 
-def near_field(table, target_fill, far, x, entries, owners, plain, chunk, chunks, carried=()):
+def near_field(table, target_fill, far, x, entries, owners, plain, chunk, chunks, carried=(), out_carried=()):
     row_leaves, rhs, leaf = far.shape
     width = row_leaves // chunks * leaf
     if plain:
@@ -336,12 +343,12 @@
     else:
         out_shape = tuple(
             jax.ShapeDtypeStruct(
-                (rhs // owners, width + (carried[0].shape[1] if m == 1 and carried else 0)), F32 if m == 0 else BF16
+                (rhs // owners, width + (carried[0].shape[1] if m in out_carried else 0)), F32 if m == 0 else BF16
             )
             for m in range(owners)
         )
     return pl.pallas_call(
-        functools.partial(near_kernel, groups=len(entries) // 2, chunk=chunk, chunks=chunks, plain=plain),
+        functools.partial(near_kernel, groups=len(entries) // 2, chunk=chunk, chunks=chunks, plain=plain, out_carried=tuple(out_carried)),
         out_shape=out_shape,
         in_specs=[SMEM] * 2 + [VMEM] * (2 + len(entries) + len(carried)),
         out_specs=(VMEM,) * len(out_shape),
@@ -365,12 +372,13 @@
             return lax.ppermute(value, axis, [(i, i ^ mask) for i in range(size)])
 
         pieces = [charges] + [swap(charges, "row", rows, mask) for mask in range(2, rows, 2)]
-    used = jnp.arange(near_source.shape[1])[None, :] < near_fill
-    ids = jnp.where(used, near_target * source_fill.shape[0] + near_source, -1)
-    row_leaves = target_fill.shape[0]
-    *entries, table, s_features, t_features = first_entries(
-        ids, source_points, source_areas, target_points, source_fill.shape[0], row_leaves
-    )
+    row_leaves, column_leaves = target_fill.shape[0], source_fill.shape[0]
+    first_outs = first_entries(
+        near_fill, near_source, near_target, source_points, source_areas, target_points,
+        (source_fill, target_fill, far_source, far_target, far_rank), (column_leaves, row_leaves),
+    )
+    entries, (table, s_features, t_features) = list(first_outs[:2]), first_outs[2:5]
+    source_fill, target_fill, far_source, far_target, far_rank = first_outs[5:]
     if not plain:
         pieces, table = lax.optimization_barrier((pieces, table))
         pieces = pieces + [swap(piece, "row", rows, 1) for piece in pieces]
@@ -392,14 +400,18 @@
     def exchange(value, mask):
         return swap(value, "col", columns, mask)
 
+    far_masks = tuple(range(2, columns))
     first = near_field(table, target_fill, far, x, entries, columns, plain, 0, 2)
-    early = [exchange(first[mask], mask) for mask in reversed(range(2, columns))]
-    second = near_field(table, target_fill, far, x, entries, columns, plain, 1, 2, (first[1],))
-    neighbour = exchange(second[1], 1)
-    late = [exchange(second[mask], mask) for mask in reversed(range(2, columns))]
-    result = jnp.concatenate([first[0], second[0]], axis=1) + neighbour.astype(F32)
-    for a, b in zip(early, late):
-        result = result + jnp.concatenate([a, b], axis=1).astype(F32)
+    early = exchange(first[1], 1)
+    second = near_field(
+        table, target_fill, far, x, entries, columns, plain, 1, 2, [first[m] for m in far_masks], far_masks
+    )
+    late = [exchange(second[mask], mask) for mask in reversed(far_masks)]
+    late_neighbour = exchange(second[1], 1)
+    result = jnp.concatenate([first[0], second[0]], axis=1)
+    result = result + jnp.concatenate([early, late_neighbour], axis=1).astype(F32)
+    for value in late:
+        result = result + value.astype(F32)
     return result
 
 

time: 44.9 us -> 40.5 us (0.902)
  starting transfers between devices: 11.5 us -> 9.13 us
  Pallas kernels: 22.3 us -> 20.7 us
  other arithmetic: 1.46 us -> 0.76 us
    ppermute x12 -> x11, starting transfers between devices: 11.5 us -> 9.13 us  [swap(): return lax.ppermute(value, axis, [(i, i ^ mask) for i in range(size)])]
    pallas_call x2, Pallas kernels: 7.5 us -> 6.22 us  [near_field(): pl.pallas_call(functools.partial(near_kernel, groups=len(entries) // 2, c...]
    select_n x1 -> x0, other arithmetic: 0.7 us -> none  [shards(): ids = jnp.where(used, near_target * source_fill.shape[0] + near_source, -1)]
    pallas_call x1, Pallas kernels: 3.43 us -> 2.86 us  [far_field(): pl.pallas_call(functools.partial(far_kernel, pieces=len(pieces), plain=pl...]
    ppermute x12 -> x11, waiting for transfers between devices: 8.46 us -> 8.86 us  [swap(): return lax.ppermute(value, axis, [(i, i ^ mask) for i in range(size)])]
  transfers between devices with their start and end apart: 12 -> 11, of which waited for: 2 -> 2; matrix products, arithmetic and copies ran while one was open for 2% -> 0% of each run, Pallas kernels for 25% -> 29%
where the time goes in v1:
time: 40.5 us; the launch traced here: 40.3 us
  Pallas kernels  20.7 us (51%)
  starting transfers between devices  9.13 us (23%)
  waiting for transfers between devices  8.86 us (22%)
  between operations  0.81 us (2%)
  other arithmetic  0.76 us (2%)
    ppermute x11, starting transfers between devices, swap(): return lax.ppermute(value, axis, [(i, i ^ mask) for i in range(size)])  9.13 us
    ppermute x11, waiting for transfers between devices, swap(): return lax.ppermute(value, axis, [(i, i ^ mask) for i in range(size)])  8.86 us
    pallas_call x1, Pallas kernels, first_entries(): pl.pallas_call(functools.partial(first_entries_kernel, column_leaves=colu...  8.11 us
    pallas_call x2, Pallas kernels, near_field(): pl.pallas_call(functools.partial(near_kernel, groups=len(entries) // 2, c...  6.22 us
    pallas_call x1, Pallas kernels, second_entries(): pl.pallas_call(second_entries_kernel, out_shape=(pltpu.VMEM((slots // 4,...  3.54 us
    pallas_call x1, Pallas kernels, far_field(): pl.pallas_call(functools.partial(far_kernel, pieces=len(pieces), plain=pl...  2.86 us
  transfers between devices with their start and end apart: 11, of which 2 were waited for; matrix products, arithmetic and copies ran while one was open for 0% of the time, Pallas kernels for 29%

profile of v1, /device:TPU:0, one launch (start us, length us, event | category | flops | bytes accessed | tf_op | source)
XLA Modules:
  0.0 40.3 jit_solution(16091573492006204663)
XLA Ops:
  0.0 3.0 %collective-permute-start = (bf16[8,8192]{1,0:T(8,128)(2,1)}, bf16[8,8192]{1,0:T(8,128)(2,1)S(1)}, u32[]{:S(2)}, u32[]{:S(2)}) collective-permute-start(bf16[8,8192]{1,0:T(8,128)(2,1)} %refs_6_.2), channel_id=1, source_target_pairs={{0,8},{4,12},{8,0},{12,4},{16,24},{20,28},{24,16},{28,20},{1,9},{5... | collective-permute-start | bytes 393224 | tf_op jit(solution)/shard_map/ppermute | solution.py:372
  3.0 1.5 %collective-permute-start.1 = (bf16[8,8192]{1,0:T(8,128)(2,1)}, bf16[8,8192]{1,0:T(8,128)(2,1)S(1)}, u32[]{:S(2)}, u32[]{:S(2)}) collective-permute-start(bf16[8,8192]{1,0:T(8,128)(2,1)} %refs_6_.2), channel_id=1, source_target_pairs={{0,16},{4,20},{8,24},{12,28},{16,0},{20,4},{24,8},{28,12},{1,17},{... | collective-permute-start | bytes 393224 | tf_op jit(solution)/shard_map/ppermute | solution.py:372
  4.5 0.0 collective-permute-start.2
  5.1 0.0 copy-start.2
  5.2 8.1 %entries.1 = (bf16[64,256,256]{2,1,0:T(8,128)(2,1)S(1)}, bf16[64,256,256]{2,1,0:T(8,128)(2,1)S(1)}, s32[8,256]{1,0:T(8,128)S(4)}, bf16[32,256,128]{2,1,0:T(8,128...) custom-call(s32[1,1]{1,0:T(1,128)S(6)} %copy.15.refs_0_, ...), custom_call_target="tpu_custom_call" | custom-call | flops 8000000000 | bytes 1048576 | tf_op jit(solution)/shard_map/entries/pallas_call | solution.py:161
  13.3 0.0 collective-permute-done.refs_7_
  13.3 0.0 collective-permute-done.1.refs_8_
  13.3 0.0 collective-permute-done.2.refs_9_
  13.3 0.0 copy-done.2
  13.3 0.1 collective-permute-start.3
  13.4 0.5 %collective-permute-start.4 = (bf16[8,8192]{1,0:T(8,128)(2,1)S(1)}, bf16[8,8192]{1,0:T(8,128)(2,1)S(1)}, u32[]{:S(2)}, u32[]{:S(2)}) collective-permute-start(bf16[8,8192]{1,0:T(8,128)(2,1)S(1)} %collective-permute-done.refs_7_), channel_id=1, source_target_pairs={{0,4},{4,0},{8,12},{12,8},{16,20},{20,16},{24,28},{28,24},{1,5},{5... | collective-permute-start | bytes 393224 | tf_op jit(solution)/shard_map/ppermute | solution.py:372
  13.9 0.1 collective-permute-start.5
  14.0 0.4 %collective-permute-start.6 = (bf16[8,8192]{1,0:T(8,128)(2,1)S(1)}, bf16[8,8192]{1,0:T(8,128)(2,1)S(1)}, u32[]{:S(2)}, u32[]{:S(2)}) collective-permute-start(bf16[8,8192]{1,0:T(8,128)(2,1)S(1)} %collective-permute-done.2.refs_9_), channel_id=1, source_target_pairs={{0,4},{4,0},{8,12},{12,8},{16,20},{20,16},{24,28},{28,24},{1,5},{5... | collective-permute-start | bytes 393224 | tf_op jit(solution)/shard_map/ppermute | solution.py:372
  14.4 0.0 copy-start
  14.4 0.0 copy-start.1
  14.4 3.5 %entries_rest.1 = (bf16[64,256,256]{2,1,0:T(8,128)(2,1)S(1)}, bf16[64,256,256]{2,1,0:T(8,128)(2,1)S(1)}) custom-call(s32[8,256]{1,0:T(8,128)S(4)} %get-tuple-element.42.table_ref.refs_0_, bf16[32,256,128]{2,1,0:T(8,128)(2,1)S(1)} %get-tuple-element.52.s_ref, bf16[16,64,256]{2,1,0:T(8,128)(2,1)S(1)} %get-tuple-element.53.t_ref), custom_call_target="tpu_custom_call" | custom-call | flops 8000000000 | bytes 1048576 | tf_op jit(solution)/shard_map/entries_rest/pallas_call | solution.py:186
  18.0 0.0 collective-permute-done.3.refs_10_
  18.0 0.0 collective-permute-done.4.refs_11_
  18.0 0.0 collective-permute-done.5.refs_12_
  18.0 0.0 collective-permute-done.6.refs_13_
  18.0 0.0 copy-done
  18.0 0.0 copy-done.1
  18.0 2.9 %far.1 = (bf16[32,64,256]{2,1,0:T(8,128)(2,1)S(1)}, f32[16,64,256]{2,1,0:T(8,128)S(1)}) custom-call(s32[32]{0:T(128)S(4)} %get-tuple-element.44.refs_0_, s32[1,96]{1,0:T(1,128)S(4)} %get-tuple-element.45.refs_1_, s32[1,96]{1,0:T(1,128)S(4)} %get-tuple-element.46.refs_2_, s32[1,96]{1,0:T(1,128)S(4)} %get-tuple-element.47.refs_3_, ...), custom_call_target="tpu_custom_call" | custom-call | flops 2000000000 | bytes 8388608 | tf_op jit(solution)/shard_map/far/pallas_call | solution.py:326
  20.9 2.7 %near.2 = (f32[16,2048]{1,0:T(8,128)S(1)}, bf16[16,2048]{1,0:T(8,128)(2,1)S(1)}, bf16[16,2048]{1,0:T(8,128)(2,1)S(1)}, bf16[16,2048]{1,0:T(8,128)(2,1)S(1)}) custom-call(s32[8,256]{1,0:T(8,128)S(4)} %get-tuple-element.42.table_ref.refs_0_, s32[16]{0:T(128)S(4)} %get-tuple-element.43.refs_1_, f32[16,64,256]{2,1,0:T(8,128)S(1)} %get-tuple-element.63.refs_2_, ...), custom_call_target="tpu_custom_call" | custom-call | flops 4000000000 | bytes 8388608 | tf_op jit(solution)/shard_map/near/pallas_call | solution.py:350
  23.5 3.6 %near.3 = (f32[16,2048]{1,0:T(8,128)S(1)}, bf16[16,2048]{1,0:T(8,128)(2,1)S(1)}, bf16[16,4096]{1,0:T(8,128)(2,1)S(1)}, bf16[16,4096]{1,0:T(8,128)(2,1)S(1)}) custom-call(s32[8,256]{1,0:T(8,128)S(4)} %get-tuple-element.42.table_ref.refs_0_, s32[16]{0:T(128)S(4)} %get-tuple-element.43.refs_1_, f32[16,64,256]{2,1,0:T(8,128)S(1)} %get-tuple-element.63.refs_2_, ...), custom_call_target="tpu_custom_call" | custom-call | flops 4000000000 | bytes 8388608 | tf_op jit(solution)/shard_map/near/pallas_call | solution.py:350
  27.1 0.1 collective-permute-start.10
  27.2 0.1 collective-permute-start.9
  27.3 3.4 %collective-permute-start.8 = (bf16[16,2048]{1,0:T(8,128)(2,1)S(1)}, bf16[16,2048]{1,0:T(8,128)(2,1)S(1)}, u32[]{:S(2)}, u32[]{:S(2)}) collective-permute-start(bf16[16,2048]{1,0:T(8,128)(2,1)S(1)} %get-tuple-element.74), channel_id=1, source_target_pairs={{0,1},{1,0},{2,3},{3,2},{4,5},{5,4},{6,7},{7,6},{8,9},{9,8},{10,11... | collective-permute-start | bytes 196616 | tf_op jit(solution)/shard_map/ppermute | solution.py:372
  30.7 0.0 collective-permute-start.7
  30.7 7.5 %collective-permute-done.8 = bf16[16,2048]{1,0:T(8,128)(2,1)S(1)} collective-permute-done((bf16[16,2048]{1,0:T(8,128)(2,1)S(1)}, bf16[16,2048]{1,0:T(8,128)(2,1)S(1)}, u32[]{:S(2)}, u32[]{:S(2)}) %collective-permute-start.8) | collective-permute-done | bytes 65568 | tf_op jit(solution)/shard_map/ppermute | solution.py:372
  38.2 1.3 %collective-permute-done.7 = bf16[16,2048]{1,0:T(8,128)(2,1)S(1)} collective-permute-done((bf16[16,2048]{1,0:T(8,128)(2,1)S(1)}, bf16[16,2048]{1,0:T(8,128)(2,1)S(1)}, u32[]{:S(2)}, u32[]{:S(2)}) %collective-permute-start.7) | collective-permute-done | bytes 65568 | tf_op jit(solution)/shard_map/ppermute | solution.py:372
  39.5 0.0 collective-permute-done.10
  39.5 0.0 collective-permute-done.9
  39.5 0.8 %fusion.1 = f32[16,4096]{1,0:T(8,128)} fusion(f32[16,2048]{1,0:T(8,128)S(1)} %get-tuple-element.72, f32[16,2048]{1,0:T(8,128)S(1)} %get-tuple-element.69, bf16[16,4096]{1,0:T(8,128)(2,1)S(1)} %collective-permute-done.10, bf16[16,4096]{1,0:T(8,128)(2,1)S(1)} %collective-permute-done.9, bf16[16,2048]{1,0:T(8,128)(2,1)S(1)} %collective-permute-done.8, ...), kind=kLoop, calls=%fused_computation.2 | loop fusion | flops 655360 | bytes 917504 | tf_op jit(solution)/shard_map/add | solution.py:414
Async XLA Ops:
  0.0 13.3 %collective-permute-start = (bf16[8,8192]{1,0:T(8,128)(2,1)}, bf16[8,8192]{1,0:T(8,128)(2,1)S(1)}, u32[]{:S(2)}, u32[]{:S(2)}) collective-permute-start(bf16[8,8192]{1,0:T(8,128)(2,1)} %refs_6_.2), channel_id=1, source_target_pairs={{0,8},{4,12},{8,0},{12,4},{16,24},{20,28},{24,16},{28,20},{1,9},{5... | collective-permute-start | bytes 393224 | tf_op jit(solution)/shard_map/ppermute | solution.py:372
  3.0 10.3 %collective-permute-start.1 = (bf16[8,8192]{1,0:T(8,128)(2,1)}, bf16[8,8192]{1,0:T(8,128)(2,1)S(1)}, u32[]{:S(2)}, u32[]{:S(2)}) collective-permute-start(bf16[8,8192]{1,0:T(8,128)(2,1)} %refs_6_.2), channel_id=1, source_target_pairs={{0,16},{4,20},{8,24},{12,28},{16,0},{20,4},{24,8},{28,12},{1,17},{... | collective-permute-start | bytes 393224 | tf_op jit(solution)/shard_map/ppermute | solution.py:372
  4.5 8.8 %collective-permute-start.2 = (bf16[8,8192]{1,0:T(8,128)(2,1)}, bf16[8,8192]{1,0:T(8,128)(2,1)S(1)}, u32[]{:S(2)}, u32[]{:S(2)}) collective-permute-start(bf16[8,8192]{1,0:T(8,128)(2,1)} %refs_6_.2), channel_id=1, source_target_pairs={{0,24},{4,28},{8,16},{12,20},{16,8},{20,12},{24,0},{28,4},{1,25},{... | collective-permute-start | bytes 393224 | tf_op jit(solution)/shard_map/ppermute | solution.py:372
  5.1 8.2 %copy-start.2 = (bf16[8,8192]{1,0:T(8,128)(2,1)S(1)}, bf16[8,8192]{1,0:T(8,128)(2,1)}, u32[]{:S(2)}) copy-start(bf16[8,8192]{1,0:T(8,128)(2,1)} %refs_6_.2) | copy-start | bytes 393220
  13.3 4.6 %collective-permute-start.3 = (bf16[8,8192]{1,0:T(8,128)(2,1)S(1)}, bf16[8,8192]{1,0:T(8,128)(2,1)S(1)}, u32[]{:S(2)}, u32[]{:S(2)}) collective-permute-start(bf16[8,8192]{1,0:T(8,128)(2,1)S(1)} %copy-done.2), channel_id=1, source_target_pairs={{0,4},{4,0},{8,12},{12,8},{16,20},{20,16},{24,28},{28,24},{1,5},{5... | collective-permute-start | bytes 393224 | tf_op jit(solution)/shard_map/ppermute | solution.py:372
  13.4 4.6 %collective-permute-start.4 = (bf16[8,8192]{1,0:T(8,128)(2,1)S(1)}, bf16[8,8192]{1,0:T(8,128)(2,1)S(1)}, u32[]{:S(2)}, u32[]{:S(2)}) collective-permute-start(bf16[8,8192]{1,0:T(8,128)(2,1)S(1)} %collective-permute-done.refs_7_), channel_id=1, source_target_pairs={{0,4},{4,0},{8,12},{12,8},{16,20},{20,16},{24,28},{28,24},{1,5},{5... | collective-permute-start | bytes 393224 | tf_op jit(solution)/shard_map/ppermute | solution.py:372
  13.9 4.1 %collective-permute-start.5 = (bf16[8,8192]{1,0:T(8,128)(2,1)S(1)}, bf16[8,8192]{1,0:T(8,128)(2,1)S(1)}, u32[]{:S(2)}, u32[]{:S(2)}) collective-permute-start(bf16[8,8192]{1,0:T(8,128)(2,1)S(1)} %collective-permute-done.1.refs_8_), channel_id=1, source_target_pairs={{0,4},{4,0},{8,12},{12,8},{16,20},{20,16},{24,28},{28,24},{1,5},{5... | collective-permute-start | bytes 393224 | tf_op jit(solution)/shard_map/ppermute | solution.py:372
  14.0 4.0 %collective-permute-start.6 = (bf16[8,8192]{1,0:T(8,128)(2,1)S(1)}, bf16[8,8192]{1,0:T(8,128)(2,1)S(1)}, u32[]{:S(2)}, u32[]{:S(2)}) collective-permute-start(bf16[8,8192]{1,0:T(8,128)(2,1)S(1)} %collective-permute-done.2.refs_9_), channel_id=1, source_target_pairs={{0,4},{4,0},{8,12},{12,8},{16,20},{20,16},{24,28},{28,24},{1,5},{5... | collective-permute-start | bytes 393224 | tf_op jit(solution)/shard_map/ppermute | solution.py:372
  14.4 3.6 %copy-start = (bf16[1,96,32,256]{3,2,1,0:T(8,128)(2,1)S(1)}, bf16[1,96,32,256]{3,2,1,0:T(8,128)(2,1)}, u32[]{:S(2)}) copy-start(bf16[1,96,32,256]{3,2,1,0:T(8,128)(2,1)} %param.26) | copy-start | bytes 4718596
  14.4 3.6 %copy-start.1 = (bf16[1,96,32,256]{3,2,1,0:T(8,128)(2,1)S(1)}, bf16[1,96,32,256]{3,2,1,0:T(8,128)(2,1)}, u32[]{:S(2)}) copy-start(bf16[1,96,32,256]{3,2,1,0:T(8,128)(2,1)} %param.27) | copy-start | bytes 4718596
  27.1 12.4 %collective-permute-start.10 = (bf16[16,4096]{1,0:T(8,128)(2,1)S(1)}, bf16[16,4096]{1,0:T(8,128)(2,1)S(1)}, u32[]{:S(2)}, u32[]{:S(2)}) collective-permute-start(bf16[16,4096]{1,0:T(8,128)(2,1)S(1)} %get-tuple-element.76), channel_id=1, source_target_pairs={{0,2},{1,3},{2,0},{3,1},{4,6},{5,7},{6,4},{7,5},{8,10},{9,11},{10,... | collective-permute-start | bytes 393224 | tf_op jit(solution)/shard_map/ppermute | solution.py:372
  27.2 12.3 %collective-permute-start.9 = (bf16[16,4096]{1,0:T(8,128)(2,1)S(1)}, bf16[16,4096]{1,0:T(8,128)(2,1)S(1)}, u32[]{:S(2)}, u32[]{:S(2)}) collective-permute-start(bf16[16,4096]{1,0:T(8,128)(2,1)S(1)} %get-tuple-element.75), channel_id=1, source_target_pairs={{0,3},{1,2},{2,1},{3,0},{4,7},{5,6},{6,5},{7,4},{8,11},{9,10},{10,... | collective-permute-start | bytes 393224 | tf_op jit(solution)/shard_map/ppermute | solution.py:372
  27.3 10.9 %collective-permute-start.8 = (bf16[16,2048]{1,0:T(8,128)(2,1)S(1)}, bf16[16,2048]{1,0:T(8,128)(2,1)S(1)}, u32[]{:S(2)}, u32[]{:S(2)}) collective-permute-start(bf16[16,2048]{1,0:T(8,128)(2,1)S(1)} %get-tuple-element.74), channel_id=1, source_target_pairs={{0,1},{1,0},{2,3},{3,2},{4,5},{5,4},{6,7},{7,6},{8,9},{9,8},{10,11... | collective-permute-start | bytes 196616 | tf_op jit(solution)/shard_map/ppermute | solution.py:372
  30.7 8.9 %collective-permute-start.7 = (bf16[16,2048]{1,0:T(8,128)(2,1)S(1)}, bf16[16,2048]{1,0:T(8,128)(2,1)S(1)}, u32[]{:S(2)}, u32[]{:S(2)}) collective-permute-start(bf16[16,2048]{1,0:T(8,128)(2,1)S(1)} %get-tuple-element.73), channel_id=1, source_target_pairs={{0,1},{1,0},{2,3},{3,2},{4,5},{5,4},{6,7},{7,6},{8,9},{9,8},{10,11... | collective-permute-start | bytes 196616 | tf_op jit(solution)/shard_map/ppermute | solution.py:372

commit v2 on v1

--- a/solution.py
+++ b/solution.py
@@ -62,45 +62,87 @@
     list_ref[...] = table.astype(jnp.int32)
 
 
-def entry_loop(table_ref, s_ref, t_ref, entries_refs, first, last):
-    parts = len(entries_refs)
+def entry_loop(table_ref, s_ref, t_ref, entries_ref, base, low, high):
     column_leaves, leaf, width = s_ref.shape
     depth = t_ref.shape[1]
-    rows = 8 // parts
-    trips = (last - first + 7) // 8
+    start, stop = (low - base) // 8, (high - base + 7) // 8
 
     def work(*accs):
-        for acc in accs:
-            pltpu.matmul_pop(acc)
-
         def drain(u, turn):
-            row = jnp.maximum(turn * rows + u // parts, 0)
-            entries_refs[u % parts][row] = lax.rsqrt(pltpu.matmul_pop(accs[u])).astype(BF16)
-
-        @pl.loop(0, trips)
-        def _(turn):
-            for u in range(8):
-                pair = table_ref[0, first + turn * 8 + u]
-                rhs = jnp.concatenate([t_ref[pair // column_leaves], jnp.zeros((leaf - depth, leaf), BF16)], axis=0)
-                lhs = jnp.concatenate([s_ref[pair % column_leaves], jnp.zeros((leaf, leaf - width), BF16)], axis=1)
-                stage = (u // 2) % 2
-                pltpu.matmul_push_rhs(rhs, staging_register=stage, mxu_index=u % 2)
-                pltpu.matmul_acc_lhs(accs[u], lhs, load_staged_rhs=stage)
-                if u < 4:
-                    drain(u + 4, turn - 1)
-                else:
-                    drain(u - 4, turn)
-
-        for u in range(4, 8):
-            drain(u, trips - 1)
+            row = jnp.maximum(turn * 8 + u, 0)
+            entries_ref[row] = lax.rsqrt(pltpu.matmul_pop(accs[u])).astype(BF16)
+
+        @pl.when(stop > start)
+        def _():
+            for acc in accs:
+                pltpu.matmul_pop(acc)
+
+            @pl.loop(start, stop)
+            def _(turn):
+                for u in range(8):
+                    pair = table_ref[0, base + turn * 8 + u]
+                    rhs = jnp.concatenate([t_ref[pair // column_leaves], jnp.zeros((leaf - depth, leaf), BF16)], axis=0)
+                    lhs = jnp.concatenate([s_ref[pair % column_leaves], jnp.zeros((leaf, leaf - width), BF16)], axis=1)
+                    stage = (u // 2) % 2
+                    pltpu.matmul_push_rhs(rhs, staging_register=stage, mxu_index=u % 2)
+                    pltpu.matmul_acc_lhs(accs[u], lhs, load_staged_rhs=stage)
+                    if u < 4:
+                        drain(u + 4, turn - 1)
+                    else:
+                        drain(u - 4, turn)
+
+            for u in range(4, 8):
+                drain(u, stop - 1)
 
     pl.run_scoped(work, *[pltpu.ACC(u % 2)((leaf, leaf), F32) for u in range(8)])
 
 
-def first_entries_kernel(*refs, column_leaves, row_leaves, leaf, parts, indices):
+def near_loop(table_ref, x_ref, entries, acc_ref, base_leaf, low, high):
+    chunk_leaves, rhs, leaf = acc_ref.shape
+    column_leaves = x_ref.shape[0]
+
+    def work(*accs):
+        def drain(u, k):
+            inside = (k >= low) & (k < high)
+            slot = jnp.maximum(k, 0)
+            t = jnp.clip(table_ref[0, slot] // column_leaves - base_leaf, 0, chunk_leaves - 1)
+            copies = jnp.where(inside, table_ref[1, slot], 0).astype(F32)
+            block = pltpu.matmul_pop(accs[u])
+            acc_ref[t] = acc_ref[t] + jnp.where(inside, block * copies, 0.0)
+
+        @pl.when(high > low)
+        def _():
+            for acc in accs:
+                pltpu.matmul_pop(acc)
+
+            for entries_ref, base in entries:
+                end = base + entries_ref.shape[0]
+                start, stop = jnp.clip(low, base, end) // 16, (jnp.clip(high, base, end) + 15) // 16
+
+                @pl.loop(start, stop)
+                def _(turn):
+                    for u in range(16):
+                        k = turn * 16 + u
+                        source = table_ref[0, k] % column_leaves
+                        stage = (u // 2) % 2
+                        pltpu.matmul_push_rhs(entries_ref[k - base], staging_register=stage, mxu_index=u % 2)
+                        pltpu.matmul_acc_lhs(accs[u], x_ref[source], load_staged_rhs=stage)
+                        if u >= 8:
+                            drain(u - 8, k - 8)
+                        else:
+                            drain(u + 8, k - 8)
+
+            end = (high + 15) // 16 * 16
+            for u in range(8, 16):
+                drain(u, end - 16 + u)
+
+    pl.run_scoped(work, *[pltpu.ACC(u % 2)((rhs, leaf), F32) for u in range(16)])
+
+
+def first_entries_kernel(*refs, column_leaves, row_leaves, leaf, indices):
     fill_ref, inputs, index_inputs = refs[0], refs[1:6], refs[6 : 6 + indices]
-    outputs, scratch = refs[6 + indices : 9 + parts + 2 * indices], refs[9 + parts + 2 * indices :]
-    entries_refs, (table_ref, s_ref, t_ref), index_outputs = outputs[:parts], outputs[parts : parts + 3], outputs[parts + 3 :]
+    outputs, scratch = refs[6 + indices : 10 + 2 * indices], refs[10 + 2 * indices :]
+    (entries_ref, table_ref, s_ref, t_ref), index_outputs = outputs[:4], outputs[4:]
     copies, (list_ref, sem, in_sem) = scratch[:5], scratch[5:]
     moves = list(zip(inputs, copies)) + list(zip(index_inputs, index_outputs))
     loads = [pltpu.make_async_copy(src, dst, in_sem.at[i]) for i, (src, dst) in enumerate(moves)]
@@ -114,7 +156,7 @@
     build_list(ids, list_ref, (row_leaves // 2) * column_leaves)
     copy = pltpu.make_async_copy(list_ref, table_ref, sem)
     copy.start()
-    for load in loads[2:]:
+    for load in loads[2:5]:
         load.wait()
 
     tx, ty, tz = (tpts_ref[i : i + 1, :] - 0.5 for i in range(3))
@@ -137,18 +179,29 @@
         s_ref[s] = jnp.concatenate([column, jnp.zeros((leaf, 128 - column.shape[1]), BF16)], axis=1)
 
     copy.wait()
-    group = parts * entries_refs[0].shape[0]
-    entry_loop(table_ref, s_ref, t_ref, entries_refs, 0, jnp.minimum(table_ref[2, 0], group))
-
-
-def second_entries_kernel(table_ref, s_ref, t_ref, *entries_refs):
-    first = table_ref.shape[1] - len(entries_refs) * entries_refs[0].shape[0]
-    entry_loop(table_ref, s_ref, t_ref, entries_refs, first, jnp.maximum(table_ref[2, 0], first))
+    entry_loop(table_ref, s_ref, t_ref, entries_ref, 0, 0, jnp.minimum(table_ref[2, 0], entries_ref.shape[0]))
+    for load in loads[5:]:
+        load.wait()
+
+
+def second_entries_kernel(table_ref, s_ref, t_ref, entries_ref, *, first):
+    total = table_ref[2, 0]
+    entry_loop(
+        table_ref, s_ref, t_ref, entries_ref, first, first, jnp.clip(total, first, first + entries_ref.shape[0])
+    )
 
 
 VMEM = pl.BlockSpec(memory_space=pltpu.VMEM)
 SMEM = pl.BlockSpec(memory_space=pltpu.SMEM)
 HBM = pl.BlockSpec(memory_space=pltpu.HBM)
+
+
+def first_count(slots):
+    return max(slots * 3 // 8 // 16 * 16, 16)
+
+
+def second_count(slots):
+    return max(slots // 8 // 16 * 16, 16)
 
 
 def first_entries(near_fill, near_source, near_target, source_points, source_areas, target_points, indices, leaves):
@@ -160,18 +213,18 @@
     hbm_inputs = tuple(pltpu.with_memory_space_constraint(value, pltpu.HBM) for value in inputs + tuple(indices))
     return pl.pallas_call(
         functools.partial(
-            first_entries_kernel, column_leaves=column_leaves, row_leaves=row_leaves, leaf=leaf, parts=2,
+            first_entries_kernel, column_leaves=column_leaves, row_leaves=row_leaves, leaf=leaf,
             indices=len(indices),
         ),
-        out_shape=(pltpu.VMEM((slots // 4, leaf, leaf), BF16),) * 2
-        + (
+        out_shape=(
+            pltpu.VMEM((first_count(slots), leaf, leaf), BF16),
             pltpu.SMEM((8, slots), jnp.int32),
             pltpu.VMEM((column_leaves, leaf, 128), BF16),
             pltpu.VMEM((row_leaves, depth, leaf), BF16),
         )
         + tuple(pltpu.SMEM(value.shape, jnp.int32) for value in indices),
         in_specs=[SMEM] + [HBM] * len(hbm_inputs),
-        out_specs=(VMEM, VMEM, SMEM, VMEM, VMEM) + (SMEM,) * len(indices),
+        out_specs=(VMEM, SMEM, VMEM, VMEM) + (SMEM,) * len(indices),
         scratch_shapes=[pltpu.VMEM(value.shape, value.dtype) for value in inputs]
         + [pltpu.VMEM((8, slots), jnp.int32), pltpu.SemaphoreType.DMA, pltpu.SemaphoreType.DMA((len(hbm_inputs),))],
         compiler_params=pltpu.CompilerParams(vmem_limit_bytes=10 << 20),
@@ -184,10 +237,10 @@
     slots = table.shape[1]
     leaf = s_features.shape[1]
     return pl.pallas_call(
-        second_entries_kernel,
-        out_shape=(pltpu.VMEM((slots // 4, leaf, leaf), BF16),) * 2,
+        functools.partial(second_entries_kernel, first=first_count(slots)),
+        out_shape=pltpu.VMEM((second_count(slots), leaf, leaf), BF16),
         in_specs=[SMEM, VMEM, VMEM],
-        out_specs=(VMEM, VMEM),
+        out_specs=VMEM,
         compiler_params=pltpu.CompilerParams(vmem_limit_bytes=4 << 20),
         cost_estimate=pl.CostEstimate(flops=8_000_000_000, bytes_accessed=1 << 20, transcendentals=0),
         name="entries_rest",
@@ -242,57 +295,25 @@
             acc_ref[t] = acc_ref[t] + blocks[u]
 
 
-def near_kernel(*refs, groups, chunk, chunks, plain, out_carried):
-    (table_ref, tfill_ref, far_ref, x_ref) = refs[:4]
-    entries_refs = refs[4 : 4 + 2 * groups]
+def near_kernel(*refs, chunk, chunks, plain, out_carried):
+    (table_ref, tfill_ref, far_ref, x_ref, first_ref, second_ref, s_ref, t_ref) = refs[:8]
     carried = len(out_carried)
-    carried_refs = refs[4 + 2 * groups : 4 + 2 * groups + carried]
-    out_refs, acc_ref = refs[4 + 2 * groups + carried : -1], refs[-1]
+    carried_refs = refs[8 : 8 + carried]
+    out_refs, (rest_ref, acc_ref) = refs[8 + carried : -2], refs[-2:]
     chunk_leaves, rhs, leaf = acc_ref.shape
-    column_leaves = x_ref.shape[0]
     base_leaf = chunk * chunk_leaves
-    group = table_ref.shape[1] // groups
     total, half = table_ref[2, 0], table_ref[3, 0]
     low = half if chunk > 0 else 0
     high = total if chunk == chunks - 1 else half
+    made = first_ref.shape[0] + second_ref.shape[0]
     acc_ref[...] = jnp.zeros_like(acc_ref)
-
-    def work(*accs):
-        for acc in accs:
-            pltpu.matmul_pop(acc)
-
-        def drain(u, k):
-            inside = (k >= low) & (k < high)
-            slot = jnp.maximum(k, 0)
-            t = jnp.clip(table_ref[0, slot] // column_leaves - base_leaf, 0, chunk_leaves - 1)
-            copies = jnp.where(inside, table_ref[1, slot], 0).astype(F32)
-            block = pltpu.matmul_pop(accs[u])
-            acc_ref[t] = acc_ref[t] + jnp.where(inside, block * copies, 0.0)
-
-        for g in range(groups):
-            pair_refs = entries_refs[2 * g : 2 * g + 2]
-            start = jnp.clip(low, g * group, (g + 1) * group) // 16
-            stop = (jnp.clip(high, g * group, (g + 1) * group) + 15) // 16
-
-            @pl.loop(start, stop)
-            def _(turn):
-                for u in range(16):
-                    k = turn * 16 + u
-                    source = table_ref[0, k] % column_leaves
-                    stage = (u // 2) % 2
-                    entries = pair_refs[u % 2][turn * 8 - g * (group // 2) + u // 2]
-                    pltpu.matmul_push_rhs(entries, staging_register=stage, mxu_index=u % 2)
-                    pltpu.matmul_acc_lhs(accs[u], x_ref[source], load_staged_rhs=stage)
-                    if u >= 8:
-                        drain(u - 8, k - 8)
-                    else:
-                        drain(u + 8, k - 8)
-
-        end = (high + 15) // 16 * 16
-        for u in range(8, 16):
-            drain(u, end - 16 + u)
-
-    pl.run_scoped(work, *[pltpu.ACC(u % 2)((rhs, leaf), F32) for u in range(16)])
+    near_loop(
+        table_ref, x_ref, [(first_ref, 0), (second_ref, first_ref.shape[0])], acc_ref, base_leaf,
+        jnp.minimum(low, made), jnp.minimum(high, made),
+    )
+    rest = (jnp.maximum(low, made), jnp.maximum(high, made))
+    entry_loop(table_ref, s_ref, t_ref, rest_ref, made, *rest)
+    near_loop(table_ref, x_ref, [(rest_ref, made)], acc_ref, base_leaf, *rest)
 
     if plain:
         lane_t = lax.broadcasted_iota(jnp.int32, (rhs, leaf), 1)
@@ -335,7 +356,7 @@
     )(source_fill, far_source, far_target, far_rank, left, right, *pieces)
 
 
-def near_field(table, target_fill, far, x, entries, owners, plain, chunk, chunks, carried=(), out_carried=()):
+def near_field(table, target_fill, far, x, made, features, owners, plain, chunk, chunks, carried=(), out_carried=()):
     row_leaves, rhs, leaf = far.shape
     width = row_leaves // chunks * leaf
     if plain:
@@ -347,16 +368,17 @@
             )
             for m in range(owners)
         )
+    rest = table.shape[1] - sum(value.shape[0] for value in made)
     return pl.pallas_call(
-        functools.partial(near_kernel, groups=len(entries) // 2, chunk=chunk, chunks=chunks, plain=plain, out_carried=tuple(out_carried)),
+        functools.partial(near_kernel, chunk=chunk, chunks=chunks, plain=plain, out_carried=tuple(out_carried)),
         out_shape=out_shape,
-        in_specs=[SMEM] * 2 + [VMEM] * (2 + len(entries) + len(carried)),
+        in_specs=[SMEM] * 2 + [VMEM] * (6 + len(carried)),
         out_specs=(VMEM,) * len(out_shape),
-        scratch_shapes=[pltpu.VMEM((row_leaves // chunks, rhs, leaf), F32)],
-        compiler_params=pltpu.CompilerParams(vmem_limit_bytes=4 << 20),
+        scratch_shapes=[pltpu.VMEM((rest, leaf, leaf), BF16), pltpu.VMEM((row_leaves // chunks, rhs, leaf), F32)],
+        compiler_params=pltpu.CompilerParams(vmem_limit_bytes=20 << 20),
         cost_estimate=pl.CostEstimate(flops=4_000_000_000, bytes_accessed=8 << 20, transcendentals=0),
         name="near",
-    )(table, target_fill, far, x, *entries, *carried)
+    )(table, target_fill, far, x, *made, *features, *carried)
 
 
 def shards(
@@ -377,19 +399,20 @@
         near_fill, near_source, near_target, source_points, source_areas, target_points,
         (source_fill, target_fill, far_source, far_target, far_rank), (column_leaves, row_leaves),
     )
-    entries, (table, s_features, t_features) = list(first_outs[:2]), first_outs[2:5]
-    source_fill, target_fill, far_source, far_target, far_rank = first_outs[5:]
+    entries, table, *features = first_outs[:4]
+    source_fill, target_fill, far_source, far_target, far_rank = first_outs[4:]
     if not plain:
         pieces, table = lax.optimization_barrier((pieces, table))
         pieces = pieces + [swap(piece, "row", rows, 1) for piece in pieces]
-    entries = entries + list(second_entries(table, s_features, t_features))
+    more_entries = second_entries(table, *features)
     if not plain:
-        pieces, entries[-1] = lax.optimization_barrier((pieces, entries[-1]))
+        pieces, more_entries = lax.optimization_barrier((pieces, more_entries))
+    made = (entries, more_entries)
     x, far = far_field(
         source_fill, row_leaves, far_source, far_target, far_rank, left_basis[0], right_basis[0], pieces, plain
     )
     if plain or row_leaves % 2 or columns < 3:
-        outs = near_field(table, target_fill, far, x, entries, columns, plain, 0, 1)
+        outs = near_field(table, target_fill, far, x, made, features, columns, plain, 0, 1)
         if plain:
             return lax.psum_scatter(outs[0], "col", scatter_dimension=0, tiled=True)
         result = outs[0]
@@ -400,18 +423,14 @@
     def exchange(value, mask):
         return swap(value, "col", columns, mask)
 
-    far_masks = tuple(range(2, columns))
-    first = near_field(table, target_fill, far, x, entries, columns, plain, 0, 2)
-    early = exchange(first[1], 1)
-    second = near_field(
-        table, target_fill, far, x, entries, columns, plain, 1, 2, [first[m] for m in far_masks], far_masks
-    )
-    late = [exchange(second[mask], mask) for mask in reversed(far_masks)]
-    late_neighbour = exchange(second[1], 1)
-    result = jnp.concatenate([first[0], second[0]], axis=1)
-    result = result + jnp.concatenate([early, late_neighbour], axis=1).astype(F32)
-    for value in late:
-        result = result + value.astype(F32)
+    last = columns - 1
+    first = near_field(table, target_fill, far, x, made, features, columns, plain, 0, 2)
+    early = {mask: exchange(first[mask], mask) for mask in range(1, last)}
+    second = near_field(table, target_fill, far, x, made, features, columns, plain, 1, 2, (first[last],), (last,))
+    late = {mask: exchange(second[mask], mask) for mask in reversed(range(1, columns))}
+    result = jnp.concatenate([first[0], second[0]], axis=1) + late[last].astype(F32)
+    for mask in early:
+        result = result + jnp.concatenate([early[mask], late[mask]], axis=1).astype(F32)
     return result
 
 

time: 40.5 us -> 42.7 us (1.054)
  Pallas kernels: 20.7 us -> 22.8 us
  starting transfers between devices: 9.13 us -> 10.6 us
  waiting for transfers between devices: 8.86 us -> 7.41 us
    pallas_call x3, Pallas kernels: 9.76 us -> 12.4 us  [the longest x2 10.4 us: near_field(): pl.pallas_call(functools.partial(near_kernel, chunk=chunk, chunks=chunks,...]
    ppermute x11 -> x12, starting transfers between devices: 9.13 us -> 10.6 us  [swap(): return lax.ppermute(value, axis, [(i, i ^ mask) for i in range(size)])]
    ppermute x11 -> x12, waiting for transfers between devices: 8.86 us -> 7.41 us  [swap(): return lax.ppermute(value, axis, [(i, i ^ mask) for i in range(size)])]
    pallas_call x1, Pallas kernels: 8.11 us -> 7.54 us  [first_entries(): pl.pallas_call(functools.partial(first_entries_kernel, column_leaves=colu...]
  transfers between devices with their start and end apart: 11 -> 12, of which waited for: 2 -> 4; matrix products, arithmetic and copies ran while one was open for 0% -> 0% of each run, Pallas kernels for 29% -> 22%
where the time goes in v2:
time: 42.7 us; the launch traced here: 42.4 us
  Pallas kernels  22.8 us (53%)
  starting transfers between devices  10.6 us (25%)
  waiting for transfers between devices  7.41 us (17%)
  between operations  0.81 us (2%)
  other arithmetic  0.76 us (2%)
    ppermute x12, starting transfers between devices, swap(): return lax.ppermute(value, axis, [(i, i ^ mask) for i in range(size)])  10.6 us
    pallas_call x2, Pallas kernels, near_field(): pl.pallas_call(functools.partial(near_kernel, chunk=chunk, chunks=chunks,...  10.4 us
    pallas_call x1, Pallas kernels, first_entries(): pl.pallas_call(functools.partial(first_entries_kernel, column_leaves=colu...  7.54 us
    ppermute x12, waiting for transfers between devices, swap(): return lax.ppermute(value, axis, [(i, i ^ mask) for i in range(size)])  7.41 us
    pallas_call x1, Pallas kernels, far_field(): pl.pallas_call(functools.partial(far_kernel, pieces=len(pieces), plain=pl...  2.84 us
    pallas_call x1, Pallas kernels, second_entries(): pl.pallas_call(functools.partial(second_entries_kernel, first=first_count...  1.96 us
  transfers between devices with their start and end apart: 12, of which 4 were waited for; matrix products, arithmetic and copies ran while one was open for 0% of the time, Pallas kernels for 22%

profile of v2, /device:TPU:0, one launch (start us, length us, event | category | flops | bytes accessed | tf_op | source)
XLA Modules:
  0.0 42.4 jit_solution(10787890094112344296)
XLA Ops:
  0.0 3.0 %collective-permute-start.1 = (bf16[8,8192]{1,0:T(8,128)(2,1)}, bf16[8,8192]{1,0:T(8,128)(2,1)S(1)}, u32[]{:S(2)}, u32[]{:S(2)}) collective-permute-start(bf16[8,8192]{1,0:T(8,128)(2,1)} %refs_6_.2), channel_id=1, source_target_pairs={{0,16},{4,20},{8,24},{12,28},{16,0},{20,4},{24,8},{28,12},{1,17},{... | collective-permute-start | bytes 393224 | tf_op jit(solution)/shard_map/ppermute | solution.py:394
  3.0 1.5 %collective-permute-start = (bf16[8,8192]{1,0:T(8,128)(2,1)}, bf16[8,8192]{1,0:T(8,128)(2,1)S(1)}, u32[]{:S(2)}, u32[]{:S(2)}) collective-permute-start(bf16[8,8192]{1,0:T(8,128)(2,1)} %refs_6_.2), channel_id=1, source_target_pairs={{0,8},{4,12},{8,0},{12,4},{16,24},{20,28},{24,16},{28,20},{1,9},{5... | collective-permute-start | bytes 393224 | tf_op jit(solution)/shard_map/ppermute | solution.py:394
  4.5 0.0 collective-permute-start.2
  5.1 0.0 copy-start.2
  5.2 7.5 %entries.1 = (bf16[96,256,256]{2,1,0:T(8,128)(2,1)S(1)}, s32[8,256]{1,0:T(8,128)S(4)}, bf16[32,256,128]{2,1,0:T(8,128)(2,1)S(1)}, bf16[16,64,256]{2,1,0:T(8,128)...) custom-call(s32[1,1]{1,0:T(1,128)S(6)} %copy.15.refs_0_, ...), custom_call_target="tpu_custom_call" | custom-call | flops 8000000000 | bytes 1048576 | tf_op jit(solution)/shard_map/entries/pallas_call | solution.py:214
  12.7 0.0 collective-permute-done.1.refs_8_
  12.7 0.0 collective-permute-done.refs_7_
  12.7 0.0 collective-permute-done.2.refs_9_
  12.7 0.0 copy-done.2
  12.7 0.1 collective-permute-start.3
  12.8 0.5 %collective-permute-start.4 = (bf16[8,8192]{1,0:T(8,128)(2,1)S(1)}, bf16[8,8192]{1,0:T(8,128)(2,1)S(1)}, u32[]{:S(2)}, u32[]{:S(2)}) collective-permute-start(bf16[8,8192]{1,0:T(8,128)(2,1)S(1)} %collective-permute-done.refs_7_), channel_id=1, source_target_pairs={{0,4},{4,0},{8,12},{12,8},{16,20},{20,16},{24,28},{28,24},{1,5},{5... | collective-permute-start | bytes 393224 | tf_op jit(solution)/shard_map/ppermute | solution.py:394
  13.3 0.1 collective-permute-start.5
  13.4 0.4 %collective-permute-start.6 = (bf16[8,8192]{1,0:T(8,128)(2,1)S(1)}, bf16[8,8192]{1,0:T(8,128)(2,1)S(1)}, u32[]{:S(2)}, u32[]{:S(2)}) collective-permute-start(bf16[8,8192]{1,0:T(8,128)(2,1)S(1)} %collective-permute-done.2.refs_9_), channel_id=1, source_target_pairs={{0,4},{4,0},{8,12},{12,8},{16,20},{20,16},{24,28},{28,24},{1,5},{5... | collective-permute-start | bytes 393224 | tf_op jit(solution)/shard_map/ppermute | solution.py:394
  13.8 0.0 copy-start
  13.8 0.0 copy-start.1
  13.8 2.0 %entries_rest.1.refs_5_ = bf16[32,256,256]{2,1,0:T(8,128)(2,1)S(1)} custom-call(s32[8,256]{1,0:T(8,128)S(4)} %get-tuple-element.39.table_ref.refs_0_, bf16[32,256,128]{2,1,0:T(8,128)(2,1)S(1)} %get-tuple-element.49.s_ref.refs_6_, bf16[16,64,256]{2,1,0:T(8,128)(2,1)S(1)} %get-tuple-element.50.t_ref.refs_7_), custom_call_target="tpu_custom_call" | custom-call | flops 8000000000 | bytes 1048576 | tf_op jit(solution)/shard_map/entries_rest/pallas_call | solution.py:239
  15.8 0.0 collective-permute-done.3.refs_10_
  15.8 0.0 collective-permute-done.4.refs_11_
  15.8 0.0 collective-permute-done.5.refs_12_
  15.8 0.0 collective-permute-done.6.refs_13_
  15.8 0.0 copy-done
  15.9 0.0 copy-done.1
  15.9 2.8 %far.1 = (bf16[32,64,256]{2,1,0:T(8,128)(2,1)S(1)}, f32[16,64,256]{2,1,0:T(8,128)S(1)}) custom-call(s32[32]{0:T(128)S(4)} %get-tuple-element.41.refs_0_, s32[1,96]{1,0:T(1,128)S(4)} %get-tuple-element.42.refs_1_, s32[1,96]{1,0:T(1,128)S(4)} %get-tuple-element.43.refs_2_, s32[1,96]{1,0:T(1,128)S(4)} %get-tuple-element.44.refs_3_, ...), custom_call_target="tpu_custom_call" | custom-call | flops 2000000000 | bytes 8388608 | tf_op jit(solution)/shard_map/far/pallas_call | solution.py:347
  18.7 2.7 %near.2 = (f32[16,2048]{1,0:T(8,128)S(1)}, bf16[16,2048]{1,0:T(8,128)(2,1)S(1)}, bf16[16,2048]{1,0:T(8,128)(2,1)S(1)}, bf16[16,2048]{1,0:T(8,128)(2,1)S(1)}) custom-call(s32[8,256]{1,0:T(8,128)S(4)} %get-tuple-element.39.table_ref.refs_0_, s32[16]{0:T(128)S(4)} %get-tuple-element.40.refs_1_, f32[16,64,256]{2,1,0:T(8,128)S(1)} %get-tuple-element.59.refs_2_, ...), custom_call_target="tpu_custom_call" | custom-call | flops 4000000000 | bytes 8388608 | tf_op jit(solution)/shard_map/near/pallas_call | solution.py:372
  21.4 7.8 %near.3 = (f32[16,2048]{1,0:T(8,128)S(1)}, bf16[16,2048]{1,0:T(8,128)(2,1)S(1)}, bf16[16,2048]{1,0:T(8,128)(2,1)S(1)}, bf16[16,4096]{1,0:T(8,128)(2,1)S(1)}) custom-call(s32[8,256]{1,0:T(8,128)S(4)} %get-tuple-element.39.table_ref.refs_0_, s32[16]{0:T(128)S(4)} %get-tuple-element.40.refs_1_, f32[16,64,256]{2,1,0:T(8,128)S(1)} %get-tuple-element.59.refs_2_, ...), custom_call_target="tpu_custom_call" | custom-call | flops 4000000000 | bytes 8388608 | tf_op jit(solution)/shard_map/near/pallas_call | solution.py:372
  29.2 0.1 collective-permute-start.7
  29.2 0.1 collective-permute-start.9
  29.3 4.3 %collective-permute-start.11 = (bf16[16,2048]{1,0:T(8,128)(2,1)S(1)}, bf16[16,2048]{1,0:T(8,128)(2,1)S(1)}, u32[]{:S(2)}, u32[]{:S(2)}) collective-permute-start(bf16[16,2048]{1,0:T(8,128)(2,1)S(1)} %get-tuple-element.70), channel_id=1, source_target_pairs={{0,2},{1,3},{2,0},{3,1},{4,6},{5,7},{6,4},{7,5},{8,10},{9,11},{10,... | collective-permute-start | bytes 196616 | tf_op jit(solution)/shard_map/ppermute | solution.py:394
  33.6 0.0 collective-permute-start.8
  33.6 0.6 %collective-permute-start.10 = (bf16[16,2048]{1,0:T(8,128)(2,1)S(1)}, bf16[16,2048]{1,0:T(8,128)(2,1)S(1)}, u32[]{:S(2)}, u32[]{:S(2)}) collective-permute-start(bf16[16,2048]{1,0:T(8,128)(2,1)S(1)} %get-tuple-element.69), channel_id=1, source_target_pairs={{0,2},{1,3},{2,0},{3,1},{4,6},{5,7},{6,4},{7,5},{8,10},{9,11},{10,... | collective-permute-start | bytes 196616 | tf_op jit(solution)/shard_map/ppermute | solution.py:394
  34.3 0.3 collective-permute-done.9
  34.5 4.4 %collective-permute-done.11 = bf16[16,2048]{1,0:T(8,128)(2,1)S(1)} collective-permute-done((bf16[16,2048]{1,0:T(8,128)(2,1)S(1)}, bf16[16,2048]{1,0:T(8,128)(2,1)S(1)}, u32[]{:S(2)}, u32[]{:S(2)}) %collective-permute-start.11) | collective-permute-done | bytes 65568 | tf_op jit(solution)/shard_map/ppermute | solution.py:394
  38.9 1.2 %collective-permute-done.8 = bf16[16,2048]{1,0:T(8,128)(2,1)S(1)} collective-permute-done((bf16[16,2048]{1,0:T(8,128)(2,1)S(1)}, bf16[16,2048]{1,0:T(8,128)(2,1)S(1)}, u32[]{:S(2)}, u32[]{:S(2)}) %collective-permute-start.8) | collective-permute-done | bytes 65568 | tf_op jit(solution)/shard_map/ppermute | solution.py:394
  40.2 1.5 %collective-permute-done.10 = bf16[16,2048]{1,0:T(8,128)(2,1)S(1)} collective-permute-done((bf16[16,2048]{1,0:T(8,128)(2,1)S(1)}, bf16[16,2048]{1,0:T(8,128)(2,1)S(1)}, u32[]{:S(2)}, u32[]{:S(2)}) %collective-permute-start.10) | collective-permute-done | bytes 65568 | tf_op jit(solution)/shard_map/ppermute | solution.py:394
  41.7 0.0 collective-permute-done.7
  41.7 0.8 %fusion.1 = f32[16,4096]{1,0:T(8,128)} fusion(f32[16,2048]{1,0:T(8,128)S(1)} %get-tuple-element.65, f32[16,2048]{1,0:T(8,128)S(1)} %get-tuple-element.63, bf16[16,4096]{1,0:T(8,128)(2,1)S(1)} %collective-permute-done.7, bf16[16,2048]{1,0:T(8,128)(2,1)S(1)} %collective-permute-done.9, bf16[16,2048]{1,0:T(8,128)(2,1)S(1)} %collective-permute-done.8, ...), kind=kLoop, calls=%fused_computation.2 | loop fusion | flops 851968 | bytes 917504 | tf_op jit(solution)/shard_map/add | solution.py:433
Async XLA Ops:
  0.0 12.7 %collective-permute-start.1 = (bf16[8,8192]{1,0:T(8,128)(2,1)}, bf16[8,8192]{1,0:T(8,128)(2,1)S(1)}, u32[]{:S(2)}, u32[]{:S(2)}) collective-permute-start(bf16[8,8192]{1,0:T(8,128)(2,1)} %refs_6_.2), channel_id=1, source_target_pairs={{0,16},{4,20},{8,24},{12,28},{16,0},{20,4},{24,8},{28,12},{1,17},{... | collective-permute-start | bytes 393224 | tf_op jit(solution)/shard_map/ppermute | solution.py:394
  3.0 9.7 %collective-permute-start = (bf16[8,8192]{1,0:T(8,128)(2,1)}, bf16[8,8192]{1,0:T(8,128)(2,1)S(1)}, u32[]{:S(2)}, u32[]{:S(2)}) collective-permute-start(bf16[8,8192]{1,0:T(8,128)(2,1)} %refs_6_.2), channel_id=1, source_target_pairs={{0,8},{4,12},{8,0},{12,4},{16,24},{20,28},{24,16},{28,20},{1,9},{5... | collective-permute-start | bytes 393224 | tf_op jit(solution)/shard_map/ppermute | solution.py:394
  4.5 8.2 %collective-permute-start.2 = (bf16[8,8192]{1,0:T(8,128)(2,1)}, bf16[8,8192]{1,0:T(8,128)(2,1)S(1)}, u32[]{:S(2)}, u32[]{:S(2)}) collective-permute-start(bf16[8,8192]{1,0:T(8,128)(2,1)} %refs_6_.2), channel_id=1, source_target_pairs={{0,24},{4,28},{8,16},{12,20},{16,8},{20,12},{24,0},{28,4},{1,25},{... | collective-permute-start | bytes 393224 | tf_op jit(solution)/shard_map/ppermute | solution.py:394
  5.1 7.6 %copy-start.2 = (bf16[8,8192]{1,0:T(8,128)(2,1)S(1)}, bf16[8,8192]{1,0:T(8,128)(2,1)}, u32[]{:S(2)}) copy-start(bf16[8,8192]{1,0:T(8,128)(2,1)} %refs_6_.2) | copy-start | bytes 393220
  12.7 3.1 %collective-permute-start.3 = (bf16[8,8192]{1,0:T(8,128)(2,1)S(1)}, bf16[8,8192]{1,0:T(8,128)(2,1)S(1)}, u32[]{:S(2)}, u32[]{:S(2)}) collective-permute-start(bf16[8,8192]{1,0:T(8,128)(2,1)S(1)} %copy-done.2), channel_id=1, source_target_pairs={{0,4},{4,0},{8,12},{12,8},{16,20},{20,16},{24,28},{28,24},{1,5},{5... | collective-permute-start | bytes 393224 | tf_op jit(solution)/shard_map/ppermute | solution.py:394
  12.8 3.0 %collective-permute-start.4 = (bf16[8,8192]{1,0:T(8,128)(2,1)S(1)}, bf16[8,8192]{1,0:T(8,128)(2,1)S(1)}, u32[]{:S(2)}, u32[]{:S(2)}) collective-permute-start(bf16[8,8192]{1,0:T(8,128)(2,1)S(1)} %collective-permute-done.refs_7_), channel_id=1, source_target_pairs={{0,4},{4,0},{8,12},{12,8},{16,20},{20,16},{24,28},{28,24},{1,5},{5... | collective-permute-start | bytes 393224 | tf_op jit(solution)/shard_map/ppermute | solution.py:394
  13.3 2.5 %collective-permute-start.5 = (bf16[8,8192]{1,0:T(8,128)(2,1)S(1)}, bf16[8,8192]{1,0:T(8,128)(2,1)S(1)}, u32[]{:S(2)}, u32[]{:S(2)}) collective-permute-start(bf16[8,8192]{1,0:T(8,128)(2,1)S(1)} %collective-permute-done.1.refs_8_), channel_id=1, source_target_pairs={{0,4},{4,0},{8,12},{12,8},{16,20},{20,16},{24,28},{28,24},{1,5},{5... | collective-permute-start | bytes 393224 | tf_op jit(solution)/shard_map/ppermute | solution.py:394
  13.4 2.4 %collective-permute-start.6 = (bf16[8,8192]{1,0:T(8,128)(2,1)S(1)}, bf16[8,8192]{1,0:T(8,128)(2,1)S(1)}, u32[]{:S(2)}, u32[]{:S(2)}) collective-permute-start(bf16[8,8192]{1,0:T(8,128)(2,1)S(1)} %collective-permute-done.2.refs_9_), channel_id=1, source_target_pairs={{0,4},{4,0},{8,12},{12,8},{16,20},{20,16},{24,28},{28,24},{1,5},{5... | collective-permute-start | bytes 393224 | tf_op jit(solution)/shard_map/ppermute | solution.py:394
  13.8 2.0 %copy-start = (bf16[1,96,32,256]{3,2,1,0:T(8,128)(2,1)S(1)}, bf16[1,96,32,256]{3,2,1,0:T(8,128)(2,1)}, u32[]{:S(2)}) copy-start(bf16[1,96,32,256]{3,2,1,0:T(8,128)(2,1)} %param.26) | copy-start | bytes 4718596
  13.8 2.0 %copy-start.1 = (bf16[1,96,32,256]{3,2,1,0:T(8,128)(2,1)S(1)}, bf16[1,96,32,256]{3,2,1,0:T(8,128)(2,1)}, u32[]{:S(2)}) copy-start(bf16[1,96,32,256]{3,2,1,0:T(8,128)(2,1)} %param.27) | copy-start | bytes 4718596
  29.2 12.5 %collective-permute-start.7 = (bf16[16,4096]{1,0:T(8,128)(2,1)S(1)}, bf16[16,4096]{1,0:T(8,128)(2,1)S(1)}, u32[]{:S(2)}, u32[]{:S(2)}) collective-permute-start(bf16[16,4096]{1,0:T(8,128)(2,1)S(1)} %get-tuple-element.66), channel_id=1, source_target_pairs={{0,3},{1,2},{2,1},{3,0},{4,7},{5,6},{6,5},{7,4},{8,11},{9,10},{10,... | collective-permute-start | bytes 393224 | tf_op jit(solution)/shard_map/ppermute | solution.py:394
  29.2 5.3 %collective-permute-start.9 = (bf16[16,2048]{1,0:T(8,128)(2,1)S(1)}, bf16[16,2048]{1,0:T(8,128)(2,1)S(1)}, u32[]{:S(2)}, u32[]{:S(2)}) collective-permute-start(bf16[16,2048]{1,0:T(8,128)(2,1)S(1)} %get-tuple-element.68), channel_id=1, source_target_pairs={{0,1},{1,0},{2,3},{3,2},{4,5},{5,4},{6,7},{7,6},{8,9},{9,8},{10,11... | collective-permute-start | bytes 196616 | tf_op jit(solution)/shard_map/ppermute | solution.py:394
  29.3 9.6 %collective-permute-start.11 = (bf16[16,2048]{1,0:T(8,128)(2,1)S(1)}, bf16[16,2048]{1,0:T(8,128)(2,1)S(1)}, u32[]{:S(2)}, u32[]{:S(2)}) collective-permute-start(bf16[16,2048]{1,0:T(8,128)(2,1)S(1)} %get-tuple-element.70), channel_id=1, source_target_pairs={{0,2},{1,3},{2,0},{3,1},{4,6},{5,7},{6,4},{7,5},{8,10},{9,11},{10,... | collective-permute-start | bytes 196616 | tf_op jit(solution)/shard_map/ppermute | solution.py:394
  33.6 6.5 %collective-permute-start.8 = (bf16[16,2048]{1,0:T(8,128)(2,1)S(1)}, bf16[16,2048]{1,0:T(8,128)(2,1)S(1)}, u32[]{:S(2)}, u32[]{:S(2)}) collective-permute-start(bf16[16,2048]{1,0:T(8,128)(2,1)S(1)} %get-tuple-element.67), channel_id=1, source_target_pairs={{0,1},{1,0},{2,3},{3,2},{4,5},{5,4},{6,7},{7,6},{8,9},{9,8},{10,11... | collective-permute-start | bytes 196616 | tf_op jit(solution)/shard_map/ppermute | solution.py:394
  33.6 8.0 %collective-permute-start.10 = (bf16[16,2048]{1,0:T(8,128)(2,1)S(1)}, bf16[16,2048]{1,0:T(8,128)(2,1)S(1)}, u32[]{:S(2)}, u32[]{:S(2)}) collective-permute-start(bf16[16,2048]{1,0:T(8,128)(2,1)S(1)} %get-tuple-element.69), channel_id=1, source_target_pairs={{0,2},{1,3},{2,0},{3,1},{4,6},{5,7},{6,4},{7,5},{8,10},{9,11},{10,... | collective-permute-start | bytes 196616 | tf_op jit(solution)/shard_map/ppermute | solution.py:394

commit v3 on v2

--- a/solution.py
+++ b/solution.py
@@ -12,6 +12,8 @@
 SOFTENING_SQ = 0.0025
 F32 = jnp.float32
 BF16 = jnp.bfloat16
+ENTRY_TRIP = 16
+NEAR_TRIP = 16
 
 
 def split3(value):
@@ -62,15 +64,15 @@
     list_ref[...] = table.astype(jnp.int32)
 
 
-def entry_loop(table_ref, s_ref, t_ref, entries_ref, base, low, high):
+def entry_loop(table_ref, s_ref, t_ref, entries_refs, base, low, high):
     column_leaves, leaf, width = s_ref.shape
     depth = t_ref.shape[1]
-    start, stop = (low - base) // 8, (high - base + 7) // 8
+    start, stop = (low - base) // ENTRY_TRIP, (high - base + ENTRY_TRIP - 1) // ENTRY_TRIP
 
     def work(*accs):
         def drain(u, turn):
-            row = jnp.maximum(turn * 8 + u, 0)
-            entries_ref[row] = lax.rsqrt(pltpu.matmul_pop(accs[u])).astype(BF16)
+            row = jnp.maximum(turn * (ENTRY_TRIP // 2) + u // 2, 0)
+            entries_refs[u % 2][row] = lax.rsqrt(pltpu.matmul_pop(accs[u % 8])).astype(BF16)
 
         @pl.when(stop > start)
         def _():
@@ -79,26 +81,26 @@
 
             @pl.loop(start, stop)
             def _(turn):
-                for u in range(8):
-                    pair = table_ref[0, base + turn * 8 + u]
+                for u in range(ENTRY_TRIP):
+                    pair = table_ref[0, base + turn * ENTRY_TRIP + u]
                     rhs = jnp.concatenate([t_ref[pair // column_leaves], jnp.zeros((leaf - depth, leaf), BF16)], axis=0)
                     lhs = jnp.concatenate([s_ref[pair % column_leaves], jnp.zeros((leaf, leaf - width), BF16)], axis=1)
                     stage = (u // 2) % 2
                     pltpu.matmul_push_rhs(rhs, staging_register=stage, mxu_index=u % 2)
-                    pltpu.matmul_acc_lhs(accs[u], lhs, load_staged_rhs=stage)
+                    pltpu.matmul_acc_lhs(accs[u % 8], lhs, load_staged_rhs=stage)
                     if u < 4:
-                        drain(u + 4, turn - 1)
+                        drain(ENTRY_TRIP - 4 + u, turn - 1)
                     else:
                         drain(u - 4, turn)
 
-            for u in range(4, 8):
+            for u in range(ENTRY_TRIP - 4, ENTRY_TRIP):
                 drain(u, stop - 1)
 
     pl.run_scoped(work, *[pltpu.ACC(u % 2)((leaf, leaf), F32) for u in range(8)])
 
 
-def near_loop(table_ref, x_ref, entries, acc_ref, base_leaf, low, high):
-    chunk_leaves, rhs, leaf = acc_ref.shape
+def near_loop(table_ref, x_ref, entries, acc_refs, base_leaf, low, high):
+    chunk_leaves, rhs, leaf = acc_refs[0].shape
     column_leaves = x_ref.shape[0]
 
     def work(*accs):
@@ -108,41 +110,40 @@
             t = jnp.clip(table_ref[0, slot] // column_leaves - base_leaf, 0, chunk_leaves - 1)
             copies = jnp.where(inside, table_ref[1, slot], 0).astype(F32)
             block = pltpu.matmul_pop(accs[u])
-            acc_ref[t] = acc_ref[t] + jnp.where(inside, block * copies, 0.0)
+            acc_refs[u % 2][t] = acc_refs[u % 2][t] + jnp.where(inside, block * copies, 0.0)
 
         @pl.when(high > low)
         def _():
             for acc in accs:
                 pltpu.matmul_pop(acc)
 
-            for entries_ref, base in entries:
-                end = base + entries_ref.shape[0]
-                start, stop = jnp.clip(low, base, end) // 16, (jnp.clip(high, base, end) + 15) // 16
+            for *entries_refs, base in entries:
+                end = base + 2 * entries_refs[0].shape[0]
+                start = jnp.clip(low, base, end) // NEAR_TRIP
+                stop = (jnp.clip(high, base, end) + NEAR_TRIP - 1) // NEAR_TRIP
 
                 @pl.loop(start, stop)
                 def _(turn):
-                    for u in range(16):
-                        k = turn * 16 + u
+                    for u in range(NEAR_TRIP):
+                        k = turn * NEAR_TRIP + u
                         source = table_ref[0, k] % column_leaves
+                        row = turn * (NEAR_TRIP // 2) - base // 2 + u // 2
                         stage = (u // 2) % 2
-                        pltpu.matmul_push_rhs(entries_ref[k - base], staging_register=stage, mxu_index=u % 2)
-                        pltpu.matmul_acc_lhs(accs[u], x_ref[source], load_staged_rhs=stage)
-                        if u >= 8:
-                            drain(u - 8, k - 8)
-                        else:
-                            drain(u + 8, k - 8)
-
-            end = (high + 15) // 16 * 16
-            for u in range(8, 16):
-                drain(u, end - 16 + u)
+                        pltpu.matmul_push_rhs(entries_refs[u % 2][row], staging_register=stage, mxu_index=u % 2)
+                        pltpu.matmul_acc_lhs(accs[u % 16], x_ref[source], load_staged_rhs=stage)
+                        drain((u + 8) % 16, k - 8)
+
+            end = (high + NEAR_TRIP - 1) // NEAR_TRIP * NEAR_TRIP
+            for u in range(8):
+                drain(u + 8, end - 8 + u)
 
     pl.run_scoped(work, *[pltpu.ACC(u % 2)((rhs, leaf), F32) for u in range(16)])
 
 
 def first_entries_kernel(*refs, column_leaves, row_leaves, leaf, indices):
     fill_ref, inputs, index_inputs = refs[0], refs[1:6], refs[6 : 6 + indices]
-    outputs, scratch = refs[6 + indices : 10 + 2 * indices], refs[10 + 2 * indices :]
-    (entries_ref, table_ref, s_ref, t_ref), index_outputs = outputs[:4], outputs[4:]
+    outputs, scratch = refs[6 + indices : 11 + 2 * indices], refs[11 + 2 * indices :]
+    (*entries_refs, table_ref, s_ref, t_ref), index_outputs = outputs[:5], outputs[5:]
     copies, (list_ref, sem, in_sem) = scratch[:5], scratch[5:]
     moves = list(zip(inputs, copies)) + list(zip(index_inputs, index_outputs))
     loads = [pltpu.make_async_copy(src, dst, in_sem.at[i]) for i, (src, dst) in enumerate(moves)]
@@ -153,7 +154,7 @@
         load.wait()
     used = lax.broadcasted_iota(jnp.int32, nsrc_ref.shape, 1) < fill_ref[0, 0]
     ids = jnp.where(used, ntgt_ref[...] * column_leaves + nsrc_ref[...], -1)
-    build_list(ids, list_ref, (row_leaves // 2) * column_leaves)
+    build_list(ids, list_ref, first_leaves(row_leaves) * column_leaves)
     copy = pltpu.make_async_copy(list_ref, table_ref, sem)
     copy.start()
     for load in loads[2:5]:
@@ -179,16 +180,14 @@
         s_ref[s] = jnp.concatenate([column, jnp.zeros((leaf, 128 - column.shape[1]), BF16)], axis=1)
 
     copy.wait()
-    entry_loop(table_ref, s_ref, t_ref, entries_ref, 0, 0, jnp.minimum(table_ref[2, 0], entries_ref.shape[0]))
+    entry_loop(table_ref, s_ref, t_ref, entries_refs, 0, 0, jnp.minimum(table_ref[2, 0], 2 * entries_refs[0].shape[0]))
     for load in loads[5:]:
         load.wait()
 
 
-def second_entries_kernel(table_ref, s_ref, t_ref, entries_ref, *, first):
-    total = table_ref[2, 0]
-    entry_loop(
-        table_ref, s_ref, t_ref, entries_ref, first, first, jnp.clip(total, first, first + entries_ref.shape[0])
-    )
+def second_entries_kernel(table_ref, s_ref, t_ref, *entries_refs, first):
+    last = first + 2 * entries_refs[0].shape[0]
+    entry_loop(table_ref, s_ref, t_ref, entries_refs, first, first, jnp.clip(table_ref[2, 0], first, last))
 
 
 VMEM = pl.BlockSpec(memory_space=pltpu.VMEM)
@@ -196,12 +195,16 @@
 HBM = pl.BlockSpec(memory_space=pltpu.HBM)
 
 
+def first_leaves(row_leaves):
+    return row_leaves * 5 // 8
+
+
 def first_count(slots):
-    return max(slots * 3 // 8 // 16 * 16, 16)
+    return max(slots * 3 // 8 // NEAR_TRIP, 1) * NEAR_TRIP
 
 
 def second_count(slots):
-    return max(slots // 8 // 16 * 16, 16)
+    return max(slots // 8 // NEAR_TRIP, 1) * NEAR_TRIP
 
 
 def first_entries(near_fill, near_source, near_target, source_points, source_areas, target_points, indices, leaves):
@@ -217,14 +220,14 @@
             indices=len(indices),
         ),
         out_shape=(
-            pltpu.VMEM((first_count(slots), leaf, leaf), BF16),
+            *[pltpu.VMEM((first_count(slots) // 2, leaf, leaf), BF16)] * 2,
             pltpu.SMEM((8, slots), jnp.int32),
             pltpu.VMEM((column_leaves, leaf, 128), BF16),
             pltpu.VMEM((row_leaves, depth, leaf), BF16),
         )
         + tuple(pltpu.SMEM(value.shape, jnp.int32) for value in indices),
         in_specs=[SMEM] + [HBM] * len(hbm_inputs),
-        out_specs=(VMEM, SMEM, VMEM, VMEM) + (SMEM,) * len(indices),
+        out_specs=(VMEM, VMEM, SMEM, VMEM, VMEM) + (SMEM,) * len(indices),
         scratch_shapes=[pltpu.VMEM(value.shape, value.dtype) for value in inputs]
         + [pltpu.VMEM((8, slots), jnp.int32), pltpu.SemaphoreType.DMA, pltpu.SemaphoreType.DMA((len(hbm_inputs),))],
         compiler_params=pltpu.CompilerParams(vmem_limit_bytes=10 << 20),
@@ -238,9 +241,9 @@
     leaf = s_features.shape[1]
     return pl.pallas_call(
         functools.partial(second_entries_kernel, first=first_count(slots)),
-        out_shape=pltpu.VMEM((second_count(slots), leaf, leaf), BF16),
+        out_shape=(pltpu.VMEM((second_count(slots) // 2, leaf, leaf), BF16),) * 2,
         in_specs=[SMEM, VMEM, VMEM],
-        out_specs=VMEM,
+        out_specs=(VMEM, VMEM),
         compiler_params=pltpu.CompilerParams(vmem_limit_bytes=4 << 20),
         cost_estimate=pl.CostEstimate(flops=8_000_000_000, bytes_accessed=1 << 20, transcendentals=0),
         name="entries_rest",
@@ -295,30 +298,31 @@
             acc_ref[t] = acc_ref[t] + blocks[u]
 
 
-def near_kernel(*refs, chunk, chunks, plain, out_carried):
-    (table_ref, tfill_ref, far_ref, x_ref, first_ref, second_ref, s_ref, t_ref) = refs[:8]
+def near_kernel(*refs, base_leaf, plain, out_carried):
+    (table_ref, tfill_ref, far_ref, x_ref), first_refs, second_refs, (s_ref, t_ref) = refs[:4], refs[4:6], refs[6:8], refs[8:10]
     carried = len(out_carried)
-    carried_refs = refs[8 : 8 + carried]
-    out_refs, (rest_ref, acc_ref) = refs[8 + carried : -2], refs[-2:]
-    chunk_leaves, rhs, leaf = acc_ref.shape
-    base_leaf = chunk * chunk_leaves
+    carried_refs = refs[10 : 10 + carried]
+    out_refs, rest_refs, acc_refs = refs[10 + carried : -4], refs[-4:-2], refs[-2:]
+    chunk_leaves, rhs, leaf = acc_refs[0].shape
     total, half = table_ref[2, 0], table_ref[3, 0]
-    low = half if chunk > 0 else 0
-    high = total if chunk == chunks - 1 else half
-    made = first_ref.shape[0] + second_ref.shape[0]
-    acc_ref[...] = jnp.zeros_like(acc_ref)
+    low = half if base_leaf > 0 else 0
+    high = total if base_leaf + chunk_leaves == far_ref.shape[0] else half
+    first, second = 2 * first_refs[0].shape[0], 2 * second_refs[0].shape[0]
+    made = first + second
+    for acc_ref in acc_refs:
+        acc_ref[...] = jnp.zeros_like(acc_ref)
     near_loop(
-        table_ref, x_ref, [(first_ref, 0), (second_ref, first_ref.shape[0])], acc_ref, base_leaf,
+        table_ref, x_ref, [(*first_refs, 0), (*second_refs, first)], acc_refs, base_leaf,
         jnp.minimum(low, made), jnp.minimum(high, made),
     )
     rest = (jnp.maximum(low, made), jnp.maximum(high, made))
-    entry_loop(table_ref, s_ref, t_ref, rest_ref, made, *rest)
-    near_loop(table_ref, x_ref, [(rest_ref, made)], acc_ref, base_leaf, *rest)
+    entry_loop(table_ref, s_ref, t_ref, rest_refs, made, *rest)
+    near_loop(table_ref, x_ref, [(*rest_refs, made)], acc_refs, base_leaf, *rest)
 
     if plain:
         lane_t = lax.broadcasted_iota(jnp.int32, (rhs, leaf), 1)
         for t in range(chunk_leaves):
-            value = acc_ref[t] + far_ref[base_leaf + t]
+            value = acc_refs[0][t] + acc_refs[1][t] + far_ref[base_leaf + t]
             out_refs[0][:, t * leaf : (t + 1) * leaf] = jnp.where(lane_t < tfill_ref[base_leaf + t], value, 0.0)
     else:
         owners = len(out_refs)
@@ -331,7 +335,8 @@
             if shift:
                 out_refs[m][:, :shift] = carried_refs[out_carried.index(m)][...]
             for t in range(chunk_leaves):
-                value = acc_ref[t, pl.ds(start, height), :] + far_ref[base_leaf + t, pl.ds(start, height), :]
+                rows = pl.ds(start, height)
+                value = acc_refs[0][t, rows, :] + acc_refs[1][t, rows, :] + far_ref[base_leaf + t, rows, :]
                 value = jnp.where(lane_t < tfill_ref[base_leaf + t], value, 0.0)
                 window = slice(shift + t * leaf, shift + (t + 1) * leaf)
                 out_refs[m][:, window] = value.astype(out_refs[m].dtype)
@@ -356,9 +361,9 @@
     )(source_fill, far_source, far_target, far_rank, left, right, *pieces)
 
 
-def near_field(table, target_fill, far, x, made, features, owners, plain, chunk, chunks, carried=(), out_carried=()):
-    row_leaves, rhs, leaf = far.shape
-    width = row_leaves // chunks * leaf
+def near_field(table, target_fill, far, x, made, features, owners, plain, leaves, carried=(), out_carried=()):
+    _, rhs, leaf = far.shape
+    width = len(leaves) * leaf
     if plain:
         out_shape = (jax.ShapeDtypeStruct((rhs, width), F32),)
     else:
@@ -368,13 +373,13 @@
             )
             for m in range(owners)
         )
-    rest = table.shape[1] - sum(value.shape[0] for value in made)
+    rest = (table.shape[1] - sum(value.shape[0] for value in made)) // 2
     return pl.pallas_call(
-        functools.partial(near_kernel, chunk=chunk, chunks=chunks, plain=plain, out_carried=tuple(out_carried)),
+        functools.partial(near_kernel, base_leaf=leaves[0], plain=plain, out_carried=tuple(out_carried)),
         out_shape=out_shape,
-        in_specs=[SMEM] * 2 + [VMEM] * (6 + len(carried)),
+        in_specs=[SMEM] * 2 + [VMEM] * (8 + len(carried)),
         out_specs=(VMEM,) * len(out_shape),
-        scratch_shapes=[pltpu.VMEM((rest, leaf, leaf), BF16), pltpu.VMEM((row_leaves // chunks, rhs, leaf), F32)],
+        scratch_shapes=[pltpu.VMEM((rest, leaf, leaf), BF16)] * 2 + [pltpu.VMEM((len(leaves), rhs, leaf), F32)] * 2,
         compiler_params=pltpu.CompilerParams(vmem_limit_bytes=20 << 20),
         cost_estimate=pl.CostEstimate(flops=4_000_000_000, bytes_accessed=8 << 20, transcendentals=0),
         name="near",
@@ -399,20 +404,21 @@
         near_fill, near_source, near_target, source_points, source_areas, target_points,
         (source_fill, target_fill, far_source, far_target, far_rank), (column_leaves, row_leaves),
     )
-    entries, table, *features = first_outs[:4]
-    source_fill, target_fill, far_source, far_target, far_rank = first_outs[4:]
+    *entries, table, s_features, t_features = first_outs[:5]
+    features = (s_features, t_features)
+    source_fill, target_fill, far_source, far_target, far_rank = first_outs[5:]
     if not plain:
         pieces, table = lax.optimization_barrier((pieces, table))
         pieces = pieces + [swap(piece, "row", rows, 1) for piece in pieces]
-    more_entries = second_entries(table, *features)
+    more_entries = list(second_entries(table, *features))
     if not plain:
-        pieces, more_entries = lax.optimization_barrier((pieces, more_entries))
-    made = (entries, more_entries)
+        pieces, more_entries[0] = lax.optimization_barrier((pieces, more_entries[0]))
+    made = (*entries, *more_entries)
     x, far = far_field(
         source_fill, row_leaves, far_source, far_target, far_rank, left_basis[0], right_basis[0], pieces, plain
     )
-    if plain or row_leaves % 2 or columns < 3:
-        outs = near_field(table, target_fill, far, x, made, features, columns, plain, 0, 1)
+    if plain or row_leaves < 2 or columns < 3:
+        outs = near_field(table, target_fill, far, x, made, features, columns, plain, range(row_leaves))
         if plain:
             return lax.psum_scatter(outs[0], "col", scatter_dimension=0, tiled=True)
         result = outs[0]
@@ -423,15 +429,20 @@
     def exchange(value, mask):
         return swap(value, "col", columns, mask)
 
-    last = columns - 1
-    first = near_field(table, target_fill, far, x, made, features, columns, plain, 0, 2)
-    early = {mask: exchange(first[mask], mask) for mask in range(1, last)}
-    second = near_field(table, target_fill, far, x, made, features, columns, plain, 1, 2, (first[last],), (last,))
-    late = {mask: exchange(second[mask], mask) for mask in reversed(range(1, columns))}
-    result = jnp.concatenate([first[0], second[0]], axis=1) + late[last].astype(F32)
+    split = first_leaves(row_leaves)
+    inputs = (table, target_fill, far, x, made, features, columns, plain)
+    first = near_field(*inputs, range(split))
+    early = {mask: exchange(first[mask], mask) for mask in range(2, columns)}
+    second = near_field(*inputs, range(split, row_leaves), (first[1],), (1,))
+    late = {mask: exchange(second[mask], mask) for mask in late_order(columns)}
+    result = jnp.concatenate([first[0], second[0]], axis=1) + late[1].astype(F32)
     for mask in early:
         result = result + jnp.concatenate([early[mask], late[mask]], axis=1).astype(F32)
     return result
+
+
+def late_order(columns):
+    return list(range(2, columns)) + [1]
 
 
 def solution(mesh):

time: 42.7 us -> 43.2 us (1.012)
  Pallas kernels: 22.8 us -> 20.8 us
  waiting for transfers between devices: 7.41 us -> 8.85 us
  starting transfers between devices: 10.6 us -> 11.5 us
    ppermute x12, waiting for transfers between devices: 7.41 us -> 8.85 us  [swap(): return lax.ppermute(value, axis, [(i, i ^ mask) for i in range(size)])]
    pallas_call x1, Pallas kernels: 7.54 us -> 6.16 us  [first_entries(): pl.pallas_call(functools.partial(first_entries_kernel, column_leaves=colu...]
    ppermute x12, starting transfers between devices: 10.6 us -> 11.5 us  [swap(): return lax.ppermute(value, axis, [(i, i ^ mask) for i in range(size)])]
  transfers between devices with their start and end apart: 12 -> 12, of which waited for: 4 -> 1; matrix products, arithmetic and copies ran while one was open for 0% -> 0% of each run, Pallas kernels for 22% -> 18%
where the time goes in v3:
time: 43.2 us; the launch traced here: 43.1 us
  Pallas kernels  20.8 us (48%)
  starting transfers between devices  11.5 us (27%)
  waiting for transfers between devices  8.85 us (20%)
  between operations  0.81 us (2%)
  other arithmetic  0.76 us (2%)
    ppermute x12, starting transfers between devices, swap(): return lax.ppermute(value, axis, [(i, i ^ mask) for i in range(size)])  11.5 us
    pallas_call x2, Pallas kernels, near_field(): pl.pallas_call(functools.partial(near_kernel, base_leaf=leaves[0], plain=...  10.3 us
    ppermute x12, waiting for transfers between devices, swap(): return lax.ppermute(value, axis, [(i, i ^ mask) for i in range(size)])  8.85 us
    pallas_call x1, Pallas kernels, first_entries(): pl.pallas_call(functools.partial(first_entries_kernel, column_leaves=colu...  6.16 us
    pallas_call x1, Pallas kernels, far_field(): pl.pallas_call(functools.partial(far_kernel, pieces=len(pieces), plain=pl...  2.83 us
    pallas_call x1, Pallas kernels, second_entries(): pl.pallas_call(functools.partial(second_entries_kernel, first=first_count...  1.54 us
  transfers between devices with their start and end apart: 12, of which 1 were waited for; matrix products, arithmetic and copies ran while one was open for 0% of the time, Pallas kernels for 18%

profile of v3, /device:TPU:0, one launch (start us, length us, event | category | flops | bytes accessed | tf_op | source)
XLA Modules:
  0.0 43.1 jit_solution(4542682159227088121)
XLA Ops:
  0.0 3.0 %collective-permute-start.1 = (bf16[8,8192]{1,0:T(8,128)(2,1)}, bf16[8,8192]{1,0:T(8,128)(2,1)S(1)}, u32[]{:S(2)}, u32[]{:S(2)}) collective-permute-start(bf16[8,8192]{1,0:T(8,128)(2,1)} %refs_6_.2), channel_id=1, source_target_pairs={{0,16},{4,20},{8,24},{12,28},{16,0},{20,4},{24,8},{28,12},{1,17},{... | collective-permute-start | bytes 393224 | tf_op jit(solution)/shard_map/ppermute | solution.py:399
  3.0 1.5 %collective-permute-start = (bf16[8,8192]{1,0:T(8,128)(2,1)}, bf16[8,8192]{1,0:T(8,128)(2,1)S(1)}, u32[]{:S(2)}, u32[]{:S(2)}) collective-permute-start(bf16[8,8192]{1,0:T(8,128)(2,1)} %refs_6_.2), channel_id=1, source_target_pairs={{0,8},{4,12},{8,0},{12,4},{16,24},{20,28},{24,16},{28,20},{1,9},{5... | collective-permute-start | bytes 393224 | tf_op jit(solution)/shard_map/ppermute | solution.py:399
  4.5 0.0 collective-permute-start.2
  5.1 0.0 copy-start.2
  5.2 6.2 %entries.1 = (bf16[48,256,256]{2,1,0:T(8,128)(2,1)S(1)}, bf16[48,256,256]{2,1,0:T(8,128)(2,1)S(1)}, s32[8,256]{1,0:T(8,128)S(4)}, bf16[32,256,128]{2,1,0:T(8,128...) custom-call(s32[1,1]{1,0:T(1,128)S(6)} %copy.15.refs_0_, ...), custom_call_target="tpu_custom_call" | custom-call | flops 8000000000 | bytes 1048576 | tf_op jit(solution)/shard_map/entries/pallas_call | solution.py:217
  11.3 0.0 collective-permute-done.1.refs_8_
  11.3 0.0 collective-permute-done.refs_7_
  11.3 0.0 collective-permute-done.2.refs_9_
  11.3 0.0 copy-done.2
  11.4 0.1 collective-permute-start.3
  11.4 0.5 %collective-permute-start.4 = (bf16[8,8192]{1,0:T(8,128)(2,1)S(1)}, bf16[8,8192]{1,0:T(8,128)(2,1)S(1)}, u32[]{:S(2)}, u32[]{:S(2)}) collective-permute-start(bf16[8,8192]{1,0:T(8,128)(2,1)S(1)} %collective-permute-done.refs_7_), channel_id=1, source_target_pairs={{0,4},{4,0},{8,12},{12,8},{16,20},{20,16},{24,28},{28,24},{1,5},{5... | collective-permute-start | bytes 393224 | tf_op jit(solution)/shard_map/ppermute | solution.py:399
  11.9 0.1 collective-permute-start.5
  12.0 0.4 %collective-permute-start.6 = (bf16[8,8192]{1,0:T(8,128)(2,1)S(1)}, bf16[8,8192]{1,0:T(8,128)(2,1)S(1)}, u32[]{:S(2)}, u32[]{:S(2)}) collective-permute-start(bf16[8,8192]{1,0:T(8,128)(2,1)S(1)} %collective-permute-done.2.refs_9_), channel_id=1, source_target_pairs={{0,4},{4,0},{8,12},{12,8},{16,20},{20,16},{24,28},{28,24},{1,5},{5... | collective-permute-start | bytes 393224 | tf_op jit(solution)/shard_map/ppermute | solution.py:399
  12.4 0.0 copy-start
  12.4 0.0 copy-start.1
  12.5 1.5 %entries_rest.1 = (bf16[16,256,256]{2,1,0:T(8,128)(2,1)S(1)}, bf16[16,256,256]{2,1,0:T(8,128)(2,1)S(1)}) custom-call(s32[8,256]{1,0:T(8,128)S(4)} %get-tuple-element.42.table_ref.refs_0_, bf16[32,256,128]{2,1,0:T(8,128)(2,1)S(1)} %get-tuple-element.52.s_ref.refs_8_, bf16[16,64,256]{2,1,0:T(8,128)(2,1)S(1)} %get-tuple-element.53.t_ref.refs_9_), custom_call_target="tpu_custom_call" | custom-call | flops 8000000000 | bytes 1048576 | tf_op jit(solution)/shard_map/entries_rest/pallas_call | solution.py:242
  14.0 0.0 collective-permute-done.3.refs_10_
  14.0 0.0 collective-permute-done.4.refs_11_
  14.0 0.0 collective-permute-done.5.refs_12_
  14.0 0.0 collective-permute-done.6.refs_13_
  14.0 0.0 copy-done
  14.1 0.3 copy-done.1
  14.3 2.8 %far.1 = (bf16[32,64,256]{2,1,0:T(8,128)(2,1)S(1)}, f32[16,64,256]{2,1,0:T(8,128)S(1)}) custom-call(s32[32]{0:T(128)S(4)} %get-tuple-element.44.refs_0_, s32[1,96]{1,0:T(1,128)S(4)} %get-tuple-element.45.refs_1_, s32[1,96]{1,0:T(1,128)S(4)} %get-tuple-element.46.refs_2_, s32[1,96]{1,0:T(1,128)S(4)} %get-tuple-element.47.refs_3_, ...), custom_call_target="tpu_custom_call" | custom-call | flops 2000000000 | bytes 8388608 | tf_op jit(solution)/shard_map/far/pallas_call | solution.py:352
  17.2 3.8 %near.2 = (f32[16,2560]{1,0:T(8,128)S(1)}, bf16[16,2560]{1,0:T(8,128)(2,1)S(1)}, bf16[16,2560]{1,0:T(8,128)(2,1)S(1)}, bf16[16,2560]{1,0:T(8,128)(2,1)S(1)}) custom-call(s32[8,256]{1,0:T(8,128)S(4)} %get-tuple-element.42.table_ref.refs_0_, s32[16]{0:T(128)S(4)} %get-tuple-element.43.refs_1_, f32[16,64,256]{2,1,0:T(8,128)S(1)} %get-tuple-element.63.refs_2_, ...), custom_call_target="tpu_custom_call" | custom-call | flops 4000000000 | bytes 8388608 | tf_op jit(solution)/shard_map/near/pallas_call | solution.py:377
  20.9 6.5 %near.3 = (f32[16,1536]{1,0:T(8,128)S(1)}, bf16[16,4096]{1,0:T(8,128)(2,1)S(1)}, bf16[16,1536]{1,0:T(8,128)(2,1)S(1)}, bf16[16,1536]{1,0:T(8,128)(2,1)S(1)}) custom-call(s32[8,256]{1,0:T(8,128)S(4)} %get-tuple-element.42.table_ref.refs_0_, s32[16]{0:T(128)S(4)} %get-tuple-element.43.refs_1_, f32[16,64,256]{2,1,0:T(8,128)S(1)} %get-tuple-element.63.refs_2_, ...), custom_call_target="tpu_custom_call" | custom-call | flops 4000000000 | bytes 8388608 | tf_op jit(solution)/shard_map/near/pallas_call | solution.py:377
  27.5 0.1 collective-permute-start.7
  27.5 0.1 collective-permute-start.8
  27.6 4.3 %collective-permute-start.10 = (bf16[16,2560]{1,0:T(8,128)(2,1)S(1)}, bf16[16,2560]{1,0:T(8,128)(2,1)S(1)}, u32[]{:S(2)}, u32[]{:S(2)}) collective-permute-start(bf16[16,2560]{1,0:T(8,128)(2,1)S(1)} %get-tuple-element.75), channel_id=1, source_target_pairs={{0,3},{1,2},{2,1},{3,0},{4,7},{5,6},{6,5},{7,4},{8,11},{9,10},{10,... | collective-permute-start | bytes 245768 | tf_op jit(solution)/shard_map/ppermute | solution.py:399
  31.9 0.0 collective-permute-start.9
  31.9 1.5 %collective-permute-start.11 = (bf16[16,1536]{1,0:T(8,128)(2,1)S(1)}, bf16[16,1536]{1,0:T(8,128)(2,1)S(1)}, u32[]{:S(2)}, u32[]{:S(2)}) collective-permute-start(bf16[16,1536]{1,0:T(8,128)(2,1)S(1)} %get-tuple-element.76), channel_id=1, source_target_pairs={{0,3},{1,2},{2,1},{3,0},{4,7},{5,6},{6,5},{7,4},{8,11},{9,10},{10,... | collective-permute-start | bytes 147464 | tf_op jit(solution)/shard_map/ppermute | solution.py:399
  33.5 8.8 %collective-permute-done.9 = bf16[16,1536]{1,0:T(8,128)(2,1)S(1)} collective-permute-done((bf16[16,1536]{1,0:T(8,128)(2,1)S(1)}, bf16[16,1536]{1,0:T(8,128)(2,1)S(1)}, u32[]{:S(2)}, u32[]{:S(2)}) %collective-permute-start.9) | collective-permute-done | bytes 49184 | tf_op jit(solution)/shard_map/ppermute | solution.py:399
  42.3 0.0 collective-permute-done.11
  42.3 0.0 collective-permute-done.8
  42.3 0.0 collective-permute-done.10
  42.3 0.0 collective-permute-done.7
  42.3 0.8 %fusion.1 = f32[16,4096]{1,0:T(8,128)} fusion(f32[16,1536]{1,0:T(8,128)S(1)} %get-tuple-element.71, f32[16,2560]{1,0:T(8,128)S(1)} %get-tuple-element.69, bf16[16,4096]{1,0:T(8,128)(2,1)S(1)} %collective-permute-done.7, bf16[16,1536]{1,0:T(8,128)(2,1)S(1)} %collective-permute-done.9, bf16[16,2560]{1,0:T(8,128)(2,1)S(1)} %collective-permute-done.8, ...), kind=kLoop, calls=%fused_computation.2 | loop fusion | flops 851968 | bytes 917504 | tf_op jit(solution)/shard_map/add | solution.py:440
Async XLA Ops:
  0.0 11.3 %collective-permute-start.1 = (bf16[8,8192]{1,0:T(8,128)(2,1)}, bf16[8,8192]{1,0:T(8,128)(2,1)S(1)}, u32[]{:S(2)}, u32[]{:S(2)}) collective-permute-start(bf16[8,8192]{1,0:T(8,128)(2,1)} %refs_6_.2), channel_id=1, source_target_pairs={{0,16},{4,20},{8,24},{12,28},{16,0},{20,4},{24,8},{28,12},{1,17},{... | collective-permute-start | bytes 393224 | tf_op jit(solution)/shard_map/ppermute | solution.py:399
  3.0 8.3 %collective-permute-start = (bf16[8,8192]{1,0:T(8,128)(2,1)}, bf16[8,8192]{1,0:T(8,128)(2,1)S(1)}, u32[]{:S(2)}, u32[]{:S(2)}) collective-permute-start(bf16[8,8192]{1,0:T(8,128)(2,1)} %refs_6_.2), channel_id=1, source_target_pairs={{0,8},{4,12},{8,0},{12,4},{16,24},{20,28},{24,16},{28,20},{1,9},{5... | collective-permute-start | bytes 393224 | tf_op jit(solution)/shard_map/ppermute | solution.py:399
  4.5 6.9 %collective-permute-start.2 = (bf16[8,8192]{1,0:T(8,128)(2,1)}, bf16[8,8192]{1,0:T(8,128)(2,1)S(1)}, u32[]{:S(2)}, u32[]{:S(2)}) collective-permute-start(bf16[8,8192]{1,0:T(8,128)(2,1)} %refs_6_.2), channel_id=1, source_target_pairs={{0,24},{4,28},{8,16},{12,20},{16,8},{20,12},{24,0},{28,4},{1,25},{... | collective-permute-start | bytes 393224 | tf_op jit(solution)/shard_map/ppermute | solution.py:399
  5.1 6.2 %copy-start.2 = (bf16[8,8192]{1,0:T(8,128)(2,1)S(1)}, bf16[8,8192]{1,0:T(8,128)(2,1)}, u32[]{:S(2)}) copy-start(bf16[8,8192]{1,0:T(8,128)(2,1)} %refs_6_.2) | copy-start | bytes 393220
  11.4 2.6 %collective-permute-start.3 = (bf16[8,8192]{1,0:T(8,128)(2,1)S(1)}, bf16[8,8192]{1,0:T(8,128)(2,1)S(1)}, u32[]{:S(2)}, u32[]{:S(2)}) collective-permute-start(bf16[8,8192]{1,0:T(8,128)(2,1)S(1)} %copy-done.2), channel_id=1, source_target_pairs={{0,4},{4,0},{8,12},{12,8},{16,20},{20,16},{24,28},{28,24},{1,5},{5... | collective-permute-start | bytes 393224 | tf_op jit(solution)/shard_map/ppermute | solution.py:399
  11.4 2.6 %collective-permute-start.4 = (bf16[8,8192]{1,0:T(8,128)(2,1)S(1)}, bf16[8,8192]{1,0:T(8,128)(2,1)S(1)}, u32[]{:S(2)}, u32[]{:S(2)}) collective-permute-start(bf16[8,8192]{1,0:T(8,128)(2,1)S(1)} %collective-permute-done.refs_7_), channel_id=1, source_target_pairs={{0,4},{4,0},{8,12},{12,8},{16,20},{20,16},{24,28},{28,24},{1,5},{5... | collective-permute-start | bytes 393224 | tf_op jit(solution)/shard_map/ppermute | solution.py:399
  11.9 2.1 %collective-permute-start.5 = (bf16[8,8192]{1,0:T(8,128)(2,1)S(1)}, bf16[8,8192]{1,0:T(8,128)(2,1)S(1)}, u32[]{:S(2)}, u32[]{:S(2)}) collective-permute-start(bf16[8,8192]{1,0:T(8,128)(2,1)S(1)} %collective-permute-done.1.refs_8_), channel_id=1, source_target_pairs={{0,4},{4,0},{8,12},{12,8},{16,20},{20,16},{24,28},{28,24},{1,5},{5... | collective-permute-start | bytes 393224 | tf_op jit(solution)/shard_map/ppermute | solution.py:399
  12.0 2.0 %collective-permute-start.6 = (bf16[8,8192]{1,0:T(8,128)(2,1)S(1)}, bf16[8,8192]{1,0:T(8,128)(2,1)S(1)}, u32[]{:S(2)}, u32[]{:S(2)}) collective-permute-start(bf16[8,8192]{1,0:T(8,128)(2,1)S(1)} %collective-permute-done.2.refs_9_), channel_id=1, source_target_pairs={{0,4},{4,0},{8,12},{12,8},{16,20},{20,16},{24,28},{28,24},{1,5},{5... | collective-permute-start | bytes 393224 | tf_op jit(solution)/shard_map/ppermute | solution.py:399
  12.4 1.6 %copy-start = (bf16[1,96,32,256]{3,2,1,0:T(8,128)(2,1)S(1)}, bf16[1,96,32,256]{3,2,1,0:T(8,128)(2,1)}, u32[]{:S(2)}) copy-start(bf16[1,96,32,256]{3,2,1,0:T(8,128)(2,1)} %param.26) | copy-start | bytes 4718596
  12.4 1.9 %copy-start.1 = (bf16[1,96,32,256]{3,2,1,0:T(8,128)(2,1)S(1)}, bf16[1,96,32,256]{3,2,1,0:T(8,128)(2,1)}, u32[]{:S(2)}) copy-start(bf16[1,96,32,256]{3,2,1,0:T(8,128)(2,1)} %param.27) | copy-start | bytes 4718596
  27.5 14.8 %collective-permute-start.7 = (bf16[16,4096]{1,0:T(8,128)(2,1)S(1)}, bf16[16,4096]{1,0:T(8,128)(2,1)S(1)}, u32[]{:S(2)}, u32[]{:S(2)}) collective-permute-start(bf16[16,4096]{1,0:T(8,128)(2,1)S(1)} %get-tuple-element.72), channel_id=1, source_target_pairs={{0,1},{1,0},{2,3},{3,2},{4,5},{5,4},{6,7},{7,6},{8,9},{9,8},{10,11... | collective-permute-start | bytes 393224 | tf_op jit(solution)/shard_map/ppermute | solution.py:399
  27.5 14.7 %collective-permute-start.8 = (bf16[16,2560]{1,0:T(8,128)(2,1)S(1)}, bf16[16,2560]{1,0:T(8,128)(2,1)S(1)}, u32[]{:S(2)}, u32[]{:S(2)}) collective-permute-start(bf16[16,2560]{1,0:T(8,128)(2,1)S(1)} %get-tuple-element.73), channel_id=1, source_target_pairs={{0,2},{1,3},{2,0},{3,1},{4,6},{5,7},{6,4},{7,5},{8,10},{9,11},{10,... | collective-permute-start | bytes 245768 | tf_op jit(solution)/shard_map/ppermute | solution.py:399
  27.6 14.7 %collective-permute-start.10 = (bf16[16,2560]{1,0:T(8,128)(2,1)S(1)}, bf16[16,2560]{1,0:T(8,128)(2,1)S(1)}, u32[]{:S(2)}, u32[]{:S(2)}) collective-permute-start(bf16[16,2560]{1,0:T(8,128)(2,1)S(1)} %get-tuple-element.75), channel_id=1, source_target_pairs={{0,3},{1,2},{2,1},{3,0},{4,7},{5,6},{6,5},{7,4},{8,11},{9,10},{10,... | collective-permute-start | bytes 245768 | tf_op jit(solution)/shard_map/ppermute | solution.py:399
  31.9 10.4 %collective-permute-start.9 = (bf16[16,1536]{1,0:T(8,128)(2,1)S(1)}, bf16[16,1536]{1,0:T(8,128)(2,1)S(1)}, u32[]{:S(2)}, u32[]{:S(2)}) collective-permute-start(bf16[16,1536]{1,0:T(8,128)(2,1)S(1)} %get-tuple-element.74), channel_id=1, source_target_pairs={{0,2},{1,3},{2,0},{3,1},{4,6},{5,7},{6,4},{7,5},{8,10},{9,11},{10,... | collective-permute-start | bytes 147464 | tf_op jit(solution)/shard_map/ppermute | solution.py:399
  31.9 10.4 %collective-permute-start.11 = (bf16[16,1536]{1,0:T(8,128)(2,1)S(1)}, bf16[16,1536]{1,0:T(8,128)(2,1)S(1)}, u32[]{:S(2)}, u32[]{:S(2)}) collective-permute-start(bf16[16,1536]{1,0:T(8,128)(2,1)S(1)} %get-tuple-element.76), channel_id=1, source_target_pairs={{0,3},{1,2},{2,1},{3,0},{4,7},{5,6},{6,5},{7,4},{8,11},{9,10},{10,... | collective-permute-start | bytes 147464 | tf_op jit(solution)/shard_map/ppermute | solution.py:399

commit v4 on v3

--- a/solution.py
+++ b/solution.py
@@ -13,6 +13,7 @@
 F32 = jnp.float32
 BF16 = jnp.bfloat16
 ENTRY_TRIP = 16
+SUMS = 2
 NEAR_TRIP = 16
 
 
@@ -64,42 +65,54 @@
     list_ref[...] = table.astype(jnp.int32)
 
 
-def entry_loop(table_ref, s_ref, t_ref, entries_refs, base, low, high):
+def entry_loop(table_ref, s_ref, t_ref, entries_refs, base, low, high, fresh):
     column_leaves, leaf, width = s_ref.shape
     depth = t_ref.shape[1]
+    slots = table_ref.shape[1]
     start, stop = (low - base) // ENTRY_TRIP, (high - base + ENTRY_TRIP - 1) // ENTRY_TRIP
+
+    def push(k, u):
+        pair = table_ref[0, jnp.minimum(k, slots - 1)]
+        rhs = jnp.concatenate([t_ref[pair // column_leaves], jnp.zeros((leaf - depth, leaf), BF16)], axis=0)
+        pltpu.matmul_push_rhs(rhs, staging_register=(u // 2) % 2, mxu_index=u % 2)
 
     def work(*accs):
         def drain(u, turn):
             row = jnp.maximum(turn * (ENTRY_TRIP // 2) + u // 2, 0)
             entries_refs[u % 2][row] = lax.rsqrt(pltpu.matmul_pop(accs[u % 8])).astype(BF16)
 
+        if fresh:
+            for acc in accs:
+                pltpu.matmul_pop(acc)
+
         @pl.when(stop > start)
         def _():
-            for acc in accs:
-                pltpu.matmul_pop(acc)
+            for u in range(2):
+                push(base + start * ENTRY_TRIP + u, u)
 
             @pl.loop(start, stop)
             def _(turn):
                 for u in range(ENTRY_TRIP):
-                    pair = table_ref[0, base + turn * ENTRY_TRIP + u]
-                    rhs = jnp.concatenate([t_ref[pair // column_leaves], jnp.zeros((leaf - depth, leaf), BF16)], axis=0)
-                    lhs = jnp.concatenate([s_ref[pair % column_leaves], jnp.zeros((leaf, leaf - width), BF16)], axis=1)
-                    stage = (u // 2) % 2
-                    pltpu.matmul_push_rhs(rhs, staging_register=stage, mxu_index=u % 2)
-                    pltpu.matmul_acc_lhs(accs[u % 8], lhs, load_staged_rhs=stage)
+                    k = base + turn * ENTRY_TRIP + u
+                    lhs = jnp.concatenate(
+                        [s_ref[table_ref[0, k] % column_leaves], jnp.zeros((leaf, leaf - width), BF16)], axis=1
+                    )
+                    pltpu.matmul_acc_lhs(accs[u % 8], lhs, load_staged_rhs=(u // 2) % 2)
+                    push(k + 2, u + 2)
                     if u < 4:
                         drain(ENTRY_TRIP - 4 + u, turn - 1)
                     else:
                         drain(u - 4, turn)
 
+            for u in range(2):
+                pltpu.matmul_acc_lhs(accs[u], jnp.zeros((leaf, leaf), BF16), load_staged_rhs=0)
             for u in range(ENTRY_TRIP - 4, ENTRY_TRIP):
                 drain(u, stop - 1)
 
     pl.run_scoped(work, *[pltpu.ACC(u % 2)((leaf, leaf), F32) for u in range(8)])
 
 
-def near_loop(table_ref, x_ref, entries, acc_refs, base_leaf, low, high):
+def near_loop(table_ref, x_ref, entries, acc_refs, base_leaf, low, high, fresh):
     chunk_leaves, rhs, leaf = acc_refs[0].shape
     column_leaves = x_ref.shape[0]
 
@@ -110,34 +123,52 @@
             t = jnp.clip(table_ref[0, slot] // column_leaves - base_leaf, 0, chunk_leaves - 1)
             copies = jnp.where(inside, table_ref[1, slot], 0).astype(F32)
             block = pltpu.matmul_pop(accs[u])
-            acc_refs[u % 2][t] = acc_refs[u % 2][t] + jnp.where(inside, block * copies, 0.0)
+            acc_ref = acc_refs[u % len(acc_refs)]
+            acc_ref[t] = acc_ref[t] + jnp.where(inside, block * copies, 0.0)
+
+        if fresh:
+            for acc in accs:
+                pltpu.matmul_pop(acc)
 
         @pl.when(high > low)
         def _():
-            for acc in accs:
-                pltpu.matmul_pop(acc)
-
             for *entries_refs, base in entries:
-                end = base + 2 * entries_refs[0].shape[0]
+                rows = entries_refs[0].shape[0]
+                end = base + 2 * rows
                 start = jnp.clip(low, base, end) // NEAR_TRIP
                 stop = (jnp.clip(high, base, end) + NEAR_TRIP - 1) // NEAR_TRIP
 
-                @pl.loop(start, stop)
-                def _(turn):
-                    for u in range(NEAR_TRIP):
-                        k = turn * NEAR_TRIP + u
-                        source = table_ref[0, k] % column_leaves
-                        row = turn * (NEAR_TRIP // 2) - base // 2 + u // 2
-                        stage = (u // 2) % 2
-                        pltpu.matmul_push_rhs(entries_refs[u % 2][row], staging_register=stage, mxu_index=u % 2)
-                        pltpu.matmul_acc_lhs(accs[u % 16], x_ref[source], load_staged_rhs=stage)
-                        drain((u + 8) % 16, k - 8)
+                def push(row, u):
+                    pltpu.matmul_push_rhs(
+                        entries_refs[u % 2][jnp.minimum(row, rows - 1)], staging_register=(u // 2) % 2, mxu_index=u % 2
+                    )
+
+                @pl.when(stop > start)
+                def _():
+                    for u in range(2):
+                        push(start * (NEAR_TRIP // 2) - base // 2, u)
+
+                    @pl.loop(start, stop)
+                    def _(turn):
+                        for u in range(NEAR_TRIP):
+                            k = turn * NEAR_TRIP + u
+                            row = turn * (NEAR_TRIP // 2) - base // 2 + u // 2
+                            source = table_ref[0, k] % column_leaves
+                            pltpu.matmul_acc_lhs(accs[u % 16], x_ref[source], load_staged_rhs=(u // 2) % 2)
+                            push(row + 1, u + 2)
+                            drain((u + 8) % 16, k - 8)
+
+                    for u in range(2):
+                        pltpu.matmul_acc_lhs(accs[16 + u], jnp.zeros((16, leaf), BF16), load_staged_rhs=0)
+                        pltpu.matmul_pop(accs[16 + u])
 
             end = (high + NEAR_TRIP - 1) // NEAR_TRIP * NEAR_TRIP
             for u in range(8):
                 drain(u + 8, end - 8 + u)
 
-    pl.run_scoped(work, *[pltpu.ACC(u % 2)((rhs, leaf), F32) for u in range(16)])
+    spare = pltpu.ACC(0)((rhs, leaf), F32), pltpu.ACC(1)((rhs, leaf), F32)
+    flush = pltpu.ACC(0)((16, leaf), F32), pltpu.ACC(1)((16, leaf), F32)
+    pl.run_scoped(work, *(spare * 8), *flush, *(spare * 7 if fresh else ()))
 
 
 def first_entries_kernel(*refs, column_leaves, row_leaves, leaf, indices):
@@ -150,15 +181,13 @@
     for load in loads:
         load.start()
     nsrc_ref, ntgt_ref, spts_ref, area_ref, tpts_ref = copies
-    for load in loads[:2]:
+    for load in loads[:5]:
         load.wait()
     used = lax.broadcasted_iota(jnp.int32, nsrc_ref.shape, 1) < fill_ref[0, 0]
     ids = jnp.where(used, ntgt_ref[...] * column_leaves + nsrc_ref[...], -1)
     build_list(ids, list_ref, first_leaves(row_leaves) * column_leaves)
     copy = pltpu.make_async_copy(list_ref, table_ref, sem)
     copy.start()
-    for load in loads[2:5]:
-        load.wait()
 
     tx, ty, tz = (tpts_ref[i : i + 1, :] - 0.5 for i in range(3))
     norm = tx * tx + ty * ty + tz * tz
@@ -180,14 +209,16 @@
         s_ref[s] = jnp.concatenate([column, jnp.zeros((leaf, 128 - column.shape[1]), BF16)], axis=1)
 
     copy.wait()
-    entry_loop(table_ref, s_ref, t_ref, entries_refs, 0, 0, jnp.minimum(table_ref[2, 0], 2 * entries_refs[0].shape[0]))
+    entry_loop(table_ref, s_ref, t_ref, entries_refs, 0, 0, jnp.minimum(table_ref[2, 0], 2 * entries_refs[0].shape[0]), True)
     for load in loads[5:]:
         load.wait()
 
 
-def second_entries_kernel(table_ref, s_ref, t_ref, *entries_refs, first):
+def more_entries_kernel(table_ref, s_ref, t_ref, *entries_refs, first):
+    slots = table_ref.shape[1]
     last = first + 2 * entries_refs[0].shape[0]
-    entry_loop(table_ref, s_ref, t_ref, entries_refs, first, first, jnp.clip(table_ref[2, 0], first, last))
+    low = jnp.clip(table_ref[3, 0], first, last) if last == slots else first
+    entry_loop(table_ref, s_ref, t_ref, entries_refs, first, low, jnp.clip(table_ref[2, 0], first, last), False)
 
 
 VMEM = pl.BlockSpec(memory_space=pltpu.VMEM)
@@ -236,12 +267,11 @@
     )(near_fill, *hbm_inputs)
 
 
-def second_entries(table, s_features, t_features):
-    slots = table.shape[1]
+def more_entries(table, s_features, t_features, first, count):
     leaf = s_features.shape[1]
     return pl.pallas_call(
-        functools.partial(second_entries_kernel, first=first_count(slots)),
-        out_shape=(pltpu.VMEM((second_count(slots) // 2, leaf, leaf), BF16),) * 2,
+        functools.partial(more_entries_kernel, first=first),
+        out_shape=(pltpu.VMEM((count // 2, leaf, leaf), BF16),) * 2,
         in_specs=[SMEM, VMEM, VMEM],
         out_specs=(VMEM, VMEM),
         compiler_params=pltpu.CompilerParams(vmem_limit_bytes=4 << 20),
@@ -298,31 +328,32 @@
             acc_ref[t] = acc_ref[t] + blocks[u]
 
 
-def near_kernel(*refs, base_leaf, plain, out_carried):
-    (table_ref, tfill_ref, far_ref, x_ref), first_refs, second_refs, (s_ref, t_ref) = refs[:4], refs[4:6], refs[6:8], refs[8:10]
-    carried = len(out_carried)
-    carried_refs = refs[10 : 10 + carried]
-    out_refs, rest_refs, acc_refs = refs[10 + carried : -4], refs[-4:-2], refs[-2:]
+def near_kernel(*refs, base_leaf, plain, out_carried, firsts, complete):
+    carried, arrays = len(out_carried), 2 * len(firsts)
+    (table_ref, tfill_ref, far_ref, x_ref, s_ref, t_ref), made_refs = refs[:6], refs[6 : 6 + arrays]
+    carried_refs = refs[6 + arrays : 6 + arrays + carried]
+    tail = len(refs) - SUMS
+    out_refs, rest_refs, acc_refs = refs[6 + arrays + carried : tail - 2], refs[tail - 2 : tail], refs[tail:]
     chunk_leaves, rhs, leaf = acc_refs[0].shape
     total, half = table_ref[2, 0], table_ref[3, 0]
     low = half if base_leaf > 0 else 0
     high = total if base_leaf + chunk_leaves == far_ref.shape[0] else half
-    first, second = 2 * first_refs[0].shape[0], 2 * second_refs[0].shape[0]
-    made = first + second
+    made = firsts[-1] + 2 * made_refs[-1].shape[0]
     for acc_ref in acc_refs:
         acc_ref[...] = jnp.zeros_like(acc_ref)
     near_loop(
-        table_ref, x_ref, [(*first_refs, 0), (*second_refs, first)], acc_refs, base_leaf,
-        jnp.minimum(low, made), jnp.minimum(high, made),
-    )
-    rest = (jnp.maximum(low, made), jnp.maximum(high, made))
-    entry_loop(table_ref, s_ref, t_ref, rest_refs, made, *rest)
-    near_loop(table_ref, x_ref, [(*rest_refs, made)], acc_refs, base_leaf, *rest)
+        table_ref, x_ref, [(made_refs[2 * i], made_refs[2 * i + 1], first) for i, first in enumerate(firsts)], acc_refs,
+        base_leaf, jnp.minimum(low, made), jnp.minimum(high, made), base_leaf == 0,
+    )
+    if not complete:
+        rest = (jnp.maximum(low, made), jnp.maximum(high, made))
+        entry_loop(table_ref, s_ref, t_ref, rest_refs, made, *rest, False)
+        near_loop(table_ref, x_ref, [(*rest_refs, made)], acc_refs, base_leaf, *rest, False)
 
     if plain:
         lane_t = lax.broadcasted_iota(jnp.int32, (rhs, leaf), 1)
         for t in range(chunk_leaves):
-            value = acc_refs[0][t] + acc_refs[1][t] + far_ref[base_leaf + t]
+            value = sum((acc_ref[t] for acc_ref in acc_refs), far_ref[base_leaf + t])
             out_refs[0][:, t * leaf : (t + 1) * leaf] = jnp.where(lane_t < tfill_ref[base_leaf + t], value, 0.0)
     else:
         owners = len(out_refs)
@@ -336,7 +367,7 @@
                 out_refs[m][:, :shift] = carried_refs[out_carried.index(m)][...]
             for t in range(chunk_leaves):
                 rows = pl.ds(start, height)
-                value = acc_refs[0][t, rows, :] + acc_refs[1][t, rows, :] + far_ref[base_leaf + t, rows, :]
+                value = sum((acc_ref[t, rows, :] for acc_ref in acc_refs), far_ref[base_leaf + t, rows, :])
                 value = jnp.where(lane_t < tfill_ref[base_leaf + t], value, 0.0)
                 window = slice(shift + t * leaf, shift + (t + 1) * leaf)
                 out_refs[m][:, window] = value.astype(out_refs[m].dtype)
@@ -362,6 +393,8 @@
 
 
 def near_field(table, target_fill, far, x, made, features, owners, plain, leaves, carried=(), out_carried=()):
+    firsts, arrays = zip(*made)
+    made = [value for pair in arrays for value in pair]
     _, rhs, leaf = far.shape
     width = len(leaves) * leaf
     if plain:
@@ -373,17 +406,22 @@
             )
             for m in range(owners)
         )
-    rest = (table.shape[1] - sum(value.shape[0] for value in made)) // 2
+    rest = table.shape[1] // 2 - sum(value.shape[0] for value in made) // 2
+    complete = rest == 0
+    rest = max(rest, 1)
     return pl.pallas_call(
-        functools.partial(near_kernel, base_leaf=leaves[0], plain=plain, out_carried=tuple(out_carried)),
+        functools.partial(
+            near_kernel, base_leaf=leaves[0], firsts=firsts, complete=complete, plain=plain,
+            out_carried=tuple(out_carried),
+        ),
         out_shape=out_shape,
-        in_specs=[SMEM] * 2 + [VMEM] * (8 + len(carried)),
+        in_specs=[SMEM] * 2 + [VMEM] * (4 + len(made) + len(carried)),
         out_specs=(VMEM,) * len(out_shape),
-        scratch_shapes=[pltpu.VMEM((rest, leaf, leaf), BF16)] * 2 + [pltpu.VMEM((len(leaves), rhs, leaf), F32)] * 2,
-        compiler_params=pltpu.CompilerParams(vmem_limit_bytes=20 << 20),
+        scratch_shapes=[pltpu.VMEM((rest, leaf, leaf), BF16)] * 2 + [pltpu.VMEM((len(leaves), rhs, leaf), F32)] * SUMS,
+        compiler_params=pltpu.CompilerParams(vmem_limit_bytes=(8 if complete else 24) << 20),
         cost_estimate=pl.CostEstimate(flops=4_000_000_000, bytes_accessed=8 << 20, transcendentals=0),
         name="near",
-    )(table, target_fill, far, x, *made, *features, *carried)
+    )(table, target_fill, far, x, *features, *made, *carried)
 
 
 def shards(
@@ -410,10 +448,12 @@
     if not plain:
         pieces, table = lax.optimization_barrier((pieces, table))
         pieces = pieces + [swap(piece, "row", rows, 1) for piece in pieces]
-    more_entries = list(second_entries(table, *features))
+    slots = near_source.shape[1]
+    first, second = first_count(slots), second_count(slots)
+    more = list(more_entries(table, *features, first, second))
     if not plain:
-        pieces, more_entries[0] = lax.optimization_barrier((pieces, more_entries[0]))
-    made = (*entries, *more_entries)
+        pieces, more[0] = lax.optimization_barrier((pieces, more[0]))
+    made = [(0, entries), (first, more)]
     x, far = far_field(
         source_fill, row_leaves, far_source, far_target, far_rank, left_basis[0], right_basis[0], pieces, plain
     )
@@ -430,18 +470,19 @@
         return swap(value, "col", columns, mask)
 
     split = first_leaves(row_leaves)
-    inputs = (table, target_fill, far, x, made, features, columns, plain)
-    first = near_field(*inputs, range(split))
-    early = {mask: exchange(first[mask], mask) for mask in range(2, columns)}
-    second = near_field(*inputs, range(split, row_leaves), (first[1],), (1,))
-    late = {mask: exchange(second[mask], mask) for mask in late_order(columns)}
-    result = jnp.concatenate([first[0], second[0]], axis=1) + late[1].astype(F32)
+    one = near_field(table, target_fill, far, x, made, features, columns, plain, range(split))
+    early = {mask: exchange(one[mask], mask) for mask in exchange_order(columns)}
+    table, one_last = lax.optimization_barrier((table, one[0]))
+    made = made + [(first + second, more_entries(table, *features, first + second, slots - first - second))]
+    two = near_field(table, target_fill, far, x, made, features, columns, plain, range(split, row_leaves))
+    late = {mask: exchange(two[mask], mask) for mask in exchange_order(columns)}
+    result = jnp.concatenate([one_last, two[0]], axis=1)
     for mask in early:
         result = result + jnp.concatenate([early[mask], late[mask]], axis=1).astype(F32)
     return result
 
 
-def late_order(columns):
+def exchange_order(columns):
     return list(range(2, columns)) + [1]
 
 

time: 43.2 us -> 41.1 us (0.951)
  waiting for transfers between devices: 8.85 us -> 5.04 us
  starting transfers between devices: 11.5 us -> 13.5 us
    ppermute x12 -> x13, waiting for transfers between devices: 8.85 us -> 5.04 us  [swap(): return lax.ppermute(value, axis, [(i, i ^ mask) for i in range(size)])]
    ppermute x12 -> x13, starting transfers between devices: 11.5 us -> 13.5 us  [swap(): return lax.ppermute(value, axis, [(i, i ^ mask) for i in range(size)])]
    pallas_call x3 -> x4, Pallas kernels: 11.8 us -> 11.3 us  [the longest x2 6.65 us: near_field(): pl.pallas_call(functools.partial(near_kernel, base_leaf=leaves[0], firsts...]
  transfers between devices with their start and end apart: 12 -> 13, of which waited for: 1 -> 1; matrix products, arithmetic and copies ran while one was open for 0% -> 0% of each run, Pallas kernels for 18% -> 19%
where the time goes in v4:
time: 41.1 us; the launch traced here: 41 us
  Pallas kernels  20.4 us (50%)
  starting transfers between devices  13.5 us (33%)
  waiting for transfers between devices  5.04 us (12%)
  between operations  0.81 us (2%)
  other arithmetic  0.76 us (2%)
  local copies, waits for them, and re-layouts  0.44 us (1%)
    ppermute x13, starting transfers between devices, swap(): return lax.ppermute(value, axis, [(i, i ^ mask) for i in range(size)])  13.5 us
    pallas_call x2, Pallas kernels, near_field(): pl.pallas_call(functools.partial(near_kernel, base_leaf=leaves[0], firsts...  6.65 us
    pallas_call x1, Pallas kernels, first_entries(): pl.pallas_call(functools.partial(first_entries_kernel, column_leaves=colu...  6.31 us
    ppermute x13, waiting for transfers between devices, swap(): return lax.ppermute(value, axis, [(i, i ^ mask) for i in range(size)])  5.04 us
    pallas_call x2, Pallas kernels, more_entries(): pl.pallas_call(functools.partial(more_entries_kernel, first=first), out_s...  4.61 us
    pallas_call x1, Pallas kernels, far_field(): pl.pallas_call(functools.partial(far_kernel, pieces=len(pieces), plain=pl...  2.84 us
  transfers between devices with their start and end apart: 13, of which 1 were waited for; matrix products, arithmetic and copies ran while one was open for 0% of the time, Pallas kernels for 19%

profile of v4, /device:TPU:0, one launch (start us, length us, event | category | flops | bytes accessed | tf_op | source)
XLA Modules:
  0.0 41.0 jit_solution(4775870743663444263)
XLA Ops:
  0.0 3.0 %collective-permute-start.1 = (bf16[8,8192]{1,0:T(8,128)(2,1)}, bf16[8,8192]{1,0:T(8,128)(2,1)S(1)}, u32[]{:S(2)}, u32[]{:S(2)}) collective-permute-start(bf16[8,8192]{1,0:T(8,128)(2,1)} %refs_6_.2), channel_id=1, source_target_pairs={{0,16},{4,20},{8,24},{12,28},{16,0},{20,4},{24,8},{28,12},{1,17},{... | collective-permute-start | bytes 393224 | tf_op jit(solution)/shard_map/ppermute | solution.py:437
  3.0 1.5 %collective-permute-start = (bf16[8,8192]{1,0:T(8,128)(2,1)}, bf16[8,8192]{1,0:T(8,128)(2,1)S(1)}, u32[]{:S(2)}, u32[]{:S(2)}) collective-permute-start(bf16[8,8192]{1,0:T(8,128)(2,1)} %refs_6_.2), channel_id=1, source_target_pairs={{0,8},{4,12},{8,0},{12,4},{16,24},{20,28},{24,16},{28,20},{1,9},{5... | collective-permute-start | bytes 393224 | tf_op jit(solution)/shard_map/ppermute | solution.py:437
  4.5 0.0 collective-permute-start.2
  5.1 0.0 copy-start.2
  5.2 6.3 %entries.1 = (bf16[48,256,256]{2,1,0:T(8,128)(2,1)S(1)}, bf16[48,256,256]{2,1,0:T(8,128)(2,1)S(1)}, s32[8,256]{1,0:T(8,128)S(4)}, bf16[32,256,128]{2,1,0:T(8,128...) custom-call(s32[1,1]{1,0:T(1,128)S(6)} %copy.15.refs_0_, ...), custom_call_target="tpu_custom_call" | custom-call | flops 8000000000 | bytes 1048576 | tf_op jit(solution)/shard_map/entries/pallas_call | solution.py:248
  11.5 0.0 collective-permute-done.1.refs_8_
  11.5 0.0 collective-permute-done.refs_7_
  11.5 0.0 collective-permute-done.2.refs_9_
  11.5 0.0 copy-done.2
  11.5 0.1 collective-permute-start.3
  11.6 0.5 %collective-permute-start.4 = (bf16[8,8192]{1,0:T(8,128)(2,1)S(1)}, bf16[8,8192]{1,0:T(8,128)(2,1)S(1)}, u32[]{:S(2)}, u32[]{:S(2)}) collective-permute-start(bf16[8,8192]{1,0:T(8,128)(2,1)S(1)} %collective-permute-done.refs_7_), channel_id=1, source_target_pairs={{0,4},{4,0},{8,12},{12,8},{16,20},{20,16},{24,28},{28,24},{1,5},{5... | collective-permute-start | bytes 393224 | tf_op jit(solution)/shard_map/ppermute | solution.py:437
  12.1 0.1 collective-permute-start.5
  12.2 0.4 %collective-permute-start.6 = (bf16[8,8192]{1,0:T(8,128)(2,1)S(1)}, bf16[8,8192]{1,0:T(8,128)(2,1)S(1)}, u32[]{:S(2)}, u32[]{:S(2)}) collective-permute-start(bf16[8,8192]{1,0:T(8,128)(2,1)S(1)} %collective-permute-done.2.refs_9_), channel_id=1, source_target_pairs={{0,4},{4,0},{8,12},{12,8},{16,20},{20,16},{24,28},{28,24},{1,5},{5... | collective-permute-start | bytes 393224 | tf_op jit(solution)/shard_map/ppermute | solution.py:437
  12.6 0.0 copy-start
  12.6 0.0 copy-start.1
  12.6 1.4 %entries_rest.2 = (bf16[16,256,256]{2,1,0:T(8,128)(2,1)S(1)}, bf16[16,256,256]{2,1,0:T(8,128)(2,1)S(1)}) custom-call(s32[8,256]{1,0:T(8,128)S(4)} %get-tuple-element.75.table_ref.refs_0_, bf16[32,256,128]{2,1,0:T(8,128)(2,1)S(1)} %get-tuple-element.56.s_ref.refs_4_, bf16[16,64,256]{2,1,0:T(8,128)(2,1)S(1)} %get-tuple-element.57.t_ref.refs_5_), custom_call_target="tpu_custom_call" | custom-call | flops 8000000000 | bytes 1048576 | tf_op jit(solution)/shard_map/entries_rest/pallas_call | solution.py:272
  14.0 0.0 collective-permute-done.3.refs_10_
  14.0 0.0 collective-permute-done.4.refs_11_
  14.0 0.0 collective-permute-done.5.refs_12_
  14.0 0.0 collective-permute-done.6.refs_13_
  14.0 0.0 copy-done
  14.1 0.4 %copy-done.1 = bf16[1,96,32,256]{3,2,1,0:T(8,128)(2,1)S(1)} copy-done((bf16[1,96,32,256]{3,2,1,0:T(8,128)(2,1)S(1)}, bf16[1,96,32,256]{3,2,1,0:T(8,128)(2,1)}, u32[]{:S(2)}) %copy-start.1) | copy-done | bytes 1572888
  14.5 2.8 %far.1 = (bf16[32,64,256]{2,1,0:T(8,128)(2,1)S(1)}, f32[16,64,256]{2,1,0:T(8,128)S(1)}) custom-call(s32[32]{0:T(128)S(4)} %get-tuple-element.48.refs_0_, s32[1,96]{1,0:T(1,128)S(4)} %get-tuple-element.49.refs_1_, s32[1,96]{1,0:T(1,128)S(4)} %get-tuple-element.50.refs_2_, s32[1,96]{1,0:T(1,128)S(4)} %get-tuple-element.51.refs_3_, ...), custom_call_target="tpu_custom_call" | custom-call | flops 2000000000 | bytes 8388608 | tf_op jit(solution)/shard_map/far/pallas_call | solution.py:383
  17.3 3.8 %near.2 = (f32[16,2560]{1,0:T(8,128)S(1)}, bf16[16,2560]{1,0:T(8,128)(2,1)S(1)}, bf16[16,2560]{1,0:T(8,128)(2,1)S(1)}, bf16[16,2560]{1,0:T(8,128)(2,1)S(1)}) custom-call(s32[8,256]{1,0:T(8,128)S(4)} %get-tuple-element.75.table_ref.refs_0_, s32[16]{0:T(128)S(4)} %get-tuple-element.47.refs_1_, f32[16,64,256]{2,1,0:T(8,128)S(1)} %get-tuple-element.67.refs_2_, ...), custom_call_target="tpu_custom_call" | custom-call | flops 4000000000 | bytes 8388608 | tf_op jit(solution)/shard_map/near/pallas_call | solution.py:412
  21.1 3.2 %entries_rest.3 = (bf16[64,256,256]{2,1,0:T(8,128)(2,1)S(1)}, bf16[64,256,256]{2,1,0:T(8,128)(2,1)S(1)}) custom-call(s32[8,256]{1,0:T(8,128)S(4)} %get-tuple-element.75.table_ref.refs_0_, bf16[32,256,128]{2,1,0:T(8,128)(2,1)S(1)} %get-tuple-element.56.s_ref.refs_4_, bf16[16,64,256]{2,1,0:T(8,128)(2,1)S(1)} %get-tuple-element.57.t_ref.refs_5_), custom_call_target="tpu_custom_call" | custom-call | flops 8000000000 | bytes 1048576 | tf_op jit(solution)/shard_map/entries_rest/pallas_call | solution.py:272
  24.4 2.9 %near.3 = (f32[16,1536]{1,0:T(8,128)S(1)}, bf16[16,1536]{1,0:T(8,128)(2,1)S(1)}, bf16[16,1536]{1,0:T(8,128)(2,1)S(1)}, bf16[16,1536]{1,0:T(8,128)(2,1)S(1)}) custom-call(s32[8,256]{1,0:T(8,128)S(4)} %get-tuple-element.75.table_ref.refs_0_, s32[16]{0:T(128)S(4)} %get-tuple-element.47.refs_1_, f32[16,64,256]{2,1,0:T(8,128)S(1)} %get-tuple-element.67.refs_2_, ...), custom_call_target="tpu_custom_call" | custom-call | flops 4000000000 | bytes 8388608 | tf_op jit(solution)/shard_map/near/pallas_call | solution.py:412
  27.2 0.1 collective-permute-start.8
  27.3 2.9 %collective-permute-start.7 = (bf16[16,2560]{1,0:T(8,128)(2,1)S(1)}, bf16[16,2560]{1,0:T(8,128)(2,1)S(1)}, u32[]{:S(2)}, u32[]{:S(2)}) collective-permute-start(bf16[16,2560]{1,0:T(8,128)(2,1)S(1)} %get-tuple-element.79), channel_id=1, source_target_pairs={{0,2},{1,3},{2,0},{3,1},{4,6},{5,7},{6,4},{7,5},{8,10},{9,11},{10,... | collective-permute-start | bytes 245768 | tf_op jit(solution)/shard_map/ppermute | solution.py:437
  30.2 0.0 collective-permute-start.9
  30.2 0.6 %collective-permute-start.11 = (bf16[16,2560]{1,0:T(8,128)(2,1)S(1)}, bf16[16,2560]{1,0:T(8,128)(2,1)S(1)}, u32[]{:S(2)}, u32[]{:S(2)}) collective-permute-start(bf16[16,2560]{1,0:T(8,128)(2,1)S(1)} %get-tuple-element.83), channel_id=1, source_target_pairs={{0,1},{1,0},{2,3},{3,2},{4,5},{5,4},{6,7},{7,6},{8,9},{9,8},{10,11... | collective-permute-start | bytes 245768 | tf_op jit(solution)/shard_map/ppermute | solution.py:437
  30.9 3.2 %collective-permute-start.10 = (bf16[16,1536]{1,0:T(8,128)(2,1)S(1)}, bf16[16,1536]{1,0:T(8,128)(2,1)S(1)}, u32[]{:S(2)}, u32[]{:S(2)}) collective-permute-start(bf16[16,1536]{1,0:T(8,128)(2,1)S(1)} %get-tuple-element.82), channel_id=1, source_target_pairs={{0,3},{1,2},{2,1},{3,0},{4,7},{5,6},{6,5},{7,4},{8,11},{9,10},{10,... | collective-permute-start | bytes 147464 | tf_op jit(solution)/shard_map/ppermute | solution.py:437
  34.0 0.0 collective-permute-done.8
  34.0 1.1 %collective-permute-start.12 = (bf16[16,1536]{1,0:T(8,128)(2,1)S(1)}, bf16[16,1536]{1,0:T(8,128)(2,1)S(1)}, u32[]{:S(2)}, u32[]{:S(2)}) collective-permute-start(bf16[16,1536]{1,0:T(8,128)(2,1)S(1)} %get-tuple-element.84), channel_id=1, source_target_pairs={{0,1},{1,0},{2,3},{3,2},{4,5},{5,4},{6,7},{7,6},{8,9},{9,8},{10,11... | collective-permute-start | bytes 147464 | tf_op jit(solution)/shard_map/ppermute | solution.py:437
  35.2 5.0 %collective-permute-done.10 = bf16[16,1536]{1,0:T(8,128)(2,1)S(1)} collective-permute-done((bf16[16,1536]{1,0:T(8,128)(2,1)S(1)}, bf16[16,1536]{1,0:T(8,128)(2,1)S(1)}, u32[]{:S(2)}, u32[]{:S(2)}) %collective-permute-start.10) | collective-permute-done | bytes 49184 | tf_op jit(solution)/shard_map/ppermute | solution.py:437
  40.2 0.0 collective-permute-done.12
  40.2 0.0 collective-permute-done.7
  40.2 0.0 collective-permute-done.9
  40.2 0.0 collective-permute-done.11
  40.2 0.8 %fusion.1 = f32[16,4096]{1,0:T(8,128)} fusion(f32[16,1536]{1,0:T(8,128)S(1)} %get-tuple-element.78, f32[16,2560]{1,0:T(8,128)S(1)} %get-tuple-element.74, bf16[16,1536]{1,0:T(8,128)(2,1)S(1)} %collective-permute-done.8, bf16[16,2560]{1,0:T(8,128)(2,1)S(1)} %collective-permute-done.7, bf16[16,1536]{1,0:T(8,128)(2,1)S(1)} %collective-permute-done.10, ...), kind=kLoop, calls=%fused_computation.2 | loop fusion | flops 1048576 | bytes 917504 | tf_op jit(solution)/shard_map/add | solution.py:481
Async XLA Ops:
  0.0 11.5 %collective-permute-start.1 = (bf16[8,8192]{1,0:T(8,128)(2,1)}, bf16[8,8192]{1,0:T(8,128)(2,1)S(1)}, u32[]{:S(2)}, u32[]{:S(2)}) collective-permute-start(bf16[8,8192]{1,0:T(8,128)(2,1)} %refs_6_.2), channel_id=1, source_target_pairs={{0,16},{4,20},{8,24},{12,28},{16,0},{20,4},{24,8},{28,12},{1,17},{... | collective-permute-start | bytes 393224 | tf_op jit(solution)/shard_map/ppermute | solution.py:437
  3.0 8.5 %collective-permute-start = (bf16[8,8192]{1,0:T(8,128)(2,1)}, bf16[8,8192]{1,0:T(8,128)(2,1)S(1)}, u32[]{:S(2)}, u32[]{:S(2)}) collective-permute-start(bf16[8,8192]{1,0:T(8,128)(2,1)} %refs_6_.2), channel_id=1, source_target_pairs={{0,8},{4,12},{8,0},{12,4},{16,24},{20,28},{24,16},{28,20},{1,9},{5... | collective-permute-start | bytes 393224 | tf_op jit(solution)/shard_map/ppermute | solution.py:437
  4.5 7.0 %collective-permute-start.2 = (bf16[8,8192]{1,0:T(8,128)(2,1)}, bf16[8,8192]{1,0:T(8,128)(2,1)S(1)}, u32[]{:S(2)}, u32[]{:S(2)}) collective-permute-start(bf16[8,8192]{1,0:T(8,128)(2,1)} %refs_6_.2), channel_id=1, source_target_pairs={{0,24},{4,28},{8,16},{12,20},{16,8},{20,12},{24,0},{28,4},{1,25},{... | collective-permute-start | bytes 393224 | tf_op jit(solution)/shard_map/ppermute | solution.py:437
  5.1 6.4 %copy-start.2 = (bf16[8,8192]{1,0:T(8,128)(2,1)S(1)}, bf16[8,8192]{1,0:T(8,128)(2,1)}, u32[]{:S(2)}) copy-start(bf16[8,8192]{1,0:T(8,128)(2,1)} %refs_6_.2) | copy-start | bytes 393220
  11.5 2.5 %collective-permute-start.3 = (bf16[8,8192]{1,0:T(8,128)(2,1)S(1)}, bf16[8,8192]{1,0:T(8,128)(2,1)S(1)}, u32[]{:S(2)}, u32[]{:S(2)}) collective-permute-start(bf16[8,8192]{1,0:T(8,128)(2,1)S(1)} %copy-done.2), channel_id=1, source_target_pairs={{0,4},{4,0},{8,12},{12,8},{16,20},{20,16},{24,28},{28,24},{1,5},{5... | collective-permute-start | bytes 393224 | tf_op jit(solution)/shard_map/ppermute | solution.py:437
  11.6 2.4 %collective-permute-start.4 = (bf16[8,8192]{1,0:T(8,128)(2,1)S(1)}, bf16[8,8192]{1,0:T(8,128)(2,1)S(1)}, u32[]{:S(2)}, u32[]{:S(2)}) collective-permute-start(bf16[8,8192]{1,0:T(8,128)(2,1)S(1)} %collective-permute-done.refs_7_), channel_id=1, source_target_pairs={{0,4},{4,0},{8,12},{12,8},{16,20},{20,16},{24,28},{28,24},{1,5},{5... | collective-permute-start | bytes 393224 | tf_op jit(solution)/shard_map/ppermute | solution.py:437
  12.1 1.9 %collective-permute-start.5 = (bf16[8,8192]{1,0:T(8,128)(2,1)S(1)}, bf16[8,8192]{1,0:T(8,128)(2,1)S(1)}, u32[]{:S(2)}, u32[]{:S(2)}) collective-permute-start(bf16[8,8192]{1,0:T(8,128)(2,1)S(1)} %collective-permute-done.1.refs_8_), channel_id=1, source_target_pairs={{0,4},{4,0},{8,12},{12,8},{16,20},{20,16},{24,28},{28,24},{1,5},{5... | collective-permute-start | bytes 393224 | tf_op jit(solution)/shard_map/ppermute | solution.py:437
  12.2 1.9 %collective-permute-start.6 = (bf16[8,8192]{1,0:T(8,128)(2,1)S(1)}, bf16[8,8192]{1,0:T(8,128)(2,1)S(1)}, u32[]{:S(2)}, u32[]{:S(2)}) collective-permute-start(bf16[8,8192]{1,0:T(8,128)(2,1)S(1)} %collective-permute-done.2.refs_9_), channel_id=1, source_target_pairs={{0,4},{4,0},{8,12},{12,8},{16,20},{20,16},{24,28},{28,24},{1,5},{5... | collective-permute-start | bytes 393224 | tf_op jit(solution)/shard_map/ppermute | solution.py:437
  12.6 1.4 %copy-start = (bf16[1,96,32,256]{3,2,1,0:T(8,128)(2,1)S(1)}, bf16[1,96,32,256]{3,2,1,0:T(8,128)(2,1)}, u32[]{:S(2)}) copy-start(bf16[1,96,32,256]{3,2,1,0:T(8,128)(2,1)} %param.26) | copy-start | bytes 4718596
  12.6 1.9 %copy-start.1 = (bf16[1,96,32,256]{3,2,1,0:T(8,128)(2,1)S(1)}, bf16[1,96,32,256]{3,2,1,0:T(8,128)(2,1)}, u32[]{:S(2)}) copy-start(bf16[1,96,32,256]{3,2,1,0:T(8,128)(2,1)} %param.27) | copy-start | bytes 4718596
  27.2 6.8 %collective-permute-start.8 = (bf16[16,1536]{1,0:T(8,128)(2,1)S(1)}, bf16[16,1536]{1,0:T(8,128)(2,1)S(1)}, u32[]{:S(2)}, u32[]{:S(2)}) collective-permute-start(bf16[16,1536]{1,0:T(8,128)(2,1)S(1)} %get-tuple-element.80), channel_id=1, source_target_pairs={{0,2},{1,3},{2,0},{3,1},{4,6},{5,7},{6,4},{7,5},{8,10},{9,11},{10,... | collective-permute-start | bytes 147464 | tf_op jit(solution)/shard_map/ppermute | solution.py:437
  27.3 12.9 %collective-permute-start.7 = (bf16[16,2560]{1,0:T(8,128)(2,1)S(1)}, bf16[16,2560]{1,0:T(8,128)(2,1)S(1)}, u32[]{:S(2)}, u32[]{:S(2)}) collective-permute-start(bf16[16,2560]{1,0:T(8,128)(2,1)S(1)} %get-tuple-element.79), channel_id=1, source_target_pairs={{0,2},{1,3},{2,0},{3,1},{4,6},{5,7},{6,4},{7,5},{8,10},{9,11},{10,... | collective-permute-start | bytes 245768 | tf_op jit(solution)/shard_map/ppermute | solution.py:437
  30.2 10.0 %collective-permute-start.9 = (bf16[16,2560]{1,0:T(8,128)(2,1)S(1)}, bf16[16,2560]{1,0:T(8,128)(2,1)S(1)}, u32[]{:S(2)}, u32[]{:S(2)}) collective-permute-start(bf16[16,2560]{1,0:T(8,128)(2,1)S(1)} %get-tuple-element.81), channel_id=1, source_target_pairs={{0,3},{1,2},{2,1},{3,0},{4,7},{5,6},{6,5},{7,4},{8,11},{9,10},{10,... | collective-permute-start | bytes 245768 | tf_op jit(solution)/shard_map/ppermute | solution.py:437
  30.2 10.0 %collective-permute-start.11 = (bf16[16,2560]{1,0:T(8,128)(2,1)S(1)}, bf16[16,2560]{1,0:T(8,128)(2,1)S(1)}, u32[]{:S(2)}, u32[]{:S(2)}) collective-permute-start(bf16[16,2560]{1,0:T(8,128)(2,1)S(1)} %get-tuple-element.83), channel_id=1, source_target_pairs={{0,1},{1,0},{2,3},{3,2},{4,5},{5,4},{6,7},{7,6},{8,9},{9,8},{10,11... | collective-permute-start | bytes 245768 | tf_op jit(solution)/shard_map/ppermute | solution.py:437
  30.9 9.3 %collective-permute-start.10 = (bf16[16,1536]{1,0:T(8,128)(2,1)S(1)}, bf16[16,1536]{1,0:T(8,128)(2,1)S(1)}, u32[]{:S(2)}, u32[]{:S(2)}) collective-permute-start(bf16[16,1536]{1,0:T(8,128)(2,1)S(1)} %get-tuple-element.82), channel_id=1, source_target_pairs={{0,3},{1,2},{2,1},{3,0},{4,7},{5,6},{6,5},{7,4},{8,11},{9,10},{10,... | collective-permute-start | bytes 147464 | tf_op jit(solution)/shard_map/ppermute | solution.py:437
  34.0 6.1 %collective-permute-start.12 = (bf16[16,1536]{1,0:T(8,128)(2,1)S(1)}, bf16[16,1536]{1,0:T(8,128)(2,1)S(1)}, u32[]{:S(2)}, u32[]{:S(2)}) collective-permute-start(bf16[16,1536]{1,0:T(8,128)(2,1)S(1)} %get-tuple-element.84), channel_id=1, source_target_pairs={{0,1},{1,0},{2,3},{3,2},{4,5},{5,4},{6,7},{7,6},{8,9},{9,8},{10,11... | collective-permute-start | bytes 147464 | tf_op jit(solution)/shard_map/ppermute | solution.py:437

commit v5 on v4

--- a/solution.py
+++ b/solution.py
@@ -171,9 +171,10 @@
     pl.run_scoped(work, *(spare * 8), *flush, *(spare * 7 if fresh else ()))
 
 
-def first_entries_kernel(*refs, column_leaves, row_leaves, leaf, indices):
-    fill_ref, inputs, index_inputs = refs[0], refs[1:6], refs[6 : 6 + indices]
-    outputs, scratch = refs[6 + indices : 11 + 2 * indices], refs[11 + 2 * indices :]
+def first_entries_kernel(*refs, column_leaves, row_leaves, leaf, indices, bases):
+    fill_ref, inputs, index_inputs = refs[0], refs[1:6], refs[6 : 6 + indices + bases]
+    moved = indices + bases
+    outputs, scratch = refs[6 + moved : 11 + 2 * moved], refs[11 + 2 * moved :]
     (*entries_refs, table_ref, s_ref, t_ref), index_outputs = outputs[:5], outputs[5:]
     copies, (list_ref, sem, in_sem) = scratch[:5], scratch[5:]
     moves = list(zip(inputs, copies)) + list(zip(index_inputs, index_outputs))
@@ -181,13 +182,15 @@
     for load in loads:
         load.start()
     nsrc_ref, ntgt_ref, spts_ref, area_ref, tpts_ref = copies
-    for load in loads[:5]:
+    for load in loads[:2]:
         load.wait()
     used = lax.broadcasted_iota(jnp.int32, nsrc_ref.shape, 1) < fill_ref[0, 0]
     ids = jnp.where(used, ntgt_ref[...] * column_leaves + nsrc_ref[...], -1)
     build_list(ids, list_ref, first_leaves(row_leaves) * column_leaves)
     copy = pltpu.make_async_copy(list_ref, table_ref, sem)
     copy.start()
+    for load in loads[2:5]:
+        load.wait()
 
     tx, ty, tz = (tpts_ref[i : i + 1, :] - 0.5 for i in range(3))
     norm = tx * tx + ty * ty + tz * tz
@@ -215,10 +218,8 @@
 
 
 def more_entries_kernel(table_ref, s_ref, t_ref, *entries_refs, first):
-    slots = table_ref.shape[1]
     last = first + 2 * entries_refs[0].shape[0]
-    low = jnp.clip(table_ref[3, 0], first, last) if last == slots else first
-    entry_loop(table_ref, s_ref, t_ref, entries_refs, first, low, jnp.clip(table_ref[2, 0], first, last), False)
+    entry_loop(table_ref, s_ref, t_ref, entries_refs, first, first, jnp.clip(table_ref[2, 0], first, last), False)
 
 
 VMEM = pl.BlockSpec(memory_space=pltpu.VMEM)
@@ -227,7 +228,7 @@
 
 
 def first_leaves(row_leaves):
-    return row_leaves * 5 // 8
+    return row_leaves * 9 // 16
 
 
 def first_count(slots):
@@ -238,17 +239,17 @@
     return max(slots // 8 // NEAR_TRIP, 1) * NEAR_TRIP
 
 
-def first_entries(near_fill, near_source, near_target, source_points, source_areas, target_points, indices, leaves):
+def first_entries(near_fill, near_source, near_target, source_points, source_areas, target_points, indices, bases, leaves):
     column_leaves, row_leaves = leaves
     slots = near_source.shape[1]
     leaf = source_points.shape[1] // column_leaves
     depth = 64
     inputs = (near_source, near_target, source_points, source_areas[None, :], target_points)
-    hbm_inputs = tuple(pltpu.with_memory_space_constraint(value, pltpu.HBM) for value in inputs + tuple(indices))
+    hbm_inputs = tuple(pltpu.with_memory_space_constraint(value, pltpu.HBM) for value in inputs + tuple(indices) + tuple(bases))
     return pl.pallas_call(
         functools.partial(
             first_entries_kernel, column_leaves=column_leaves, row_leaves=row_leaves, leaf=leaf,
-            indices=len(indices),
+            indices=len(indices), bases=len(bases),
         ),
         out_shape=(
             *[pltpu.VMEM((first_count(slots) // 2, leaf, leaf), BF16)] * 2,
@@ -256,9 +257,10 @@
             pltpu.VMEM((column_leaves, leaf, 128), BF16),
             pltpu.VMEM((row_leaves, depth, leaf), BF16),
         )
-        + tuple(pltpu.SMEM(value.shape, jnp.int32) for value in indices),
+        + tuple(pltpu.SMEM(value.shape, jnp.int32) for value in indices)
+        + tuple(pltpu.VMEM(value.shape, value.dtype) for value in bases),
         in_specs=[SMEM] + [HBM] * len(hbm_inputs),
-        out_specs=(VMEM, VMEM, SMEM, VMEM, VMEM) + (SMEM,) * len(indices),
+        out_specs=(VMEM, VMEM, SMEM, VMEM, VMEM) + (SMEM,) * len(indices) + (VMEM,) * len(bases),
         scratch_shapes=[pltpu.VMEM(value.shape, value.dtype) for value in inputs]
         + [pltpu.VMEM((8, slots), jnp.int32), pltpu.SemaphoreType.DMA, pltpu.SemaphoreType.DMA((len(hbm_inputs),))],
         compiler_params=pltpu.CompilerParams(vmem_limit_bytes=10 << 20),
@@ -418,7 +420,7 @@
         in_specs=[SMEM] * 2 + [VMEM] * (4 + len(made) + len(carried)),
         out_specs=(VMEM,) * len(out_shape),
         scratch_shapes=[pltpu.VMEM((rest, leaf, leaf), BF16)] * 2 + [pltpu.VMEM((len(leaves), rhs, leaf), F32)] * SUMS,
-        compiler_params=pltpu.CompilerParams(vmem_limit_bytes=(8 if complete else 24) << 20),
+        compiler_params=pltpu.CompilerParams(vmem_limit_bytes=20 << 20),
         cost_estimate=pl.CostEstimate(flops=4_000_000_000, bytes_accessed=8 << 20, transcendentals=0),
         name="near",
     )(table, target_fill, far, x, *features, *made, *carried)
@@ -440,11 +442,12 @@
     row_leaves, column_leaves = target_fill.shape[0], source_fill.shape[0]
     first_outs = first_entries(
         near_fill, near_source, near_target, source_points, source_areas, target_points,
-        (source_fill, target_fill, far_source, far_target, far_rank), (column_leaves, row_leaves),
+        (source_fill, target_fill, far_source, far_target, far_rank), (left_basis[0], right_basis[0]),
+        (column_leaves, row_leaves),
     )
     *entries, table, s_features, t_features = first_outs[:5]
     features = (s_features, t_features)
-    source_fill, target_fill, far_source, far_target, far_rank = first_outs[5:]
+    source_fill, target_fill, far_source, far_target, far_rank, left, right = first_outs[5:]
     if not plain:
         pieces, table = lax.optimization_barrier((pieces, table))
         pieces = pieces + [swap(piece, "row", rows, 1) for piece in pieces]
@@ -455,7 +458,7 @@
         pieces, more[0] = lax.optimization_barrier((pieces, more[0]))
     made = [(0, entries), (first, more)]
     x, far = far_field(
-        source_fill, row_leaves, far_source, far_target, far_rank, left_basis[0], right_basis[0], pieces, plain
+        source_fill, row_leaves, far_source, far_target, far_rank, left, right, pieces, plain
     )
     if plain or row_leaves < 2 or columns < 3:
         outs = near_field(table, target_fill, far, x, made, features, columns, plain, range(row_leaves))
@@ -470,20 +473,19 @@
         return swap(value, "col", columns, mask)
 
     split = first_leaves(row_leaves)
-    one = near_field(table, target_fill, far, x, made, features, columns, plain, range(split))
-    early = {mask: exchange(one[mask], mask) for mask in exchange_order(columns)}
-    table, one_last = lax.optimization_barrier((table, one[0]))
-    made = made + [(first + second, more_entries(table, *features, first + second, slots - first - second))]
-    two = near_field(table, target_fill, far, x, made, features, columns, plain, range(split, row_leaves))
-    late = {mask: exchange(two[mask], mask) for mask in exchange_order(columns)}
-    result = jnp.concatenate([one_last, two[0]], axis=1)
+    inputs = (table, target_fill, far, x, made, features, columns, plain)
+    one = near_field(*inputs, range(split))
+    early = {mask: exchange(one[mask], mask) for mask in far_masks(columns)}
+    two = near_field(*inputs, range(split, row_leaves), (one[1],), (1,))
+    late = {mask: exchange(two[mask], mask) for mask in far_masks(columns) + [1]}
+    result = jnp.concatenate([one[0], two[0]], axis=1) + late[1].astype(F32)
     for mask in early:
         result = result + jnp.concatenate([early[mask], late[mask]], axis=1).astype(F32)
     return result
 
 
-def exchange_order(columns):
-    return list(range(2, columns)) + [1]
+def far_masks(columns):
+    return list(range(2, columns))
 
 
 def solution(mesh):

time: 41.1 us -> 42.2 us (1.027)
  waiting for transfers between devices: 5.04 us -> 8.39 us
  starting transfers between devices: 13.5 us -> 11.5 us
  local copies, waits for them, and re-layouts: 0.44 us -> 0.01 us
    pallas_call x2, Pallas kernels: 6.65 us -> 10.1 us  [near_field(): pl.pallas_call(functools.partial(near_kernel, base_leaf=leaves[0], firsts...]
    ppermute x13 -> x12, waiting for transfers between devices: 5.04 us -> 8.39 us  [swap(): return lax.ppermute(value, axis, [(i, i ^ mask) for i in range(size)])]
    pallas_call x2 -> x1, Pallas kernels: 4.61 us -> 1.39 us  [more_entries(): pl.pallas_call(functools.partial(more_entries_kernel, first=first), out_s...]
    ppermute x13 -> x12, starting transfers between devices: 13.5 us -> 11.5 us  [swap(): return lax.ppermute(value, axis, [(i, i ^ mask) for i in range(size)])]
    unnamed x6 -> x2, local copies, waits for them, and re-layouts: 0.44 us -> 0.01 us
  transfers between devices with their start and end apart: 13 -> 12, of which waited for: 1 -> 1; matrix products, arithmetic and copies ran while one was open for 0% -> 0% of each run, Pallas kernels for 19% -> 18%
where the time goes in v5:
time: 42.2 us; the launch traced here: 41.9 us
  Pallas kernels  20.4 us (48%)
  starting transfers between devices  11.5 us (27%)
  waiting for transfers between devices  8.39 us (20%)
  between operations  0.8 us (2%)
  other arithmetic  0.77 us (2%)
    ppermute x12, starting transfers between devices, swap(): return lax.ppermute(value, axis, [(i, i ^ mask) for i in range(size)])  11.5 us
    pallas_call x2, Pallas kernels, near_field(): pl.pallas_call(functools.partial(near_kernel, base_leaf=leaves[0], firsts...  10.1 us
    ppermute x12, waiting for transfers between devices, swap(): return lax.ppermute(value, axis, [(i, i ^ mask) for i in range(size)])  8.39 us
    pallas_call x1, Pallas kernels, first_entries(): pl.pallas_call(functools.partial(first_entries_kernel, column_leaves=colu...  6.04 us
    pallas_call x1, Pallas kernels, far_field(): pl.pallas_call(functools.partial(far_kernel, pieces=len(pieces), plain=pl...  2.84 us
    pallas_call x1, Pallas kernels, more_entries(): pl.pallas_call(functools.partial(more_entries_kernel, first=first), out_s...  1.39 us
  transfers between devices with their start and end apart: 12, of which 1 were waited for; matrix products, arithmetic and copies ran while one was open for 0% of the time, Pallas kernels for 18%

profile of v5, /device:TPU:0, one launch (start us, length us, event | category | flops | bytes accessed | tf_op | source)
XLA Modules:
  0.0 41.9 jit_solution(4852421072591305504)
XLA Ops:
  0.0 3.0 %collective-permute-start.1 = (bf16[8,8192]{1,0:T(8,128)(2,1)}, bf16[8,8192]{1,0:T(8,128)(2,1)S(1)}, u32[]{:S(2)}, u32[]{:S(2)}) collective-permute-start(bf16[8,8192]{1,0:T(8,128)(2,1)} %refs_6_.2), channel_id=1, source_target_pairs={{0,16},{4,20},{8,24},{12,28},{16,0},{20,4},{24,8},{28,12},{1,17},{... | collective-permute-start | bytes 393224 | tf_op jit(solution)/shard_map/ppermute | solution.py:439
  3.0 1.5 %collective-permute-start = (bf16[8,8192]{1,0:T(8,128)(2,1)}, bf16[8,8192]{1,0:T(8,128)(2,1)S(1)}, u32[]{:S(2)}, u32[]{:S(2)}) collective-permute-start(bf16[8,8192]{1,0:T(8,128)(2,1)} %refs_6_.2), channel_id=1, source_target_pairs={{0,8},{4,12},{8,0},{12,4},{16,24},{20,28},{24,16},{28,20},{1,9},{5... | collective-permute-start | bytes 393224 | tf_op jit(solution)/shard_map/ppermute | solution.py:439
  4.5 0.0 collective-permute-start.2
  5.1 0.0 copy-start
  5.2 6.0 %entries.1 = (bf16[48,256,256]{2,1,0:T(8,128)(2,1)S(1)}, bf16[48,256,256]{2,1,0:T(8,128)(2,1)S(1)}, s32[8,256]{1,0:T(8,128)S(4)}, bf16[32,256,128]{2,1,0:T(8,128...) custom-call(s32[1,1]{1,0:T(1,128)S(6)} %copy.15.refs_0_, ...), custom_call_target="tpu_custom_call" | custom-call | flops 8000000000 | bytes 1048576 | tf_op jit(solution)/shard_map/entries/pallas_call | solution.py:249
  11.2 0.0 collective-permute-done.1.refs_8_
  11.2 0.0 collective-permute-done.refs_7_
  11.2 0.0 collective-permute-done.2.refs_9_
  11.2 0.0 copy-done
  11.2 0.1 collective-permute-start.3
  11.3 0.5 %collective-permute-start.4 = (bf16[8,8192]{1,0:T(8,128)(2,1)S(1)}, bf16[8,8192]{1,0:T(8,128)(2,1)S(1)}, u32[]{:S(2)}, u32[]{:S(2)}) collective-permute-start(bf16[8,8192]{1,0:T(8,128)(2,1)S(1)} %collective-permute-done.refs_7_), channel_id=1, source_target_pairs={{0,4},{4,0},{8,12},{12,8},{16,20},{20,16},{24,28},{28,24},{1,5},{5... | collective-permute-start | bytes 393224 | tf_op jit(solution)/shard_map/ppermute | solution.py:439
  11.8 0.1 collective-permute-start.5
  11.9 0.4 %collective-permute-start.6 = (bf16[8,8192]{1,0:T(8,128)(2,1)S(1)}, bf16[8,8192]{1,0:T(8,128)(2,1)S(1)}, u32[]{:S(2)}, u32[]{:S(2)}) collective-permute-start(bf16[8,8192]{1,0:T(8,128)(2,1)S(1)} %collective-permute-done.2.refs_9_), channel_id=1, source_target_pairs={{0,4},{4,0},{8,12},{12,8},{16,20},{20,16},{24,28},{28,24},{1,5},{5... | collective-permute-start | bytes 393224 | tf_op jit(solution)/shard_map/ppermute | solution.py:439
  12.3 1.4 %entries_rest.1 = (bf16[16,256,256]{2,1,0:T(8,128)(2,1)S(1)}, bf16[16,256,256]{2,1,0:T(8,128)(2,1)S(1)}) custom-call(s32[8,256]{1,0:T(8,128)S(4)} %get-tuple-element.44.table_ref.refs_0_, bf16[32,256,128]{2,1,0:T(8,128)(2,1)S(1)} %get-tuple-element.56.s_ref.refs_4_, bf16[16,64,256]{2,1,0:T(8,128)(2,1)S(1)} %get-tuple-element.57.t_ref.refs_5_), custom_call_target="tpu_custom_call" | custom-call | flops 8000000000 | bytes 1048576 | tf_op jit(solution)/shard_map/entries_rest/pallas_call | solution.py:274
  13.7 0.0 collective-permute-done.3.refs_10_
  13.7 0.0 collective-permute-done.4.refs_11_
  13.7 0.0 collective-permute-done.5.refs_12_
  13.8 0.0 collective-permute-done.6.refs_13_
  13.8 2.8 %far.1 = (bf16[32,64,256]{2,1,0:T(8,128)(2,1)S(1)}, f32[16,64,256]{2,1,0:T(8,128)S(1)}) custom-call(s32[32]{0:T(128)S(4)} %get-tuple-element.46.refs_0_, s32[1,96]{1,0:T(1,128)S(4)} %get-tuple-element.47.refs_1_, s32[1,96]{1,0:T(1,128)S(4)} %get-tuple-element.48.refs_2_, s32[1,96]{1,0:T(1,128)S(4)} %get-tuple-element.49.refs_3_, ...), custom_call_target="tpu_custom_call" | custom-call | flops 2000000000 | bytes 8388608 | tf_op jit(solution)/shard_map/far/pallas_call | solution.py:385
  16.6 3.6 %near.2 = (f32[16,2304]{1,0:T(8,128)S(1)}, bf16[16,2304]{1,0:T(8,128)(2,1)S(1)}, bf16[16,2304]{1,0:T(8,128)(2,1)S(1)}, bf16[16,2304]{1,0:T(8,128)(2,1)S(1)}) custom-call(s32[8,256]{1,0:T(8,128)S(4)} %get-tuple-element.44.table_ref.refs_0_, s32[16]{0:T(128)S(4)} %get-tuple-element.45.refs_1_, f32[16,64,256]{2,1,0:T(8,128)S(1)} %get-tuple-element.67.refs_2_, ...), custom_call_target="tpu_custom_call" | custom-call | flops 4000000000 | bytes 8388608 | tf_op jit(solution)/shard_map/near/pallas_call | solution.py:414
  20.2 6.6 %near.3 = (f32[16,1792]{1,0:T(8,128)S(1)}, bf16[16,4096]{1,0:T(8,128)(2,1)S(1)}, bf16[16,1792]{1,0:T(8,128)(2,1)S(1)}, bf16[16,1792]{1,0:T(8,128)(2,1)S(1)}) custom-call(s32[8,256]{1,0:T(8,128)S(4)} %get-tuple-element.44.table_ref.refs_0_, s32[16]{0:T(128)S(4)} %get-tuple-element.45.refs_1_, f32[16,64,256]{2,1,0:T(8,128)S(1)} %get-tuple-element.67.refs_2_, ...), custom_call_target="tpu_custom_call" | custom-call | flops 4000000000 | bytes 8388608 | tf_op jit(solution)/shard_map/near/pallas_call | solution.py:414
  26.8 0.1 collective-permute-start.7
  26.9 0.1 collective-permute-start.8
  26.9 4.3 %collective-permute-start.10 = (bf16[16,2304]{1,0:T(8,128)(2,1)S(1)}, bf16[16,2304]{1,0:T(8,128)(2,1)S(1)}, u32[]{:S(2)}, u32[]{:S(2)}) collective-permute-start(bf16[16,2304]{1,0:T(8,128)(2,1)S(1)} %get-tuple-element.79), channel_id=1, source_target_pairs={{0,3},{1,2},{2,1},{3,0},{4,7},{5,6},{6,5},{7,4},{8,11},{9,10},{10,... | collective-permute-start | bytes 221192 | tf_op jit(solution)/shard_map/ppermute | solution.py:439
  31.2 0.0 collective-permute-start.9
  31.2 1.5 %collective-permute-start.11 = (bf16[16,1792]{1,0:T(8,128)(2,1)S(1)}, bf16[16,1792]{1,0:T(8,128)(2,1)S(1)}, u32[]{:S(2)}, u32[]{:S(2)}) collective-permute-start(bf16[16,1792]{1,0:T(8,128)(2,1)S(1)} %get-tuple-element.80), channel_id=1, source_target_pairs={{0,3},{1,2},{2,1},{3,0},{4,7},{5,6},{6,5},{7,4},{8,11},{9,10},{10,... | collective-permute-start | bytes 172040 | tf_op jit(solution)/shard_map/ppermute | solution.py:439
  32.8 8.4 %collective-permute-done.9 = bf16[16,1792]{1,0:T(8,128)(2,1)S(1)} collective-permute-done((bf16[16,1792]{1,0:T(8,128)(2,1)S(1)}, bf16[16,1792]{1,0:T(8,128)(2,1)S(1)}, u32[]{:S(2)}, u32[]{:S(2)}) %collective-permute-start.9) | collective-permute-done | bytes 57376 | tf_op jit(solution)/shard_map/ppermute | solution.py:439
  41.1 0.0 collective-permute-done.11
  41.1 0.0 collective-permute-done.8
  41.1 0.0 collective-permute-done.10
  41.1 0.0 collective-permute-done.7
  41.1 0.8 %fusion.1 = f32[16,4096]{1,0:T(8,128)} fusion(f32[16,1792]{1,0:T(8,128)S(1)} %get-tuple-element.75, f32[16,2304]{1,0:T(8,128)S(1)} %get-tuple-element.73, bf16[16,4096]{1,0:T(8,128)(2,1)S(1)} %collective-permute-done.7, bf16[16,1792]{1,0:T(8,128)(2,1)S(1)} %collective-permute-done.9, bf16[16,2304]{1,0:T(8,128)(2,1)S(1)} %collective-permute-done.8, ...), kind=kLoop, calls=%fused_computation.2 | loop fusion | flops 851968 | bytes 917504 | tf_op jit(solution)/shard_map/add | solution.py:483
Async XLA Ops:
  0.0 11.2 %collective-permute-start.1 = (bf16[8,8192]{1,0:T(8,128)(2,1)}, bf16[8,8192]{1,0:T(8,128)(2,1)S(1)}, u32[]{:S(2)}, u32[]{:S(2)}) collective-permute-start(bf16[8,8192]{1,0:T(8,128)(2,1)} %refs_6_.2), channel_id=1, source_target_pairs={{0,16},{4,20},{8,24},{12,28},{16,0},{20,4},{24,8},{28,12},{1,17},{... | collective-permute-start | bytes 393224 | tf_op jit(solution)/shard_map/ppermute | solution.py:439
  3.0 8.2 %collective-permute-start = (bf16[8,8192]{1,0:T(8,128)(2,1)}, bf16[8,8192]{1,0:T(8,128)(2,1)S(1)}, u32[]{:S(2)}, u32[]{:S(2)}) collective-permute-start(bf16[8,8192]{1,0:T(8,128)(2,1)} %refs_6_.2), channel_id=1, source_target_pairs={{0,8},{4,12},{8,0},{12,4},{16,24},{20,28},{24,16},{28,20},{1,9},{5... | collective-permute-start | bytes 393224 | tf_op jit(solution)/shard_map/ppermute | solution.py:439
  4.5 6.7 %collective-permute-start.2 = (bf16[8,8192]{1,0:T(8,128)(2,1)}, bf16[8,8192]{1,0:T(8,128)(2,1)S(1)}, u32[]{:S(2)}, u32[]{:S(2)}) collective-permute-start(bf16[8,8192]{1,0:T(8,128)(2,1)} %refs_6_.2), channel_id=1, source_target_pairs={{0,24},{4,28},{8,16},{12,20},{16,8},{20,12},{24,0},{28,4},{1,25},{... | collective-permute-start | bytes 393224 | tf_op jit(solution)/shard_map/ppermute | solution.py:439
  5.1 6.1 %copy-start = (bf16[8,8192]{1,0:T(8,128)(2,1)S(1)}, bf16[8,8192]{1,0:T(8,128)(2,1)}, u32[]{:S(2)}) copy-start(bf16[8,8192]{1,0:T(8,128)(2,1)} %refs_6_.2) | copy-start | bytes 393220
  11.2 2.5 %collective-permute-start.3 = (bf16[8,8192]{1,0:T(8,128)(2,1)S(1)}, bf16[8,8192]{1,0:T(8,128)(2,1)S(1)}, u32[]{:S(2)}, u32[]{:S(2)}) collective-permute-start(bf16[8,8192]{1,0:T(8,128)(2,1)S(1)} %copy-done), channel_id=1, source_target_pairs={{0,4},{4,0},{8,12},{12,8},{16,20},{20,16},{24,28},{28,24},{1,5},{5... | collective-permute-start | bytes 393224 | tf_op jit(solution)/shard_map/ppermute | solution.py:439
  11.3 2.4 %collective-permute-start.4 = (bf16[8,8192]{1,0:T(8,128)(2,1)S(1)}, bf16[8,8192]{1,0:T(8,128)(2,1)S(1)}, u32[]{:S(2)}, u32[]{:S(2)}) collective-permute-start(bf16[8,8192]{1,0:T(8,128)(2,1)S(1)} %collective-permute-done.refs_7_), channel_id=1, source_target_pairs={{0,4},{4,0},{8,12},{12,8},{16,20},{20,16},{24,28},{28,24},{1,5},{5... | collective-permute-start | bytes 393224 | tf_op jit(solution)/shard_map/ppermute | solution.py:439
  11.8 1.9 %collective-permute-start.5 = (bf16[8,8192]{1,0:T(8,128)(2,1)S(1)}, bf16[8,8192]{1,0:T(8,128)(2,1)S(1)}, u32[]{:S(2)}, u32[]{:S(2)}) collective-permute-start(bf16[8,8192]{1,0:T(8,128)(2,1)S(1)} %collective-permute-done.1.refs_8_), channel_id=1, source_target_pairs={{0,4},{4,0},{8,12},{12,8},{16,20},{20,16},{24,28},{28,24},{1,5},{5... | collective-permute-start | bytes 393224 | tf_op jit(solution)/shard_map/ppermute | solution.py:439
  11.9 1.9 %collective-permute-start.6 = (bf16[8,8192]{1,0:T(8,128)(2,1)S(1)}, bf16[8,8192]{1,0:T(8,128)(2,1)S(1)}, u32[]{:S(2)}, u32[]{:S(2)}) collective-permute-start(bf16[8,8192]{1,0:T(8,128)(2,1)S(1)} %collective-permute-done.2.refs_9_), channel_id=1, source_target_pairs={{0,4},{4,0},{8,12},{12,8},{16,20},{20,16},{24,28},{28,24},{1,5},{5... | collective-permute-start | bytes 393224 | tf_op jit(solution)/shard_map/ppermute | solution.py:439
  26.8 14.4 %collective-permute-start.7 = (bf16[16,4096]{1,0:T(8,128)(2,1)S(1)}, bf16[16,4096]{1,0:T(8,128)(2,1)S(1)}, u32[]{:S(2)}, u32[]{:S(2)}) collective-permute-start(bf16[16,4096]{1,0:T(8,128)(2,1)S(1)} %get-tuple-element.76), channel_id=1, source_target_pairs={{0,1},{1,0},{2,3},{3,2},{4,5},{5,4},{6,7},{7,6},{8,9},{9,8},{10,11... | collective-permute-start | bytes 393224 | tf_op jit(solution)/shard_map/ppermute | solution.py:439
  26.9 14.3 %collective-permute-start.8 = (bf16[16,2304]{1,0:T(8,128)(2,1)S(1)}, bf16[16,2304]{1,0:T(8,128)(2,1)S(1)}, u32[]{:S(2)}, u32[]{:S(2)}) collective-permute-start(bf16[16,2304]{1,0:T(8,128)(2,1)S(1)} %get-tuple-element.77), channel_id=1, source_target_pairs={{0,2},{1,3},{2,0},{3,1},{4,6},{5,7},{6,4},{7,5},{8,10},{9,11},{10,... | collective-permute-start | bytes 221192 | tf_op jit(solution)/shard_map/ppermute | solution.py:439
  26.9 14.2 %collective-permute-start.10 = (bf16[16,2304]{1,0:T(8,128)(2,1)S(1)}, bf16[16,2304]{1,0:T(8,128)(2,1)S(1)}, u32[]{:S(2)}, u32[]{:S(2)}) collective-permute-start(bf16[16,2304]{1,0:T(8,128)(2,1)S(1)} %get-tuple-element.79), channel_id=1, source_target_pairs={{0,3},{1,2},{2,1},{3,0},{4,7},{5,6},{6,5},{7,4},{8,11},{9,10},{10,... | collective-permute-start | bytes 221192 | tf_op jit(solution)/shard_map/ppermute | solution.py:439
  31.2 9.9 %collective-permute-start.9 = (bf16[16,1792]{1,0:T(8,128)(2,1)S(1)}, bf16[16,1792]{1,0:T(8,128)(2,1)S(1)}, u32[]{:S(2)}, u32[]{:S(2)}) collective-permute-start(bf16[16,1792]{1,0:T(8,128)(2,1)S(1)} %get-tuple-element.78), channel_id=1, source_target_pairs={{0,2},{1,3},{2,0},{3,1},{4,6},{5,7},{6,4},{7,5},{8,10},{9,11},{10,... | collective-permute-start | bytes 172040 | tf_op jit(solution)/shard_map/ppermute | solution.py:439
  31.2 9.9 %collective-permute-start.11 = (bf16[16,1792]{1,0:T(8,128)(2,1)S(1)}, bf16[16,1792]{1,0:T(8,128)(2,1)S(1)}, u32[]{:S(2)}, u32[]{:S(2)}) collective-permute-start(bf16[16,1792]{1,0:T(8,128)(2,1)S(1)} %get-tuple-element.80), channel_id=1, source_target_pairs={{0,3},{1,2},{2,1},{3,0},{4,7},{5,6},{6,5},{7,4},{8,11},{9,10},{10,... | collective-permute-start | bytes 172040 | tf_op jit(solution)/shard_map/ppermute | solution.py:439

commit v6 on v5

--- a/solution.py
+++ b/solution.py
@@ -13,7 +13,7 @@
 F32 = jnp.float32
 BF16 = jnp.bfloat16
 ENTRY_TRIP = 16
-SUMS = 2
+SUMS = 1
 NEAR_TRIP = 16
 
 
@@ -133,42 +133,27 @@
         @pl.when(high > low)
         def _():
             for *entries_refs, base in entries:
-                rows = entries_refs[0].shape[0]
-                end = base + 2 * rows
+                end = base + 2 * entries_refs[0].shape[0]
                 start = jnp.clip(low, base, end) // NEAR_TRIP
                 stop = (jnp.clip(high, base, end) + NEAR_TRIP - 1) // NEAR_TRIP
 
-                def push(row, u):
-                    pltpu.matmul_push_rhs(
-                        entries_refs[u % 2][jnp.minimum(row, rows - 1)], staging_register=(u // 2) % 2, mxu_index=u % 2
-                    )
-
-                @pl.when(stop > start)
-                def _():
-                    for u in range(2):
-                        push(start * (NEAR_TRIP // 2) - base // 2, u)
-
-                    @pl.loop(start, stop)
-                    def _(turn):
-                        for u in range(NEAR_TRIP):
-                            k = turn * NEAR_TRIP + u
-                            row = turn * (NEAR_TRIP // 2) - base // 2 + u // 2
-                            source = table_ref[0, k] % column_leaves
-                            pltpu.matmul_acc_lhs(accs[u % 16], x_ref[source], load_staged_rhs=(u // 2) % 2)
-                            push(row + 1, u + 2)
-                            drain((u + 8) % 16, k - 8)
-
-                    for u in range(2):
-                        pltpu.matmul_acc_lhs(accs[16 + u], jnp.zeros((16, leaf), BF16), load_staged_rhs=0)
-                        pltpu.matmul_pop(accs[16 + u])
+                @pl.loop(start, stop)
+                def _(turn):
+                    for u in range(NEAR_TRIP):
+                        k = turn * NEAR_TRIP + u
+                        source = table_ref[0, k] % column_leaves
+                        row = turn * (NEAR_TRIP // 2) - base // 2 + u // 2
+                        stage = (u // 2) % 2
+                        pltpu.matmul_push_rhs(entries_refs[u % 2][row], staging_register=stage, mxu_index=u % 2)
+                        pltpu.matmul_acc_lhs(accs[u % 16], x_ref[source], load_staged_rhs=stage)
+                        drain((u + 8) % 16, k - 8)
 
             end = (high + NEAR_TRIP - 1) // NEAR_TRIP * NEAR_TRIP
             for u in range(8):
                 drain(u + 8, end - 8 + u)
 
     spare = pltpu.ACC(0)((rhs, leaf), F32), pltpu.ACC(1)((rhs, leaf), F32)
-    flush = pltpu.ACC(0)((16, leaf), F32), pltpu.ACC(1)((16, leaf), F32)
-    pl.run_scoped(work, *(spare * 8), *flush, *(spare * 7 if fresh else ()))
+    pl.run_scoped(work, *(spare * (16 if fresh else 8)))
 
 
 def first_entries_kernel(*refs, column_leaves, row_leaves, leaf, indices, bases):

time: 42.2 us -> 41.9 us (level)
  no operation moved by 1% of the time
where the time goes in v6:
time: 41.9 us; the launch traced here: 41.6 us
  Pallas kernels  20.1 us (48%)
  starting transfers between devices  11.5 us (27%)
  waiting for transfers between devices  8.38 us (20%)
  between operations  0.8 us (2%)
  other arithmetic  0.77 us (2%)
    ppermute x12, starting transfers between devices, swap(): return lax.ppermute(value, axis, [(i, i ^ mask) for i in range(size)])  11.5 us
    pallas_call x2, Pallas kernels, near_field(): pl.pallas_call(functools.partial(near_kernel, base_leaf=leaves[0], firsts...  9.86 us
    ppermute x12, waiting for transfers between devices, swap(): return lax.ppermute(value, axis, [(i, i ^ mask) for i in range(size)])  8.38 us
    pallas_call x1, Pallas kernels, first_entries(): pl.pallas_call(functools.partial(first_entries_kernel, column_leaves=colu...  6.04 us
    pallas_call x1, Pallas kernels, far_field(): pl.pallas_call(functools.partial(far_kernel, pieces=len(pieces), plain=pl...  2.84 us
    pallas_call x1, Pallas kernels, more_entries(): pl.pallas_call(functools.partial(more_entries_kernel, first=first), out_s...  1.39 us
  transfers between devices with their start and end apart: 12, of which 1 were waited for; matrix products, arithmetic and copies ran while one was open for 0% of the time, Pallas kernels for 18%

profile of v6, /device:TPU:0, one launch (start us, length us, event | category | flops | bytes accessed | tf_op | source)
XLA Modules:
  0.0 41.6 jit_solution(13817366534464168411)
XLA Ops:
  0.0 3.0 %collective-permute-start.1 = (bf16[8,8192]{1,0:T(8,128)(2,1)}, bf16[8,8192]{1,0:T(8,128)(2,1)S(1)}, u32[]{:S(2)}, u32[]{:S(2)}) collective-permute-start(bf16[8,8192]{1,0:T(8,128)(2,1)} %refs_6_.2), channel_id=1, source_target_pairs={{0,16},{4,20},{8,24},{12,28},{16,0},{20,4},{24,8},{28,12},{1,17},{... | collective-permute-start | bytes 393224 | tf_op jit(solution)/shard_map/ppermute | solution.py:424
  3.0 1.5 %collective-permute-start = (bf16[8,8192]{1,0:T(8,128)(2,1)}, bf16[8,8192]{1,0:T(8,128)(2,1)S(1)}, u32[]{:S(2)}, u32[]{:S(2)}) collective-permute-start(bf16[8,8192]{1,0:T(8,128)(2,1)} %refs_6_.2), channel_id=1, source_target_pairs={{0,8},{4,12},{8,0},{12,4},{16,24},{20,28},{24,16},{28,20},{1,9},{5... | collective-permute-start | bytes 393224 | tf_op jit(solution)/shard_map/ppermute | solution.py:424
  4.5 0.0 collective-permute-start.2
  5.1 0.0 copy-start
  5.2 6.0 %entries.1 = (bf16[48,256,256]{2,1,0:T(8,128)(2,1)S(1)}, bf16[48,256,256]{2,1,0:T(8,128)(2,1)S(1)}, s32[8,256]{1,0:T(8,128)S(4)}, bf16[32,256,128]{2,1,0:T(8,128...) custom-call(s32[1,1]{1,0:T(1,128)S(6)} %copy.15.refs_0_, ...), custom_call_target="tpu_custom_call" | custom-call | flops 8000000000 | bytes 1048576 | tf_op jit(solution)/shard_map/entries/pallas_call | solution.py:234
  11.2 0.0 collective-permute-done.1.refs_8_
  11.2 0.0 collective-permute-done.refs_7_
  11.2 0.0 collective-permute-done.2.refs_9_
  11.2 0.0 copy-done
  11.2 0.1 collective-permute-start.3
  11.3 0.5 %collective-permute-start.4 = (bf16[8,8192]{1,0:T(8,128)(2,1)S(1)}, bf16[8,8192]{1,0:T(8,128)(2,1)S(1)}, u32[]{:S(2)}, u32[]{:S(2)}) collective-permute-start(bf16[8,8192]{1,0:T(8,128)(2,1)S(1)} %collective-permute-done.refs_7_), channel_id=1, source_target_pairs={{0,4},{4,0},{8,12},{12,8},{16,20},{20,16},{24,28},{28,24},{1,5},{5... | collective-permute-start | bytes 393224 | tf_op jit(solution)/shard_map/ppermute | solution.py:424
  11.8 0.1 collective-permute-start.5
  11.9 0.4 %collective-permute-start.6 = (bf16[8,8192]{1,0:T(8,128)(2,1)S(1)}, bf16[8,8192]{1,0:T(8,128)(2,1)S(1)}, u32[]{:S(2)}, u32[]{:S(2)}) collective-permute-start(bf16[8,8192]{1,0:T(8,128)(2,1)S(1)} %collective-permute-done.2.refs_9_), channel_id=1, source_target_pairs={{0,4},{4,0},{8,12},{12,8},{16,20},{20,16},{24,28},{28,24},{1,5},{5... | collective-permute-start | bytes 393224 | tf_op jit(solution)/shard_map/ppermute | solution.py:424
  12.3 1.4 %entries_rest.1 = (bf16[16,256,256]{2,1,0:T(8,128)(2,1)S(1)}, bf16[16,256,256]{2,1,0:T(8,128)(2,1)S(1)}) custom-call(s32[8,256]{1,0:T(8,128)S(4)} %get-tuple-element.44.table_ref.refs_0_, bf16[32,256,128]{2,1,0:T(8,128)(2,1)S(1)} %get-tuple-element.56.s_ref.refs_4_, bf16[16,64,256]{2,1,0:T(8,128)(2,1)S(1)} %get-tuple-element.57.t_ref.refs_5_), custom_call_target="tpu_custom_call" | custom-call | flops 8000000000 | bytes 1048576 | tf_op jit(solution)/shard_map/entries_rest/pallas_call | solution.py:259
  13.7 0.0 collective-permute-done.3.refs_10_
  13.7 0.0 collective-permute-done.4.refs_11_
  13.7 0.0 collective-permute-done.5.refs_12_
  13.8 0.0 collective-permute-done.6.refs_13_
  13.8 2.8 %far.1 = (bf16[32,64,256]{2,1,0:T(8,128)(2,1)S(1)}, f32[16,64,256]{2,1,0:T(8,128)S(1)}) custom-call(s32[32]{0:T(128)S(4)} %get-tuple-element.46.refs_0_, s32[1,96]{1,0:T(1,128)S(4)} %get-tuple-element.47.refs_1_, s32[1,96]{1,0:T(1,128)S(4)} %get-tuple-element.48.refs_2_, s32[1,96]{1,0:T(1,128)S(4)} %get-tuple-element.49.refs_3_, ...), custom_call_target="tpu_custom_call" | custom-call | flops 2000000000 | bytes 8388608 | tf_op jit(solution)/shard_map/far/pallas_call | solution.py:370
  16.6 3.3 %near.2 = (f32[16,2304]{1,0:T(8,128)S(1)}, bf16[16,2304]{1,0:T(8,128)(2,1)S(1)}, bf16[16,2304]{1,0:T(8,128)(2,1)S(1)}, bf16[16,2304]{1,0:T(8,128)(2,1)S(1)}) custom-call(s32[8,256]{1,0:T(8,128)S(4)} %get-tuple-element.44.table_ref.refs_0_, s32[16]{0:T(128)S(4)} %get-tuple-element.45.refs_1_, f32[16,64,256]{2,1,0:T(8,128)S(1)} %get-tuple-element.67.refs_2_, ...), custom_call_target="tpu_custom_call" | custom-call | flops 4000000000 | bytes 8388608 | tf_op jit(solution)/shard_map/near/pallas_call | solution.py:399
  20.0 6.5 %near.3 = (f32[16,1792]{1,0:T(8,128)S(1)}, bf16[16,4096]{1,0:T(8,128)(2,1)S(1)}, bf16[16,1792]{1,0:T(8,128)(2,1)S(1)}, bf16[16,1792]{1,0:T(8,128)(2,1)S(1)}) custom-call(s32[8,256]{1,0:T(8,128)S(4)} %get-tuple-element.44.table_ref.refs_0_, s32[16]{0:T(128)S(4)} %get-tuple-element.45.refs_1_, f32[16,64,256]{2,1,0:T(8,128)S(1)} %get-tuple-element.67.refs_2_, ...), custom_call_target="tpu_custom_call" | custom-call | flops 4000000000 | bytes 8388608 | tf_op jit(solution)/shard_map/near/pallas_call | solution.py:399
  26.5 0.1 collective-permute-start.7
  26.6 0.1 collective-permute-start.8
  26.6 4.3 %collective-permute-start.10 = (bf16[16,2304]{1,0:T(8,128)(2,1)S(1)}, bf16[16,2304]{1,0:T(8,128)(2,1)S(1)}, u32[]{:S(2)}, u32[]{:S(2)}) collective-permute-start(bf16[16,2304]{1,0:T(8,128)(2,1)S(1)} %get-tuple-element.79), channel_id=1, source_target_pairs={{0,3},{1,2},{2,1},{3,0},{4,7},{5,6},{6,5},{7,4},{8,11},{9,10},{10,... | collective-permute-start | bytes 221192 | tf_op jit(solution)/shard_map/ppermute | solution.py:424
  30.9 0.0 collective-permute-start.9
  30.9 1.5 %collective-permute-start.11 = (bf16[16,1792]{1,0:T(8,128)(2,1)S(1)}, bf16[16,1792]{1,0:T(8,128)(2,1)S(1)}, u32[]{:S(2)}, u32[]{:S(2)}) collective-permute-start(bf16[16,1792]{1,0:T(8,128)(2,1)S(1)} %get-tuple-element.80), channel_id=1, source_target_pairs={{0,3},{1,2},{2,1},{3,0},{4,7},{5,6},{6,5},{7,4},{8,11},{9,10},{10,... | collective-permute-start | bytes 172040 | tf_op jit(solution)/shard_map/ppermute | solution.py:424
  32.5 8.4 %collective-permute-done.9 = bf16[16,1792]{1,0:T(8,128)(2,1)S(1)} collective-permute-done((bf16[16,1792]{1,0:T(8,128)(2,1)S(1)}, bf16[16,1792]{1,0:T(8,128)(2,1)S(1)}, u32[]{:S(2)}, u32[]{:S(2)}) %collective-permute-start.9) | collective-permute-done | bytes 57376 | tf_op jit(solution)/shard_map/ppermute | solution.py:424
  40.8 0.0 collective-permute-done.11
  40.8 0.0 collective-permute-done.8
  40.8 0.0 collective-permute-done.10
  40.8 0.0 collective-permute-done.7
  40.9 0.8 %fusion.1 = f32[16,4096]{1,0:T(8,128)} fusion(f32[16,1792]{1,0:T(8,128)S(1)} %get-tuple-element.75, f32[16,2304]{1,0:T(8,128)S(1)} %get-tuple-element.73, bf16[16,4096]{1,0:T(8,128)(2,1)S(1)} %collective-permute-done.7, bf16[16,1792]{1,0:T(8,128)(2,1)S(1)} %collective-permute-done.9, bf16[16,2304]{1,0:T(8,128)(2,1)S(1)} %collective-permute-done.8, ...), kind=kLoop, calls=%fused_computation.2 | loop fusion | flops 851968 | bytes 917504 | tf_op jit(solution)/shard_map/add | solution.py:468
Async XLA Ops:
  0.0 11.2 %collective-permute-start.1 = (bf16[8,8192]{1,0:T(8,128)(2,1)}, bf16[8,8192]{1,0:T(8,128)(2,1)S(1)}, u32[]{:S(2)}, u32[]{:S(2)}) collective-permute-start(bf16[8,8192]{1,0:T(8,128)(2,1)} %refs_6_.2), channel_id=1, source_target_pairs={{0,16},{4,20},{8,24},{12,28},{16,0},{20,4},{24,8},{28,12},{1,17},{... | collective-permute-start | bytes 393224 | tf_op jit(solution)/shard_map/ppermute | solution.py:424
  3.0 8.2 %collective-permute-start = (bf16[8,8192]{1,0:T(8,128)(2,1)}, bf16[8,8192]{1,0:T(8,128)(2,1)S(1)}, u32[]{:S(2)}, u32[]{:S(2)}) collective-permute-start(bf16[8,8192]{1,0:T(8,128)(2,1)} %refs_6_.2), channel_id=1, source_target_pairs={{0,8},{4,12},{8,0},{12,4},{16,24},{20,28},{24,16},{28,20},{1,9},{5... | collective-permute-start | bytes 393224 | tf_op jit(solution)/shard_map/ppermute | solution.py:424
  4.5 6.7 %collective-permute-start.2 = (bf16[8,8192]{1,0:T(8,128)(2,1)}, bf16[8,8192]{1,0:T(8,128)(2,1)S(1)}, u32[]{:S(2)}, u32[]{:S(2)}) collective-permute-start(bf16[8,8192]{1,0:T(8,128)(2,1)} %refs_6_.2), channel_id=1, source_target_pairs={{0,24},{4,28},{8,16},{12,20},{16,8},{20,12},{24,0},{28,4},{1,25},{... | collective-permute-start | bytes 393224 | tf_op jit(solution)/shard_map/ppermute | solution.py:424
  5.1 6.1 %copy-start = (bf16[8,8192]{1,0:T(8,128)(2,1)S(1)}, bf16[8,8192]{1,0:T(8,128)(2,1)}, u32[]{:S(2)}) copy-start(bf16[8,8192]{1,0:T(8,128)(2,1)} %refs_6_.2) | copy-start | bytes 393220
  11.2 2.5 %collective-permute-start.3 = (bf16[8,8192]{1,0:T(8,128)(2,1)S(1)}, bf16[8,8192]{1,0:T(8,128)(2,1)S(1)}, u32[]{:S(2)}, u32[]{:S(2)}) collective-permute-start(bf16[8,8192]{1,0:T(8,128)(2,1)S(1)} %copy-done), channel_id=1, source_target_pairs={{0,4},{4,0},{8,12},{12,8},{16,20},{20,16},{24,28},{28,24},{1,5},{5... | collective-permute-start | bytes 393224 | tf_op jit(solution)/shard_map/ppermute | solution.py:424
  11.3 2.4 %collective-permute-start.4 = (bf16[8,8192]{1,0:T(8,128)(2,1)S(1)}, bf16[8,8192]{1,0:T(8,128)(2,1)S(1)}, u32[]{:S(2)}, u32[]{:S(2)}) collective-permute-start(bf16[8,8192]{1,0:T(8,128)(2,1)S(1)} %collective-permute-done.refs_7_), channel_id=1, source_target_pairs={{0,4},{4,0},{8,12},{12,8},{16,20},{20,16},{24,28},{28,24},{1,5},{5... | collective-permute-start | bytes 393224 | tf_op jit(solution)/shard_map/ppermute | solution.py:424
  11.8 1.9 %collective-permute-start.5 = (bf16[8,8192]{1,0:T(8,128)(2,1)S(1)}, bf16[8,8192]{1,0:T(8,128)(2,1)S(1)}, u32[]{:S(2)}, u32[]{:S(2)}) collective-permute-start(bf16[8,8192]{1,0:T(8,128)(2,1)S(1)} %collective-permute-done.1.refs_8_), channel_id=1, source_target_pairs={{0,4},{4,0},{8,12},{12,8},{16,20},{20,16},{24,28},{28,24},{1,5},{5... | collective-permute-start | bytes 393224 | tf_op jit(solution)/shard_map/ppermute | solution.py:424
  11.9 1.9 %collective-permute-start.6 = (bf16[8,8192]{1,0:T(8,128)(2,1)S(1)}, bf16[8,8192]{1,0:T(8,128)(2,1)S(1)}, u32[]{:S(2)}, u32[]{:S(2)}) collective-permute-start(bf16[8,8192]{1,0:T(8,128)(2,1)S(1)} %collective-permute-done.2.refs_9_), channel_id=1, source_target_pairs={{0,4},{4,0},{8,12},{12,8},{16,20},{20,16},{24,28},{28,24},{1,5},{5... | collective-permute-start | bytes 393224 | tf_op jit(solution)/shard_map/ppermute | solution.py:424
  26.5 14.4 %collective-permute-start.7 = (bf16[16,4096]{1,0:T(8,128)(2,1)S(1)}, bf16[16,4096]{1,0:T(8,128)(2,1)S(1)}, u32[]{:S(2)}, u32[]{:S(2)}) collective-permute-start(bf16[16,4096]{1,0:T(8,128)(2,1)S(1)} %get-tuple-element.76), channel_id=1, source_target_pairs={{0,1},{1,0},{2,3},{3,2},{4,5},{5,4},{6,7},{7,6},{8,9},{9,8},{10,11... | collective-permute-start | bytes 393224 | tf_op jit(solution)/shard_map/ppermute | solution.py:424
  26.6 14.3 %collective-permute-start.8 = (bf16[16,2304]{1,0:T(8,128)(2,1)S(1)}, bf16[16,2304]{1,0:T(8,128)(2,1)S(1)}, u32[]{:S(2)}, u32[]{:S(2)}) collective-permute-start(bf16[16,2304]{1,0:T(8,128)(2,1)S(1)} %get-tuple-element.77), channel_id=1, source_target_pairs={{0,2},{1,3},{2,0},{3,1},{4,6},{5,7},{6,4},{7,5},{8,10},{9,11},{10,... | collective-permute-start | bytes 221192 | tf_op jit(solution)/shard_map/ppermute | solution.py:424
  26.6 14.2 %collective-permute-start.10 = (bf16[16,2304]{1,0:T(8,128)(2,1)S(1)}, bf16[16,2304]{1,0:T(8,128)(2,1)S(1)}, u32[]{:S(2)}, u32[]{:S(2)}) collective-permute-start(bf16[16,2304]{1,0:T(8,128)(2,1)S(1)} %get-tuple-element.79), channel_id=1, source_target_pairs={{0,3},{1,2},{2,1},{3,0},{4,7},{5,6},{6,5},{7,4},{8,11},{9,10},{10,... | collective-permute-start | bytes 221192 | tf_op jit(solution)/shard_map/ppermute | solution.py:424
  30.9 9.9 %collective-permute-start.9 = (bf16[16,1792]{1,0:T(8,128)(2,1)S(1)}, bf16[16,1792]{1,0:T(8,128)(2,1)S(1)}, u32[]{:S(2)}, u32[]{:S(2)}) collective-permute-start(bf16[16,1792]{1,0:T(8,128)(2,1)S(1)} %get-tuple-element.78), channel_id=1, source_target_pairs={{0,2},{1,3},{2,0},{3,1},{4,6},{5,7},{6,4},{7,5},{8,10},{9,11},{10,... | collective-permute-start | bytes 172040 | tf_op jit(solution)/shard_map/ppermute | solution.py:424
  30.9 9.9 %collective-permute-start.11 = (bf16[16,1792]{1,0:T(8,128)(2,1)S(1)}, bf16[16,1792]{1,0:T(8,128)(2,1)S(1)}, u32[]{:S(2)}, u32[]{:S(2)}) collective-permute-start(bf16[16,1792]{1,0:T(8,128)(2,1)S(1)} %get-tuple-element.80), channel_id=1, source_target_pairs={{0,3},{1,2},{2,1},{3,0},{4,7},{5,6},{6,5},{7,4},{8,11},{9,10},{10,... | collective-permute-start | bytes 172040 | tf_op jit(solution)/shard_map/ppermute | solution.py:424

commit v7 on v6

--- a/solution.py
+++ b/solution.py
@@ -213,7 +213,7 @@
 
 
 def first_leaves(row_leaves):
-    return row_leaves * 9 // 16
+    return row_leaves * 11 // 16
 
 
 def first_count(slots):
@@ -221,7 +221,7 @@
 
 
 def second_count(slots):
-    return max(slots // 8 // NEAR_TRIP, 1) * NEAR_TRIP
+    return max(slots // 4 // NEAR_TRIP, 1) * NEAR_TRIP
 
 
 def first_entries(near_fill, near_source, near_target, source_points, source_areas, target_points, indices, bases, leaves):
@@ -462,7 +462,7 @@
     one = near_field(*inputs, range(split))
     early = {mask: exchange(one[mask], mask) for mask in far_masks(columns)}
     two = near_field(*inputs, range(split, row_leaves), (one[1],), (1,))
-    late = {mask: exchange(two[mask], mask) for mask in far_masks(columns) + [1]}
+    late = {mask: exchange(two[mask], mask) for mask in late_masks(columns)}
     result = jnp.concatenate([one[0], two[0]], axis=1) + late[1].astype(F32)
     for mask in early:
         result = result + jnp.concatenate([early[mask], late[mask]], axis=1).astype(F32)
@@ -471,6 +471,10 @@
 
 def far_masks(columns):
     return list(range(2, columns))
+
+
+def late_masks(columns):
+    return [1] + far_masks(columns)[::-1]
 
 
 def solution(mesh):

time: 41.9 us -> 42.1 us (level)
    pallas_call x2, Pallas kernels: 9.86 us -> 8.65 us  [near_field(): pl.pallas_call(functools.partial(near_kernel, base_leaf=leaves[0], firsts...]
    pallas_call x1, Pallas kernels: 1.39 us -> 2.58 us  [more_entries(): pl.pallas_call(functools.partial(more_entries_kernel, first=first), out_s...]
  transfers between devices with their start and end apart: 12 -> 12, of which waited for: 1 -> 1; matrix products, arithmetic and copies ran while one was open for 0% -> 0% of each run, Pallas kernels for 18% -> 21%
where the time goes in v7:
time: 42.1 us; the launch traced here: 41.8 us
  Pallas kernels  20.1 us (48%)
  starting transfers between devices  11.5 us (27%)
  waiting for transfers between devices  8.61 us (20%)
  between operations  0.8 us (2%)
  other arithmetic  0.76 us (2%)
    ppermute x12, starting transfers between devices, swap(): return lax.ppermute(value, axis, [(i, i ^ mask) for i in range(size)])  11.5 us
    pallas_call x2, Pallas kernels, near_field(): pl.pallas_call(functools.partial(near_kernel, base_leaf=leaves[0], firsts...  8.65 us
    ppermute x12, waiting for transfers between devices, swap(): return lax.ppermute(value, axis, [(i, i ^ mask) for i in range(size)])  8.61 us
    pallas_call x1, Pallas kernels, first_entries(): pl.pallas_call(functools.partial(first_entries_kernel, column_leaves=colu...  6.04 us
    pallas_call x1, Pallas kernels, far_field(): pl.pallas_call(functools.partial(far_kernel, pieces=len(pieces), plain=pl...  2.84 us
    pallas_call x1, Pallas kernels, more_entries(): pl.pallas_call(functools.partial(more_entries_kernel, first=first), out_s...  2.58 us
  transfers between devices with their start and end apart: 12, of which 1 were waited for; matrix products, arithmetic and copies ran while one was open for 0% of the time, Pallas kernels for 21%

profile of v7, /device:TPU:0, one launch (start us, length us, event | category | flops | bytes accessed | tf_op | source)
XLA Modules:
  0.0 41.8 jit_solution(2560261608745917239)
XLA Ops:
  0.0 3.0 %collective-permute-start.1 = (bf16[8,8192]{1,0:T(8,128)(2,1)}, bf16[8,8192]{1,0:T(8,128)(2,1)S(1)}, u32[]{:S(2)}, u32[]{:S(2)}) collective-permute-start(bf16[8,8192]{1,0:T(8,128)(2,1)} %refs_6_.2), channel_id=1, source_target_pairs={{0,16},{4,20},{8,24},{12,28},{16,0},{20,4},{24,8},{28,12},{1,17},{... | collective-permute-start | bytes 393224 | tf_op jit(solution)/shard_map/ppermute | solution.py:424
  3.0 1.5 %collective-permute-start = (bf16[8,8192]{1,0:T(8,128)(2,1)}, bf16[8,8192]{1,0:T(8,128)(2,1)S(1)}, u32[]{:S(2)}, u32[]{:S(2)}) collective-permute-start(bf16[8,8192]{1,0:T(8,128)(2,1)} %refs_6_.2), channel_id=1, source_target_pairs={{0,8},{4,12},{8,0},{12,4},{16,24},{20,28},{24,16},{28,20},{1,9},{5... | collective-permute-start | bytes 393224 | tf_op jit(solution)/shard_map/ppermute | solution.py:424
  4.5 0.0 collective-permute-start.2
  5.1 0.0 copy-start
  5.2 6.0 %entries.1 = (bf16[48,256,256]{2,1,0:T(8,128)(2,1)S(1)}, bf16[48,256,256]{2,1,0:T(8,128)(2,1)S(1)}, s32[8,256]{1,0:T(8,128)S(4)}, bf16[32,256,128]{2,1,0:T(8,128...) custom-call(s32[1,1]{1,0:T(1,128)S(6)} %copy.15.refs_0_, ...), custom_call_target="tpu_custom_call" | custom-call | flops 8000000000 | bytes 1048576 | tf_op jit(solution)/shard_map/entries/pallas_call | solution.py:234
  11.2 0.0 collective-permute-done.1.refs_8_
  11.2 0.0 collective-permute-done.refs_7_
  11.2 0.0 collective-permute-done.2.refs_9_
  11.2 0.0 copy-done
  11.2 0.1 collective-permute-start.3
  11.3 0.5 %collective-permute-start.4 = (bf16[8,8192]{1,0:T(8,128)(2,1)S(1)}, bf16[8,8192]{1,0:T(8,128)(2,1)S(1)}, u32[]{:S(2)}, u32[]{:S(2)}) collective-permute-start(bf16[8,8192]{1,0:T(8,128)(2,1)S(1)} %collective-permute-done.refs_7_), channel_id=1, source_target_pairs={{0,4},{4,0},{8,12},{12,8},{16,20},{20,16},{24,28},{28,24},{1,5},{5... | collective-permute-start | bytes 393224 | tf_op jit(solution)/shard_map/ppermute | solution.py:424
  11.8 0.1 collective-permute-start.5
  11.9 0.4 %collective-permute-start.6 = (bf16[8,8192]{1,0:T(8,128)(2,1)S(1)}, bf16[8,8192]{1,0:T(8,128)(2,1)S(1)}, u32[]{:S(2)}, u32[]{:S(2)}) collective-permute-start(bf16[8,8192]{1,0:T(8,128)(2,1)S(1)} %collective-permute-done.2.refs_9_), channel_id=1, source_target_pairs={{0,4},{4,0},{8,12},{12,8},{16,20},{20,16},{24,28},{28,24},{1,5},{5... | collective-permute-start | bytes 393224 | tf_op jit(solution)/shard_map/ppermute | solution.py:424
  12.3 2.6 %entries_rest.1 = (bf16[32,256,256]{2,1,0:T(8,128)(2,1)S(1)}, bf16[32,256,256]{2,1,0:T(8,128)(2,1)S(1)}) custom-call(s32[8,256]{1,0:T(8,128)S(4)} %get-tuple-element.44.table_ref.refs_0_, bf16[32,256,128]{2,1,0:T(8,128)(2,1)S(1)} %get-tuple-element.56.s_ref.refs_4_, bf16[16,64,256]{2,1,0:T(8,128)(2,1)S(1)} %get-tuple-element.57.t_ref.refs_5_), custom_call_target="tpu_custom_call" | custom-call | flops 8000000000 | bytes 1048576 | tf_op jit(solution)/shard_map/entries_rest/pallas_call | solution.py:259
  14.9 0.0 collective-permute-done.3.refs_10_
  14.9 0.0 collective-permute-done.4.refs_11_
  14.9 0.0 collective-permute-done.5.refs_12_
  14.9 0.0 collective-permute-done.6.refs_13_
  15.0 2.8 %far.1 = (bf16[32,64,256]{2,1,0:T(8,128)(2,1)S(1)}, f32[16,64,256]{2,1,0:T(8,128)S(1)}) custom-call(s32[32]{0:T(128)S(4)} %get-tuple-element.46.refs_0_, s32[1,96]{1,0:T(1,128)S(4)} %get-tuple-element.47.refs_1_, s32[1,96]{1,0:T(1,128)S(4)} %get-tuple-element.48.refs_2_, s32[1,96]{1,0:T(1,128)S(4)} %get-tuple-element.49.refs_3_, ...), custom_call_target="tpu_custom_call" | custom-call | flops 2000000000 | bytes 8388608 | tf_op jit(solution)/shard_map/far/pallas_call | solution.py:370
  17.8 4.2 %near.2 = (f32[16,2816]{1,0:T(8,128)S(1)}, bf16[16,2816]{1,0:T(8,128)(2,1)S(1)}, bf16[16,2816]{1,0:T(8,128)(2,1)S(1)}, bf16[16,2816]{1,0:T(8,128)(2,1)S(1)}) custom-call(s32[8,256]{1,0:T(8,128)S(4)} %get-tuple-element.44.table_ref.refs_0_, s32[16]{0:T(128)S(4)} %get-tuple-element.45.refs_1_, f32[16,64,256]{2,1,0:T(8,128)S(1)} %get-tuple-element.67.refs_2_, ...), custom_call_target="tpu_custom_call" | custom-call | flops 4000000000 | bytes 8388608 | tf_op jit(solution)/shard_map/near/pallas_call | solution.py:399
  22.0 4.5 %near.3 = (f32[16,1280]{1,0:T(8,128)S(1)}, bf16[16,4096]{1,0:T(8,128)(2,1)S(1)}, bf16[16,1280]{1,0:T(8,128)(2,1)S(1)}, bf16[16,1280]{1,0:T(8,128)(2,1)S(1)}) custom-call(s32[8,256]{1,0:T(8,128)S(4)} %get-tuple-element.44.table_ref.refs_0_, s32[16]{0:T(128)S(4)} %get-tuple-element.45.refs_1_, f32[16,64,256]{2,1,0:T(8,128)S(1)} %get-tuple-element.67.refs_2_, ...), custom_call_target="tpu_custom_call" | custom-call | flops 4000000000 | bytes 8388608 | tf_op jit(solution)/shard_map/near/pallas_call | solution.py:399
  26.5 0.1 collective-permute-start.7
  26.6 0.1 collective-permute-start.8
  26.6 4.3 %collective-permute-start.10 = (bf16[16,2816]{1,0:T(8,128)(2,1)S(1)}, bf16[16,2816]{1,0:T(8,128)(2,1)S(1)}, u32[]{:S(2)}, u32[]{:S(2)}) collective-permute-start(bf16[16,2816]{1,0:T(8,128)(2,1)S(1)} %get-tuple-element.79), channel_id=1, source_target_pairs={{0,3},{1,2},{2,1},{3,0},{4,7},{5,6},{6,5},{7,4},{8,11},{9,10},{10,... | collective-permute-start | bytes 270344 | tf_op jit(solution)/shard_map/ppermute | solution.py:424
  30.9 0.0 collective-permute-start.9
  30.9 1.5 %collective-permute-start.11 = (bf16[16,1280]{1,0:T(8,128)(2,1)S(1)}, bf16[16,1280]{1,0:T(8,128)(2,1)S(1)}, u32[]{:S(2)}, u32[]{:S(2)}) collective-permute-start(bf16[16,1280]{1,0:T(8,128)(2,1)S(1)} %get-tuple-element.80), channel_id=1, source_target_pairs={{0,3},{1,2},{2,1},{3,0},{4,7},{5,6},{6,5},{7,4},{8,11},{9,10},{10,... | collective-permute-start | bytes 122888 | tf_op jit(solution)/shard_map/ppermute | solution.py:424
  32.5 8.6 %collective-permute-done.9 = bf16[16,1280]{1,0:T(8,128)(2,1)S(1)} collective-permute-done((bf16[16,1280]{1,0:T(8,128)(2,1)S(1)}, bf16[16,1280]{1,0:T(8,128)(2,1)S(1)}, u32[]{:S(2)}, u32[]{:S(2)}) %collective-permute-start.9) | collective-permute-done | bytes 40992 | tf_op jit(solution)/shard_map/ppermute | solution.py:424
  41.1 0.0 collective-permute-done.11
  41.1 0.0 collective-permute-done.8
  41.1 0.0 collective-permute-done.10
  41.1 0.0 collective-permute-done.7
  41.1 0.8 %fusion.1 = f32[16,4096]{1,0:T(8,128)} fusion(f32[16,1280]{1,0:T(8,128)S(1)} %get-tuple-element.75, f32[16,2816]{1,0:T(8,128)S(1)} %get-tuple-element.73, bf16[16,4096]{1,0:T(8,128)(2,1)S(1)} %collective-permute-done.7, bf16[16,1280]{1,0:T(8,128)(2,1)S(1)} %collective-permute-done.9, bf16[16,2816]{1,0:T(8,128)(2,1)S(1)} %collective-permute-done.8, ...), kind=kLoop, calls=%fused_computation.2 | loop fusion | flops 851968 | bytes 917504 | tf_op jit(solution)/shard_map/add | solution.py:468
Async XLA Ops:
  0.0 11.2 %collective-permute-start.1 = (bf16[8,8192]{1,0:T(8,128)(2,1)}, bf16[8,8192]{1,0:T(8,128)(2,1)S(1)}, u32[]{:S(2)}, u32[]{:S(2)}) collective-permute-start(bf16[8,8192]{1,0:T(8,128)(2,1)} %refs_6_.2), channel_id=1, source_target_pairs={{0,16},{4,20},{8,24},{12,28},{16,0},{20,4},{24,8},{28,12},{1,17},{... | collective-permute-start | bytes 393224 | tf_op jit(solution)/shard_map/ppermute | solution.py:424
  3.0 8.2 %collective-permute-start = (bf16[8,8192]{1,0:T(8,128)(2,1)}, bf16[8,8192]{1,0:T(8,128)(2,1)S(1)}, u32[]{:S(2)}, u32[]{:S(2)}) collective-permute-start(bf16[8,8192]{1,0:T(8,128)(2,1)} %refs_6_.2), channel_id=1, source_target_pairs={{0,8},{4,12},{8,0},{12,4},{16,24},{20,28},{24,16},{28,20},{1,9},{5... | collective-permute-start | bytes 393224 | tf_op jit(solution)/shard_map/ppermute | solution.py:424
  4.5 6.7 %collective-permute-start.2 = (bf16[8,8192]{1,0:T(8,128)(2,1)}, bf16[8,8192]{1,0:T(8,128)(2,1)S(1)}, u32[]{:S(2)}, u32[]{:S(2)}) collective-permute-start(bf16[8,8192]{1,0:T(8,128)(2,1)} %refs_6_.2), channel_id=1, source_target_pairs={{0,24},{4,28},{8,16},{12,20},{16,8},{20,12},{24,0},{28,4},{1,25},{... | collective-permute-start | bytes 393224 | tf_op jit(solution)/shard_map/ppermute | solution.py:424
  5.1 6.1 %copy-start = (bf16[8,8192]{1,0:T(8,128)(2,1)S(1)}, bf16[8,8192]{1,0:T(8,128)(2,1)}, u32[]{:S(2)}) copy-start(bf16[8,8192]{1,0:T(8,128)(2,1)} %refs_6_.2) | copy-start | bytes 393220
  11.2 3.7 %collective-permute-start.3 = (bf16[8,8192]{1,0:T(8,128)(2,1)S(1)}, bf16[8,8192]{1,0:T(8,128)(2,1)S(1)}, u32[]{:S(2)}, u32[]{:S(2)}) collective-permute-start(bf16[8,8192]{1,0:T(8,128)(2,1)S(1)} %copy-done), channel_id=1, source_target_pairs={{0,4},{4,0},{8,12},{12,8},{16,20},{20,16},{24,28},{28,24},{1,5},{5... | collective-permute-start | bytes 393224 | tf_op jit(solution)/shard_map/ppermute | solution.py:424
  11.3 3.6 %collective-permute-start.4 = (bf16[8,8192]{1,0:T(8,128)(2,1)S(1)}, bf16[8,8192]{1,0:T(8,128)(2,1)S(1)}, u32[]{:S(2)}, u32[]{:S(2)}) collective-permute-start(bf16[8,8192]{1,0:T(8,128)(2,1)S(1)} %collective-permute-done.refs_7_), channel_id=1, source_target_pairs={{0,4},{4,0},{8,12},{12,8},{16,20},{20,16},{24,28},{28,24},{1,5},{5... | collective-permute-start | bytes 393224 | tf_op jit(solution)/shard_map/ppermute | solution.py:424
  11.8 3.1 %collective-permute-start.5 = (bf16[8,8192]{1,0:T(8,128)(2,1)S(1)}, bf16[8,8192]{1,0:T(8,128)(2,1)S(1)}, u32[]{:S(2)}, u32[]{:S(2)}) collective-permute-start(bf16[8,8192]{1,0:T(8,128)(2,1)S(1)} %collective-permute-done.1.refs_8_), channel_id=1, source_target_pairs={{0,4},{4,0},{8,12},{12,8},{16,20},{20,16},{24,28},{28,24},{1,5},{5... | collective-permute-start | bytes 393224 | tf_op jit(solution)/shard_map/ppermute | solution.py:424
  11.9 3.1 %collective-permute-start.6 = (bf16[8,8192]{1,0:T(8,128)(2,1)S(1)}, bf16[8,8192]{1,0:T(8,128)(2,1)S(1)}, u32[]{:S(2)}, u32[]{:S(2)}) collective-permute-start(bf16[8,8192]{1,0:T(8,128)(2,1)S(1)} %collective-permute-done.2.refs_9_), channel_id=1, source_target_pairs={{0,4},{4,0},{8,12},{12,8},{16,20},{20,16},{24,28},{28,24},{1,5},{5... | collective-permute-start | bytes 393224 | tf_op jit(solution)/shard_map/ppermute | solution.py:424
  26.5 14.6 %collective-permute-start.7 = (bf16[16,4096]{1,0:T(8,128)(2,1)S(1)}, bf16[16,4096]{1,0:T(8,128)(2,1)S(1)}, u32[]{:S(2)}, u32[]{:S(2)}) collective-permute-start(bf16[16,4096]{1,0:T(8,128)(2,1)S(1)} %get-tuple-element.76), channel_id=1, source_target_pairs={{0,1},{1,0},{2,3},{3,2},{4,5},{5,4},{6,7},{7,6},{8,9},{9,8},{10,11... | collective-permute-start | bytes 393224 | tf_op jit(solution)/shard_map/ppermute | solution.py:424
  26.6 14.5 %collective-permute-start.8 = (bf16[16,2816]{1,0:T(8,128)(2,1)S(1)}, bf16[16,2816]{1,0:T(8,128)(2,1)S(1)}, u32[]{:S(2)}, u32[]{:S(2)}) collective-permute-start(bf16[16,2816]{1,0:T(8,128)(2,1)S(1)} %get-tuple-element.77), channel_id=1, source_target_pairs={{0,2},{1,3},{2,0},{3,1},{4,6},{5,7},{6,4},{7,5},{8,10},{9,11},{10,... | collective-permute-start | bytes 270344 | tf_op jit(solution)/shard_map/ppermute | solution.py:424
  26.6 14.4 %collective-permute-start.10 = (bf16[16,2816]{1,0:T(8,128)(2,1)S(1)}, bf16[16,2816]{1,0:T(8,128)(2,1)S(1)}, u32[]{:S(2)}, u32[]{:S(2)}) collective-permute-start(bf16[16,2816]{1,0:T(8,128)(2,1)S(1)} %get-tuple-element.79), channel_id=1, source_target_pairs={{0,3},{1,2},{2,1},{3,0},{4,7},{5,6},{6,5},{7,4},{8,11},{9,10},{10,... | collective-permute-start | bytes 270344 | tf_op jit(solution)/shard_map/ppermute | solution.py:424
  30.9 10.1 %collective-permute-start.9 = (bf16[16,1280]{1,0:T(8,128)(2,1)S(1)}, bf16[16,1280]{1,0:T(8,128)(2,1)S(1)}, u32[]{:S(2)}, u32[]{:S(2)}) collective-permute-start(bf16[16,1280]{1,0:T(8,128)(2,1)S(1)} %get-tuple-element.78), channel_id=1, source_target_pairs={{0,2},{1,3},{2,0},{3,1},{4,6},{5,7},{6,4},{7,5},{8,10},{9,11},{10,... | collective-permute-start | bytes 122888 | tf_op jit(solution)/shard_map/ppermute | solution.py:424
  30.9 10.1 %collective-permute-start.11 = (bf16[16,1280]{1,0:T(8,128)(2,1)S(1)}, bf16[16,1280]{1,0:T(8,128)(2,1)S(1)}, u32[]{:S(2)}, u32[]{:S(2)}) collective-permute-start(bf16[16,1280]{1,0:T(8,128)(2,1)S(1)} %get-tuple-element.80), channel_id=1, source_target_pairs={{0,3},{1,2},{2,1},{3,0},{4,7},{5,6},{6,5},{7,4},{8,11},{9,10},{10,... | collective-permute-start | bytes 122888 | tf_op jit(solution)/shard_map/ppermute | solution.py:424
